TPU v7x, 1024 devices: a whole 4x4x32 slice. The times are simulated.
1024 devices in a mesh: gx: 4 (over y), gy: 8 (over x, core), gz: 32 (over z).
Axes of the slice: x: 4, y: 4, z: 32, core: 2. Of those that a mesh axis runs over, the one named last changes fastest.
Arguments:
- loads: float32 [16, 8, 32, 8192], P(None, 'gx', 'gy', 'gz'), may hold values from -60 to 60
- moduli: float32 [8], replicated, may hold values from 0.5 to 4
- material: int32 [8, 32, 8192], P('gx', 'gy', 'gz'), may hold values from 0 to 7
Outputs:
- solution: float32 [16, 8, 32, 8192], P(None, 'gx', 'gy', 'gz')
- residual: float32 [16, 8, 32, 8192], P(None, 'gx', 'gy', 'gz')
All inputs are finite; a program needn't handle non-finite values.
Results may differ from a plain program's by a relative error of at most 0.005.
The roundings to bfloat16 on the way count: a program that leaves them out, or rounds other values in their place, can miss the bound.
Values may be sent and summed in bfloat16 or wider, within the bound.
No kernel may reach another device: no remote copies, remote signals or barrier semaphores. Data moves between devices by JAX's collectives and lax.ppermute only.
A program may use at most 32 MiB of HBM per device.

v0:
```python
import functools

import jax
import jax.numpy as jnp
import numpy as np
from jax import lax
from jax.sharding import Mesh
from jax.sharding import PartitionSpec as P

ITERS = 2
GX_GY_GZ = ("gx", "gy_0", "gy_1", "gz")
GY = ("gy_0", "gy_1")


SIGMA = 0.25


def padded_2(cells, sides, width):
    for axis, dim in sides:
        count = lax.axis_size(axis)
        ends = count - 1
        head = lax.slice_in_dim(cells, 0, width, axis=dim)
        tail = lax.slice_in_dim(cells, cells.shape[dim] - width, cells.shape[dim], axis=dim)
        cells = jnp.concatenate(
            [
                lax.ppermute(tail, axis, [(i, (i + 1) % count) for i in range(ends)]),
                cells,
                lax.ppermute(head, axis, [((i + 1) % count, i) for i in range(ends)]),
            ],
            axis=dim,
        )
    return cells


def one_axis_at_a_time(value, axes):
    return functools.reduce(lax.psum, axes, value)


def stiffness_table():
    line_mass = np.array([[1.0 / 3.0, 1.0 / 6.0], [1.0 / 6.0, 1.0 / 3.0]])
    line_stiff = np.array([[1.0, -1.0], [-1.0, 1.0]])
    table = np.zeros((8, 8))
    for target in range(8):
        for source in range(8):
            target_bits = [target >> 2 & 1, target >> 1 & 1, target & 1]
            source_bits = [source >> 2 & 1, source >> 1 & 1, source & 1]
            total = 0.0
            for stiff_dim in range(3):
                factor = 1.0
                for other in range(3):
                    if other == stiff_dim:
                        factor = factor * line_stiff[target_bits[other], source_bits[other]]
                    else:
                        factor = factor * line_mass[target_bits[other], source_bits[other]]
                total = total + factor
            table[target, source] = total
    return table


def corner_bits(corner):
    return (corner >> 2 & 1, corner >> 1 & 1, corner & 1)


def apply_operator(field, weights, kernel):
    lowered = field.astype(jnp.bfloat16)
    padded = padded_2(lowered, (("gx", 1), (GY, 2), ("gz", 3)), 1)
    size_x, size_y, size_z = (field.shape[1], field.shape[2], field.shape[3])
    pieces = []
    for corner in range(8):
        bit_x, bit_y, bit_z = corner_bits(corner)
        pieces.append(
            padded[
                :,
                bit_x : bit_x + size_x + 1,
                bit_y : bit_y + size_y + 1,
                bit_z : bit_z + size_z + 1,
            ]
        )
    stacked = jnp.stack(pieces)
    total = SIGMA * field
    for corner in range(8):
        bit_x, bit_y, bit_z = corner_bits(corner)
        part = (
            jnp.einsum("b,bcxyz->cxyz", kernel[corner], stacked, preferred_element_type=jnp.float32)
            * weights
        )
        total = (
            total
            + part[
                :,
                1 - bit_x : 1 - bit_x + size_x,
                1 - bit_y : 1 - bit_y + size_y,
                1 - bit_z : 1 - bit_z + size_z,
            ]
        )
    return total


def local_gram(left, right):
    return jnp.einsum("cxyz,dxyz->cd", left, right, precision=lax.Precision.HIGHEST)


def combine(block, coeffs):
    return jnp.einsum("cxyz,cd->dxyz", block, coeffs, precision=lax.Precision.HIGHEST)


def solve_small(matrix, rhs_small):
    factor = jnp.linalg.cholesky(matrix)
    return jax.scipy.linalg.cho_solve((factor, True), rhs_small)


def residual_gram(residual):
    return one_axis_at_a_time(local_gram(residual, residual), GX_GY_GZ)


def on_device(loads, moduli, material):
    kernel = jnp.asarray(stiffness_table(), jnp.float32).astype(jnp.bfloat16)
    levels = jnp.arange(moduli.shape[0], dtype=jnp.int32)
    node_modulus = jnp.sum(jnp.where(material[..., None] == levels, moduli, 0.0), axis=-1)
    padded_mod = padded_2(node_modulus, (("gx", 0), (GY, 1), ("gz", 2)), 1)
    size_x, size_y, size_z = material.shape
    weights = jnp.zeros((size_x + 1, size_y + 1, size_z + 1), jnp.float32)
    for corner in range(8):
        bit_x, bit_y, bit_z = corner_bits(corner)
        weights = (
            weights
            + padded_mod[
                bit_x : bit_x + size_x + 1, bit_y : bit_y + size_y + 1, bit_z : bit_z + size_z + 1
            ]
        )
    weights = weights * 0.125
    solution = jnp.zeros_like(loads)
    residual = loads
    direction = loads
    current = residual_gram(residual)
    for iteration in range(ITERS):
        image = apply_operator(direction, weights, kernel)
        curvature, cross, image_sq = (
            one_axis_at_a_time(local_gram(direction, image), GX_GY_GZ),
            one_axis_at_a_time(local_gram(image, residual), GX_GY_GZ),
            one_axis_at_a_time(local_gram(image, image), GX_GY_GZ),
        )
        alpha = solve_small(curvature, current)
        solution = solution + combine(direction, alpha)
        residual = residual - combine(image, alpha)
        if iteration + 1 < ITERS:
            high = lax.Precision.HIGHEST
            cross_term = jnp.dot(alpha.T, cross, precision=high)
            quad_term = jnp.dot(jnp.dot(alpha.T, image_sq, precision=high), alpha, precision=high)
            updated = current - cross_term - cross_term.T + quad_term
            beta = solve_small(current, updated)
            direction = residual + combine(direction, beta)
            current = updated
    return (solution, residual)


def solution(mesh):
    split = Mesh(
        mesh.devices.reshape(mesh.shape["gx"], 4, 2, mesh.shape["gz"]), ("gx", "gy_0", "gy_1", "gz")
    )
    placed = (P(None, "gx", GY, "gz"), P(), P("gx", GY, "gz"))
    return jax.shard_map(
        on_device,
        mesh=split,
        in_specs=placed,
        out_specs=(P(None, "gx", GY, "gz"), P(None, "gx", GY, "gz")),
        check_vma=False,
    )
```

profile of v0, /device:TPU:2, one launch (start us, length us, event | category | flops | bytes accessed | tf_op | source)
XLA Modules:
  0.0 339.8 jit_solution(10848079016955452637)
XLA Ops:
  0.6 0.8 select_reduce_fusion
  1.4 3.5 %collective-permute-start.6 = (f32[1,4,256]{2,1,0:T(4,128)S(1)}, f32[1,4,256]{2,1,0:T(4,128)S(1)}, u32[]{:S(2)}, u32[]{:S(2)}) collective-permute-start(f32[1,4,256]{2,1,0:T(4,128)S(1)} %get-tuple-element.54), channel_id=1, source_target_pairs={{0,256},{256,512},{512,768},{1,257},{257,513},{513,769},{2,258},{2... | collective-permute-start | bytes 12296 | tf_op jit(solution)/shard_map/ppermute | solution.py:26
  4.9 1.3 collective-permute-start.7
  6.2 0.9 convert_element_type.9
  7.2 4.5 %collective-permute-start = (bf16[16,1,4,256]{3,2,1,0:T(4,128)(2,1)S(1)}, bf16[16,1,4,256]{3,2,1,0:T(4,128)(2,1)S(1)}, u32[]{:S(2)}, u32[]{:S(2)}) collective-permute-start(bf16[16,1,4,256]{3,2,1,0:T(4,128)(2,1)S(1)} %get-tuple-element.38), channel_id=1, source_target_pairs={{0,256},{256,512},{512,768},{1,257},{257,513},{513,769},{2,258},{2... | collective-permute-start | bytes 98312 | tf_op jit(solution)/shard_map/ppermute | solution.py:26
  11.8 1.3 collective-permute-start.1
  13.1 1.9 collective-permute-start.8
  15.0 3.6 %collective-permute-start.9 = (f32[4,1,256]{2,1,0:T(1,128)S(1)}, f32[4,1,256]{2,1,0:T(1,128)S(1)}, u32[]{:S(2)}, u32[]{:S(2)}) collective-permute-start(f32[4,1,256]{2,1,0:T(1,128)S(1)} %get-tuple-element.53), channel_id=1, source_target_pairs={{32,0},{64,32},{96,64},{128,96},{160,128},{192,160},{224,192},{33,... | collective-permute-start | bytes 12296 | tf_op jit(solution)/shard_map/ppermute | solution.py:28
  18.7 1.3 convolution_bitcast_fusion.4
  20.1 3.8 %collective-permute-start.10 = (f32[4,6,1]{2,1,0:T(8,128)S(1)}, f32[4,6,1]{2,1,0:T(8,128)S(1)}, u32[]{:S(2)}, u32[]{:S(2)}) collective-permute-start(f32[4,6,1]{2,1,0:T(8,128)S(1)} %get-tuple-element.48), channel_id=1, source_target_pairs={{0,1},{1,2},{2,3},{3,4},{4,5},{5,6},{6,7},{7,8},{8,9},{9,10},{10,1... | collective-permute-start | bytes 296 | tf_op jit(solution)/shard_map/ppermute | solution.py:26
  23.9 1.3 collective-permute-start.11
  25.4 4.2 %collective-permute-done.11 = f32[4,6,1]{2,1,0:T(8,128)S(1)} collective-permute-done((f32[4,6,1]{2,1,0:T(8,128)S(1)}, f32[4,6,1]{2,1,0:T(8,128)S(1)}, u32[]{:S(2)}, u32[]{:S(2)}) %collective-permute-start.11) | collective-permute-done | bytes 128 | tf_op jit(solution)/shard_map/ppermute | solution.py:28
  29.9 2.2 collective-permute-start.2
  32.1 6.7 %collective-permute-start.3 = (bf16[16,4,1,256]{3,2,1,0:T(2,128)(2,1)S(1)}, bf16[16,4,1,256]{3,2,1,0:T(2,128)(2,1)S(1)}, u32[]{:S(2)}, u32[]{:S(2)}) collective-permute-start(bf16[16,4,1,256]{3,2,1,0:T(2,128)(2,1)S(1)} %get-tuple-element.35), channel_id=1, source_target_pairs={{32,0},{64,32},{96,64},{128,96},{160,128},{192,160},{224,192},{33,... | collective-permute-start | bytes 98312 | tf_op jit(solution)/shard_map/ppermute | solution.py:28
  38.8 1.8 collective-permute-done.3
  41.0 1.9 collective-permute-start.4
  42.9 1.3 collective-permute-start.5
  44.3 1.7 collective-permute-done.4
  46.1 4.8 %collective-permute-done.5 = bf16[16,4,6,1]{3,2,1,0:T(8,128)(2,1)S(1)} collective-permute-done((bf16[16,4,6,1]{3,2,1,0:T(8,128)(2,1)S(1)}, bf16[16,4,6,1]{3,2,1,0:T(8,128)(2,1)S(1)}, u32[]{:S(2)}, u32[]{:S(2)}) %collective-permute-start.5) | collective-permute-done | bytes 800 | tf_op jit(solution)/shard_map/ppermute | solution.py:28
  50.9 0.9 pad_maximum_fusion
  52.4 1.6 copy.46
  58.8 0.8 copy-done
  60.4 17.7 %all-reduce.2 = (f32[16,16]{0,1:T(8,128)S(1)}, f32[16,16]{0,1:T(8,128)S(1)}, f32[16,16]{1,0:T(8,128)S(1)}, f32[16,16]{1,0:T(8,128)S(1)}) all-reduce(f32[16,16]{0,1:T(8,128)S(1)} %convolution_bitcast_fusion.4, f32[16,16]{0,1:T(8,128)S(1)} %bitcast.265, ...), channel_id=1, replica_groups=mesh['gx'=4,'gy_0'=4,'gy_1'=2,'gz'=32] {'gx'}, use_global_device_ids=true, to_apply=%region_7.0 | all-reduce | flops 1024 | bytes 8192 | tf_op jit(solution)/shard_map/psum | solution.py:36
  78.1 14.3 %all-reduce.1 = (f32[16,16]{0,1:T(8,128)S(1)}, f32[16,16]{0,1:T(8,128)S(1)}, f32[16,16]{1,0:T(8,128)S(1)}, f32[16,16]{1,0:T(8,128)S(1)}) all-reduce(f32[16,16]{0,1:T(8,128)S(1)} %get-tuple-element.16, f32[16,16]{0,1:T(8,128)S(1)} %get-tuple-element.17, ...), channel_id=1, replica_groups=mesh['gx'=4,'gy_0'=4,'gy_1'=2,'gz'=32] {'gy_0'}, use_global_device_ids=true, to_apply=%region_8.0 | all-reduce | flops 1024 | bytes 8192 | tf_op jit(solution)/shard_map/psum | solution.py:36
  92.3 3.4 %all-reduce.3 = (f32[16,16]{0,1:T(8,128)S(1)}, f32[16,16]{0,1:T(8,128)S(1)}, f32[16,16]{1,0:T(8,128)S(1)}, f32[16,16]{1,0:T(8,128)S(1)}) all-reduce(f32[16,16]{0,1:T(8,128)S(1)} %get-tuple-element.12, f32[16,16]{0,1:T(8,128)S(1)} %get-tuple-element.13, ...), channel_id=1, replica_groups=mesh['gx'=4,'gy_0'=4,'gy_1'=2,'gz'=32] {'gy_1'}, use_global_device_ids=true, to_apply=%region_9.0 | all-reduce | flops 1024 | bytes 8192 | tf_op jit(solution)/shard_map/psum | solution.py:36
  95.8 118.6 %all-reduce = (f32[16,16]{0,1:T(8,128)S(1)}, f32[16,16]{0,1:T(8,128)S(1)}, f32[16,16]{1,0:T(8,128)S(1)}, f32[16,16]{1,0:T(8,128)S(1)}) all-reduce(f32[16,16]{0,1:T(8,128)S(1)} %get-tuple-element.20, f32[16,16]{0,1:T(8,128)S(1)} %get-tuple-element.21, ...), channel_id=1, replica_groups=mesh['gx'=4,'gy_0'=4,'gy_1'=2,'gz'=32] {'gz'}, use_global_device_ids=true, to_apply=%region_10.0 | all-reduce | flops 1024 | bytes 8192 | tf_op jit(solution)/shard_map/psum | solution.py:36
  214.4 1.5 cholesky.70
  216.6 0.6 fusion.56
  217.2 1.2 custom-call.10
  218.5 1.5 cholesky.59
  221.3 1.2 custom-call.9
  224.6 1.3 collective-permute-start.12
  225.9 1.3 collective-permute-start.13
  227.5 4.2 %collective-permute-done.13 = bf16[16,1,4,256]{3,0,2,1:T(8,128)(2,1)S(1)} collective-permute-done((bf16[16,1,4,256]{3,0,2,1:T(8,128)(2,1)S(1)}, bf16[16,1,4,256]{3,0,2,1:T(8,128)(2,1)S(1)}, u32[]{:S(2)}, u32[]{:S(2)}) %collective-permute-start.13) | collective-permute-done | bytes 32800 | tf_op jit(solution)/shard_map/ppermute | solution.py:28
  231.8 1.9 collective-permute-start.14
  233.7 3.6 %collective-permute-start.15 = (bf16[16,4,1,256]{3,0,2,1:T(8,128)(2,1)S(1)}, bf16[16,4,1,256]{3,0,2,1:T(8,128)(2,1)S(1)}, u32[]{:S(2)}, u32[]{:S(2)}) collective-permute-start(bf16[16,4,1,256]{3,0,2,1:T(8,128)(2,1)S(1)} %get-tuple-element.33), channel_id=1, source_target_pairs={{32,0},{64,32},{96,64},{128,96},{160,128},{192,160},{224,192},{33,... | collective-permute-start | bytes 98312 | tf_op jit(solution)/shard_map/ppermute | solution.py:28
  237.4 1.6 collective-permute-done.15
  239.1 1.6 collective-permute-start.16
  240.7 1.3 collective-permute-start.17
  243.0 4.7 %collective-permute-done.17 = bf16[16,4,6,1]{3,0,2,1:T(8,128)(2,1)S(1)} collective-permute-done((bf16[16,4,6,1]{3,0,2,1:T(8,128)(2,1)S(1)}, bf16[16,4,6,1]{3,0,2,1:T(8,128)(2,1)S(1)}, u32[]{:S(2)}, u32[]{:S(2)}) %collective-permute-start.17) | collective-permute-done | bytes 800 | tf_op jit(solution)/shard_map/ppermute | solution.py:28
  253.1 9.9 %psum.156 = f32[16,16]{0,1:T(8,128)S(1)} all-reduce(f32[16,16]{0,1:T(8,128)S(1)} %convolution_bitcast_fusion.1), channel_id=1, replica_groups=mesh['gx'=4,'gy_0'=4,'gy_1'=2,'gz'=32] {'gx'}, use_global_device_ids=true, to_apply=%region_19.22 | all-reduce | flops 256 | bytes 2048 | tf_op jit(solution)/shard_map/psum | solution.py:36
  263.0 9.3 %psum.157 = f32[16,16]{0,1:T(8,128)S(1)} all-reduce(f32[16,16]{0,1:T(8,128)S(1)} %psum.156), channel_id=1, replica_groups=mesh['gx'=4,'gy_0'=4,'gy_1'=2,'gz'=32] {'gy_0'}, use_global_device_ids=true, to_apply=%region_20.23 | all-reduce | flops 256 | bytes 2048 | tf_op jit(solution)/shard_map/psum | solution.py:36
  272.3 2.5 psum.158
  274.8 58.5 %psum.159 = f32[16,16]{0,1:T(8,128)S(1)} all-reduce(f32[16,16]{0,1:T(8,128)S(1)} %psum.158), channel_id=1, replica_groups=mesh['gx'=4,'gy_0'=4,'gy_1'=2,'gz'=32] {'gz'}, use_global_device_ids=true, to_apply=%region_22.25 | all-reduce | flops 256 | bytes 2048 | tf_op jit(solution)/shard_map/psum | solution.py:36
  333.4 1.5 cholesky.81
  336.1 1.2 custom-call.11
  338.1 0.7 copy.45
  339.1 0.7 copy.44
  (123 shorter events, 20.3 us)
Async XLA Ops:
  1.4 11.6 %collective-permute-start.6 = (f32[1,4,256]{2,1,0:T(4,128)S(1)}, f32[1,4,256]{2,1,0:T(4,128)S(1)}, u32[]{:S(2)}, u32[]{:S(2)}) collective-permute-start(f32[1,4,256]{2,1,0:T(4,128)S(1)} %get-tuple-element.54), channel_id=1, source_target_pairs={{0,256},{256,512},{512,768},{1,257},{257,513},{513,769},{2,258},{2... | collective-permute-start | bytes 12296 | tf_op jit(solution)/shard_map/ppermute | solution.py:26
  4.9 8.1 %collective-permute-start.7 = (f32[1,4,256]{2,1,0:T(4,128)S(1)}, f32[1,4,256]{2,1,0:T(4,128)S(1)}, u32[]{:S(2)}, u32[]{:S(2)}) collective-permute-start(f32[1,4,256]{2,1,0:T(4,128)S(1)} %get-tuple-element.55), channel_id=1, source_target_pairs={{256,0},{512,256},{768,512},{257,1},{513,257},{769,513},{258,2},{5... | collective-permute-start | bytes 12296 | tf_op jit(solution)/shard_map/ppermute | solution.py:28
  7.2 22.5 %collective-permute-start = (bf16[16,1,4,256]{3,2,1,0:T(4,128)(2,1)S(1)}, bf16[16,1,4,256]{3,2,1,0:T(4,128)(2,1)S(1)}, u32[]{:S(2)}, u32[]{:S(2)}) collective-permute-start(bf16[16,1,4,256]{3,2,1,0:T(4,128)(2,1)S(1)} %get-tuple-element.38), channel_id=1, source_target_pairs={{0,256},{256,512},{512,768},{1,257},{257,513},{513,769},{2,258},{2... | collective-permute-start | bytes 98312 | tf_op jit(solution)/shard_map/ppermute | solution.py:26
  11.8 17.9 %collective-permute-start.1 = (bf16[16,1,4,256]{3,2,1,0:T(4,128)(2,1)S(1)}, bf16[16,1,4,256]{3,2,1,0:T(4,128)(2,1)S(1)}, u32[]{:S(2)}, u32[]{:S(2)}) collective-permute-start(bf16[16,1,4,256]{3,2,1,0:T(4,128)(2,1)S(1)} %get-tuple-element.39), channel_id=1, source_target_pairs={{256,0},{512,256},{768,512},{257,1},{513,257},{769,513},{258,2},{5... | collective-permute-start | bytes 98312 | tf_op jit(solution)/shard_map/ppermute | solution.py:28
  13.1 6.9 %collective-permute-start.8 = (f32[4,1,256]{2,1,0:T(1,128)S(1)}, f32[4,1,256]{2,1,0:T(1,128)S(1)}, u32[]{:S(2)}, u32[]{:S(2)}) collective-permute-start(f32[4,1,256]{2,1,0:T(1,128)S(1)} %get-tuple-element.52), channel_id=1, source_target_pairs={{0,32},{32,64},{64,96},{96,128},{128,160},{160,192},{192,224},{1,3... | collective-permute-start | bytes 12296 | tf_op jit(solution)/shard_map/ppermute | solution.py:26
  15.0 5.0 %collective-permute-start.9 = (f32[4,1,256]{2,1,0:T(1,128)S(1)}, f32[4,1,256]{2,1,0:T(1,128)S(1)}, u32[]{:S(2)}, u32[]{:S(2)}) collective-permute-start(f32[4,1,256]{2,1,0:T(1,128)S(1)} %get-tuple-element.53), channel_id=1, source_target_pairs={{32,0},{64,32},{96,64},{128,96},{160,128},{192,160},{224,192},{33,... | collective-permute-start | bytes 12296 | tf_op jit(solution)/shard_map/ppermute | solution.py:28
  20.1 5.2 %collective-permute-start.10 = (f32[4,6,1]{2,1,0:T(8,128)S(1)}, f32[4,6,1]{2,1,0:T(8,128)S(1)}, u32[]{:S(2)}, u32[]{:S(2)}) collective-permute-start(f32[4,6,1]{2,1,0:T(8,128)S(1)} %get-tuple-element.48), channel_id=1, source_target_pairs={{0,1},{1,2},{2,3},{3,4},{4,5},{5,6},{6,7},{7,8},{8,9},{9,10},{10,1... | collective-permute-start | bytes 296 | tf_op jit(solution)/shard_map/ppermute | solution.py:26
  23.9 5.6 %collective-permute-start.11 = (f32[4,6,1]{2,1,0:T(8,128)S(1)}, f32[4,6,1]{2,1,0:T(8,128)S(1)}, u32[]{:S(2)}, u32[]{:S(2)}) collective-permute-start(f32[4,6,1]{2,1,0:T(8,128)S(1)} %get-tuple-element.49), channel_id=1, source_target_pairs={{1,0},{2,1},{3,2},{4,3},{5,4},{6,5},{7,6},{8,7},{9,8},{10,9},{11,1... | collective-permute-start | bytes 296 | tf_op jit(solution)/shard_map/ppermute | solution.py:28
  29.9 8.9 %collective-permute-start.2 = (bf16[16,4,1,256]{3,2,1,0:T(2,128)(2,1)S(1)}, bf16[16,4,1,256]{3,2,1,0:T(2,128)(2,1)S(1)}, u32[]{:S(2)}, u32[]{:S(2)}) collective-permute-start(bf16[16,4,1,256]{3,2,1,0:T(2,128)(2,1)S(1)} %get-tuple-element.34), channel_id=1, source_target_pairs={{0,32},{32,64},{64,96},{96,128},{128,160},{160,192},{192,224},{1,3... | collective-permute-start | bytes 98312 | tf_op jit(solution)/shard_map/ppermute | solution.py:26
  32.1 8.6 %collective-permute-start.3 = (bf16[16,4,1,256]{3,2,1,0:T(2,128)(2,1)S(1)}, bf16[16,4,1,256]{3,2,1,0:T(2,128)(2,1)S(1)}, u32[]{:S(2)}, u32[]{:S(2)}) collective-permute-start(bf16[16,4,1,256]{3,2,1,0:T(2,128)(2,1)S(1)} %get-tuple-element.35), channel_id=1, source_target_pairs={{32,0},{64,32},{96,64},{128,96},{160,128},{192,160},{224,192},{33,... | collective-permute-start | bytes 98312 | tf_op jit(solution)/shard_map/ppermute | solution.py:28
  41.0 5.1 %collective-permute-start.4 = (bf16[16,4,6,1]{3,2,1,0:T(8,128)(2,1)S(1)}, bf16[16,4,6,1]{3,2,1,0:T(8,128)(2,1)S(1)}, u32[]{:S(2)}, u32[]{:S(2)}) collective-permute-start(bf16[16,4,6,1]{3,2,1,0:T(8,128)(2,1)S(1)} %get-tuple-element.27), channel_id=1, source_target_pairs={{0,1},{1,2},{2,3},{3,4},{4,5},{5,6},{6,7},{7,8},{8,9},{9,10},{10,1... | collective-permute-start | bytes 2312 | tf_op jit(solution)/shard_map/ppermute | solution.py:26
  42.9 8.0 %collective-permute-start.5 = (bf16[16,4,6,1]{3,2,1,0:T(8,128)(2,1)S(1)}, bf16[16,4,6,1]{3,2,1,0:T(8,128)(2,1)S(1)}, u32[]{:S(2)}, u32[]{:S(2)}) collective-permute-start(bf16[16,4,6,1]{3,2,1,0:T(8,128)(2,1)S(1)} %get-tuple-element.26), channel_id=1, source_target_pairs={{1,0},{2,1},{3,2},{4,3},{5,4},{6,5},{7,6},{8,7},{9,8},{10,9},{11,1... | collective-permute-start | bytes 2312 | tf_op jit(solution)/shard_map/ppermute | solution.py:28
  52.4 1.6 copy-start.1
  54.0 0.7 copy-start.2
  54.0 1.2 copy-start.3
  54.7 1.1 copy-start.4
  55.2 1.1 copy-start.5
  55.8 1.1 copy-start.6
  56.3 1.1 copy-start.7
  56.9 1.1 copy-start.8
  58.7 0.9 copy-start
  224.6 2.9 collective-permute-start.12
  225.9 5.8 %collective-permute-start.13 = (bf16[16,1,4,256]{3,0,2,1:T(8,128)(2,1)S(1)}, bf16[16,1,4,256]{3,0,2,1:T(8,128)(2,1)S(1)}, u32[]{:S(2)}, u32[]{:S(2)}) collective-permute-start(bf16[16,1,4,256]{3,0,2,1:T(8,128)(2,1)S(1)} %get-tuple-element.37), channel_id=1, source_target_pairs={{256,0},{512,256},{768,512},{257,1},{513,257},{769,513},{258,2},{5... | collective-permute-start | bytes 98312 | tf_op jit(solution)/shard_map/ppermute | solution.py:28
  231.8 5.6 %collective-permute-start.14 = (bf16[16,4,1,256]{3,0,2,1:T(8,128)(2,1)S(1)}, bf16[16,4,1,256]{3,0,2,1:T(8,128)(2,1)S(1)}, u32[]{:S(2)}, u32[]{:S(2)}) collective-permute-start(bf16[16,4,1,256]{3,0,2,1:T(8,128)(2,1)S(1)} %get-tuple-element.32), channel_id=1, source_target_pairs={{0,32},{32,64},{64,96},{96,128},{128,160},{160,192},{192,224},{1,3... | collective-permute-start | bytes 98312 | tf_op jit(solution)/shard_map/ppermute | solution.py:26
  233.7 5.2 %collective-permute-start.15 = (bf16[16,4,1,256]{3,0,2,1:T(8,128)(2,1)S(1)}, bf16[16,4,1,256]{3,0,2,1:T(8,128)(2,1)S(1)}, u32[]{:S(2)}, u32[]{:S(2)}) collective-permute-start(bf16[16,4,1,256]{3,0,2,1:T(8,128)(2,1)S(1)} %get-tuple-element.33), channel_id=1, source_target_pairs={{32,0},{64,32},{96,64},{128,96},{160,128},{192,160},{224,192},{33,... | collective-permute-start | bytes 98312 | tf_op jit(solution)/shard_map/ppermute | solution.py:28
  239.1 3.9 %collective-permute-start.16 = (bf16[16,4,6,1]{3,0,2,1:T(8,128)(2,1)S(1)}, bf16[16,4,6,1]{3,0,2,1:T(8,128)(2,1)S(1)}, u32[]{:S(2)}, u32[]{:S(2)}) collective-permute-start(bf16[16,4,6,1]{3,0,2,1:T(8,128)(2,1)S(1)} %get-tuple-element.31), channel_id=1, source_target_pairs={{0,1},{1,2},{2,3},{3,4},{4,5},{5,6},{6,7},{7,8},{8,9},{9,10},{10,1... | collective-permute-start | bytes 2312 | tf_op jit(solution)/shard_map/ppermute | solution.py:26
  240.7 6.9 %collective-permute-start.17 = (bf16[16,4,6,1]{3,0,2,1:T(8,128)(2,1)S(1)}, bf16[16,4,6,1]{3,0,2,1:T(8,128)(2,1)S(1)}, u32[]{:S(2)}, u32[]{:S(2)}) collective-permute-start(bf16[16,4,6,1]{3,0,2,1:T(8,128)(2,1)S(1)} %get-tuple-element.30), channel_id=1, source_target_pairs={{1,0},{2,1},{3,2},{4,3},{5,4},{6,5},{7,6},{8,7},{9,8},{10,9},{11,1... | collective-permute-start | bytes 2312 | tf_op jit(solution)/shard_map/ppermute | solution.py:28
where the time goes:
time: 341 us; the launch traced here: 340 us
  blocking collectives  234 us (69%)
  starting transfers between devices  44.4 us (13%)
  waiting for transfers between devices  24.2 us (7%)
  other arithmetic  15.8 us (5%)
  matrix products  13.6 us (4%)
  local copies, waits for them, and re-layouts  6.08 us (2%)
    psum x8, blocking collectives, one_axis_at_a_time(): return functools.reduce(lax.psum, axes, value)  234 us
    ppermute x9, starting transfers between devices, padded_2(): lax.ppermute(tail, axis, [(i, (i + 1) % count) for i in range(ends)])  22.7 us
    ppermute x9, starting transfers between devices, padded_2(): lax.ppermute(head, axis, [((i + 1) % count, i) for i in range(ends)])  21.7 us
    ppermute x9, waiting for transfers between devices, padded_2(): lax.ppermute(head, axis, [((i + 1) % count, i) for i in range(ends)])  21.4 us
    dot_general x16, matrix products, apply_operator(): jnp.einsum('b,bcxyz->cxyz', kernel[corner], stacked, preferred_element_ty...  8.4 us
  transfers between devices with their start and end apart: 18, of which 11 were waited for; matrix products, arithmetic and copies ran while one was open for 1% of the time, Pallas kernels for 0%

commit v1 on v0

v1 whole, which is shorter than its diff:
```python
import functools

import jax
import jax.numpy as jnp
import numpy as np
from jax import lax
from jax.experimental import pallas as pl
from jax.experimental.pallas import tpu as pltpu
from jax.sharding import Mesh
from jax.sharding import PartitionSpec as P

PLANE = ("gx", "gy_0", "gy_1")
GY = ("gy_0", "gy_1")
SIGMA = 0.25
COLS = 16
LANES = 128
HIGH = lax.Precision.HIGHEST


def stiffness_table():
    line_mass = np.array([[1.0 / 3.0, 1.0 / 6.0], [1.0 / 6.0, 1.0 / 3.0]])
    line_stiff = np.array([[1.0, -1.0], [-1.0, 1.0]])
    table = np.zeros((8, 8))
    for target in range(8):
        for source in range(8):
            target_bits = [target >> 2 & 1, target >> 1 & 1, target & 1]
            source_bits = [source >> 2 & 1, source >> 1 & 1, source & 1]
            total = 0.0
            for stiff_dim in range(3):
                factor = 1.0
                for other in range(3):
                    if other == stiff_dim:
                        factor = factor * line_stiff[target_bits[other], source_bits[other]]
                    else:
                        factor = factor * line_mass[target_bits[other], source_bits[other]]
                total = total + factor
            table[target, source] = total
    return table


def kernel_scale():
    table = np.asarray(jnp.asarray(stiffness_table(), jnp.bfloat16).astype(jnp.float32))
    unit = -float(table[0, 7])
    for target in range(8):
        for source in range(8):
            bits = bin(target ^ source).count("1")
            want = (4.0, 0.0, -1.0, -1.0)[bits] * unit
            assert abs(float(table[target, source]) - want) < 1e-12
    return unit


UNIT = kernel_scale()


def lowered(value):
    return value.astype(jnp.bfloat16).astype(jnp.float32)


def shifted(tiles, step):
    lane = lax.broadcasted_iota(jnp.int32, tiles[0].shape, 1)
    turned = [pltpu.roll(t, (-step) % LANES, 1) for t in tiles]
    count = len(tiles)
    edge = lane < LANES - 1 if step == 1 else lane > 0
    return [jnp.where(edge, turned[i], turned[(i + step) % count]) for i in range(count)]


def operator(field, low, above, below, both, x, y, wx, wy):
    plane, up, down = [], [], []
    for tile in range(3):
        around = {
            (i, j): low(x + i, y + j, tile) for i in (-1, 0, 1) for j in (-1, 0, 1)
        }
        centre = 4.0 * around[0, 0]
        in_plane, from_above, from_below = None, None, None
        for i in (-1, 1):
            for j in (-1, 1):
                ex, ey = wx + (i - 1) // 2, wy + (j - 1) // 2
                others = around[i, 0] + around[0, j] + around[i, j]
                terms = (
                    both(ex, ey, tile) * (centre - around[i, j]),
                    below(ex, ey, tile) * others,
                    above(ex, ey, tile) * others,
                )
                if in_plane is None:
                    in_plane, from_above, from_below = terms
                else:
                    in_plane = in_plane + terms[0]
                    from_above = from_above + terms[1]
                    from_below = from_below + terms[2]
        plane.append(in_plane)
        up.append(from_above)
        down.append(from_below)
    up, down = shifted(up, 1), shifted(down, -1)
    return [SIGMA * field(t) + (plane[t] - up[t] - down[t]) for t in range(3)]


def tile_of(tile):
    return slice(tile * LANES, (tile + 1) * LANES)


def moments_kernel(v_ref, e_ref, q_ref, above_ref, below_ref, both_ref, g_ref, low_ref, qlow_ref, w_ref):
    ext_x, ext_y = v_ref.shape[0], v_ref.shape[1]
    for ex in range(ext_x - 1):
        for tile in range(3):
            pass
        flat = []
        for tile in range(3):
            ours = e_ref[ex * ext_y : ex * ext_y + ext_y, tile_of(tile)]
            next_x = e_ref[(ex + 1) * ext_y : (ex + 1) * ext_y + ext_y, tile_of(tile)]
            both_x = ours + next_x
            flat.append(both_x + pltpu.roll(both_x, ext_y - 1, 0))
        ahead = shifted(flat, 1)
        weights = [(0.125 * UNIT) * (flat[t] + ahead[t]) for t in range(3)]
        behind = shifted(weights, -1)
        for t in range(3):
            above_ref[ex, :, tile_of(t)] = weights[t]
            below_ref[ex, :, tile_of(t)] = behind[t]
            both_ref[ex, :, tile_of(t)] = weights[t] + behind[t]
    for x in range(ext_x):
        for y in range(ext_y):
            low_ref[x, y] = lowered(v_ref[x, y])

    def weight(ref):
        return lambda ex, ey, t: ref[ex, ey : ey + 1, tile_of(t)]

    sides = (weight(above_ref), weight(below_ref), weight(both_ref))
    for x in range(1, ext_x - 1):
        for y in range(1, ext_y - 1):
            image = operator(
                lambda t: v_ref[x, y, :, tile_of(t)],
                lambda i, j, t: low_ref[i, j, :, tile_of(t)],
                *sides,
                x,
                y,
                x,
                y,
            )
            for t in range(3):
                inside = e_ref[x * ext_y + y : x * ext_y + y + 1, tile_of(t)] > 0.0
                value = jnp.where(inside, image[t], 0.0)
                q_ref[x - 1, y - 1, :, tile_of(t)] = value
                qlow_ref[x - 1, y - 1, :, tile_of(t)] = lowered(value)
    total = jnp.zeros((2 * COLS, LANES), jnp.float32)
    pad = jnp.zeros((LANES - 3 * COLS, 2 * LANES), jnp.float32)
    for x in range(2, ext_x - 2):
        for y in range(2, ext_y - 2):
            image = operator(
                lambda t: q_ref[x - 1, y - 1, :, tile_of(t)],
                lambda i, j, t: qlow_ref[i, j, :, tile_of(t)],
                *sides,
                x - 1,
                y - 1,
                x,
                y,
            )
            b = v_ref[x, y, :, : 2 * LANES]
            q = q_ref[x - 1, y - 1, :, : 2 * LANES]
            w = jnp.concatenate(image[:2], axis=1)
            left = jnp.concatenate([b, q], axis=0)
            right = jnp.concatenate([b, q, w, pad], axis=0)
            total = total + lax.dot_general(
                left, right, (((1,), (1,)), ((), ())), precision=HIGH, preferred_element_type=jnp.float32
            )
    lane = lax.broadcasted_iota(jnp.int32, (8, LANES), 1)
    first, second = total[:COLS], total[COLS:]
    crossed = 0.5 * (first + pltpu.roll(second, COLS, 1))
    lane16 = lax.broadcasted_iota(jnp.int32, (COLS, LANES), 1)
    low_pair = jnp.where(lane16 < COLS, first, crossed)
    high_pair = pltpu.roll(second, LANES - COLS, 1)
    quarters = (low_pair[:8], low_pair[8:], high_pair[:8], high_pair[8:])
    packed = jnp.where(lane < 2 * COLS, quarters[0], 0.0)
    for n in range(1, 4):
        moved = pltpu.roll(quarters[n], 2 * COLS * n, 1)
        packed = jnp.where((lane >= 2 * COLS * n) & (lane < 2 * COLS * (n + 1)), moved, packed)
    g_ref[...] = packed


def dot(left, right, dims=((1,), (0,))):
    return lax.dot_general(left, right, (dims, ((), ())), precision=HIGH, preferred_element_type=jnp.float32)


def inverse(matrix):
    size = COLS
    sub = lax.broadcasted_iota(jnp.int32, (size, LANES), 0)
    rows = [jnp.broadcast_to(matrix[:, i : i + 1], (size, LANES)) for i in range(size)]
    for k in range(size):
        scale = 1.0 / rows[k][k : k + 1, :]
        pivot_row = rows[k] * scale
        for i in range(size):
            if i != k:
                factor = rows[i][k : k + 1, :]
                moved = rows[i] - factor * pivot_row
                rows[i] = jnp.where(sub == k, factor * scale, moved)
        rows[k] = jnp.where(sub == k, -scale, pivot_row)
    lane = lax.broadcasted_iota(jnp.int32, (size, LANES), 1)
    out = jnp.zeros((size, LANES), jnp.float32)
    for i in range(size):
        out = jnp.where(lane == i, -rows[i], out)
    return out[:, :size]


def solve(matrix, right):
    inv = inverse(matrix)
    guess = dot(inv, right)
    return guess + dot(inv, right - dot(matrix, guess))


def finish_kernel(g_ref, v_ref, e_ref, q_ref, above_ref, below_ref, both_ref, sol_ref, res_ref, d_ref, dlow_ref):
    ext_x, ext_y = v_ref.shape[0], v_ref.shape[1]
    packed = g_ref[...]
    turned = [packed] + [pltpu.roll(packed, LANES - 2 * COLS * n, 1) for n in range(1, 4)]
    low_pair = jnp.concatenate(turned[:2], axis=0)
    high_pair = jnp.concatenate(turned[2:], axis=0)
    m0 = low_pair[:, :COLS]
    m1 = pltpu.roll(low_pair, LANES - COLS, 1)[:, :COLS]
    m2 = high_pair[:, :COLS]
    m3 = pltpu.roll(high_pair, LANES - COLS, 1)[:, :COLS]
    first = ((0,), (0,))
    alpha = solve(m1, m0)
    m1a, m2a, m3a = dot(m1, alpha), dot(m2, alpha), dot(m3, alpha)
    updated = m0 - m1a - dot(alpha, m1, first) + dot(alpha, m2a, first)
    beta = solve(m0, updated)
    row = lax.broadcasted_iota(jnp.int32, (COLS, COLS), 0)
    col = lax.broadcasted_iota(jnp.int32, (COLS, COLS), 1)
    mix = beta + jnp.where(row == col, 1.0, 0.0)
    curved = dot(mix, dot(m1, mix) - m2a, first) + dot(alpha, m3a - dot(m2, mix), first)
    curved = 0.5 * (curved + curved.T)
    gamma = solve(curved, updated)
    both = jnp.concatenate([mix, -alpha], axis=0)
    for x in range(1, ext_x - 1):
        for y in range(1, ext_y - 1):
            block = jnp.concatenate([v_ref[x, y], q_ref[x - 1, y - 1]], axis=0)
            value = dot(both, block, first)
            inside = e_ref[x * ext_y + y : x * ext_y + y + 1, :] > 0.0
            value = jnp.where(inside, value, 0.0)
            d_ref[x - 1, y - 1] = value
            dlow_ref[x - 1, y - 1] = lowered(value)

    def weight(ref):
        return lambda ex, ey, t: ref[ex, ey : ey + 1, tile_of(t)]

    sides = (weight(above_ref), weight(below_ref), weight(both_ref))
    zero = jnp.zeros((COLS, COLS), jnp.float32)
    to_sol = jnp.concatenate([alpha, gamma, zero], axis=0)
    to_res = jnp.concatenate([-alpha, -gamma], axis=0)
    for x in range(2, ext_x - 2):
        for y in range(2, ext_y - 2):
            image = operator(
                lambda t: d_ref[x - 1, y - 1, :, tile_of(t)],
                lambda i, j, t: dlow_ref[i, j, :, tile_of(t)],
                *sides,
                x - 1,
                y - 1,
                x,
                y,
            )
            b = v_ref[x, y, :, : 2 * LANES]
            q = q_ref[x - 1, y - 1, :, : 2 * LANES]
            d = d_ref[x - 1, y - 1, :, : 2 * LANES]
            i2 = jnp.concatenate(image[:2], axis=1)
            sol_ref[x - 2, y - 2] = dot(to_sol[: 2 * COLS], jnp.concatenate([b, d], axis=0), first)
            res_ref[x - 2, y - 2] = b + dot(to_res, jnp.concatenate([q, i2], axis=0), first)


def ring(axis, step):
    count = lax.axis_size(axis)
    ends = range(count - 1)
    return [(i, i + 1) for i in ends] if step > 0 else [(i + 1, i) for i in ends]


def both_ways(axis, to_next, to_last):
    return lax.ppermute(to_next, axis, ring(axis, 1)), lax.ppermute(to_last, axis, ring(axis, -1))


def spread(value, axes):
    count = lax.axis_size(axes)
    copies = jnp.broadcast_to(value[None], (count, *value.shape))
    return jnp.sum(lax.all_to_all(copies, axes, 0, 0), axis=0)


def on_device(loads, moduli, material):
    levels = jnp.arange(moduli.shape[0], dtype=jnp.int32)
    modulus = jnp.sum(jnp.where(material[..., None] == levels, moduli, 0.0), axis=-1)
    own = jnp.concatenate([loads, modulus[None]], axis=0)
    before, after = both_ways("gz", own[..., LANES:], own[..., :LANES])
    lane = lax.broadcasted_iota(jnp.int32, before.shape, 3)
    own = jnp.concatenate([own, jnp.where(lane < LANES // 2, after, before)], axis=3)
    before, after = both_ways("gx", own, own)
    own = jnp.concatenate([before, own, after], axis=1)
    before, after = both_ways(GY, own[:, :, 2:], own[:, :, :2])
    own = jnp.concatenate([before, own, after], axis=2)
    ext_x, ext_y = own.shape[1], own.shape[2]
    block = jnp.transpose(own[:COLS], (1, 2, 0, 3))
    modulus = own[COLS].reshape(ext_x * ext_y, 3 * LANES)
    f32 = jnp.float32
    wide = 3 * LANES
    weights = jax.ShapeDtypeStruct((ext_x - 1, ext_y, wide), f32)
    image, above, below, both, moments = pl.pallas_call(
        moments_kernel,
        out_shape=(
            jax.ShapeDtypeStruct((ext_x - 2, ext_y - 2, COLS, wide), f32),
            weights,
            weights,
            weights,
            jax.ShapeDtypeStruct((8, LANES), f32),
        ),
        scratch_shapes=[
            pltpu.VMEM((ext_x, ext_y, COLS, wide), f32),
            pltpu.VMEM((ext_x - 2, ext_y - 2, COLS, wide), f32),
            pltpu.VMEM((8, 128), f32),
        ],
        name="moments",
    )(block, modulus)
    moments = spread(spread(moments, PLANE), "gz")
    out = jax.ShapeDtypeStruct((ext_x - 4, ext_y - 4, COLS, 2 * LANES), f32)
    solution, residual = pl.pallas_call(
        finish_kernel,
        out_shape=(out, out),
        scratch_shapes=[pltpu.VMEM((ext_x - 2, ext_y - 2, COLS, wide), f32)] * 2,
        name="finish",
    )(moments, block, modulus, image, above, below, both)
    return jnp.transpose(solution, (2, 0, 1, 3)), jnp.transpose(residual, (2, 0, 1, 3))


def solution(mesh):
    wide, long = mesh.shape["gy"] // 2, mesh.shape["gz"]
    split = Mesh(mesh.devices.reshape(mesh.shape["gx"], wide, 2, long), ("gx", "gy_0", "gy_1", "gz"))
    spec = P(None, "gx", GY, "gz")
    return jax.shard_map(
        on_device,
        mesh=split,
        in_specs=(spec, P(), P("gx", GY, "gz")),
        out_specs=(spec, spec),
        check_vma=False,
    )
```

time: 341 us -> 128 us (0.38)
  the two profiles are of different devices: /device:TPU:2 before, /device:TPU:1 now
where the time goes in v1:
time: 128 us; the launch traced here: 127 us
  blocking collectives  71.5 us (56%)
  starting transfers between devices  27.3 us (21%)
  Pallas kernels  9.99 us (8%)
  waiting for transfers between devices  9.25 us (7%)
  local copies, waits for them, and re-layouts  6.84 us (5%)
  other arithmetic  1.76 us (1%)
    all_to_all x2, blocking collectives, spread(): return jnp.sum(lax.all_to_all(copies, axes, 0, 0), axis=0)  71.5 us
    ppermute x3, starting transfers between devices, both_ways(): lax.ppermute(to_next, axis, ring(axis, 1))  14.9 us
    ppermute x3, starting transfers between devices, both_ways(): lax.ppermute(to_last, axis, ring(axis, -1))  12.4 us
    ppermute x3, waiting for transfers between devices, both_ways(): lax.ppermute(to_last, axis, ring(axis, -1))  7.47 us
    pallas_call x1, Pallas kernels, on_device(): pl.pallas_call(finish_kernel, out_shape=(out, out), scratch_shapes=[pltpu...  6.47 us
    unnamed x4, local copies, waits for them, and re-layouts  4.88 us
    pallas_call x1, Pallas kernels, on_device(): pl.pallas_call(moments_kernel, out_shape=(jax.ShapeDtypeStruct((ext_x - 2...  3.52 us
  transfers between devices with their start and end apart: 6, of which 5 were waited for; matrix products, arithmetic and copies ran while one was open for 0% of the time, Pallas kernels for 0%

profile of v1, /device:TPU:1, one launch (start us, length us, event | category | flops | bytes accessed | tf_op | source)
XLA Modules:
  0.0 127.4 jit_solution(15268304694726151252)
XLA Ops:
  0.6 0.8 select_reduce_fusion
  1.5 1.0 copy_dynamic-update-slice_fusion
  2.4 0.1 dynamic-update-slice.1
  2.5 4.4 %collective-permute-start.1 = (f32[17,2,4,128]{3,0,2,1:T(8,128)S(1)}, f32[17,2,4,128]{3,0,2,1:T(8,128)S(1)}, u32[]{:S(2)}, u32[]{:S(2)}) collective-permute-start(f32[17,2,4,128]{3,0,2,1:T(8,128)S(1)} %get-tuple-element.22), channel_id=1, source_target_pairs={{0,1},{1,2},{2,3},{3,4},{4,5},{5,6},{6,7},{7,8},{8,9},{9,10},{10,1... | collective-permute-start | bytes 208904 | tf_op jit(solution)/shard_map/ppermute | solution.py:272
  6.9 1.3 %collective-permute-start = (f32[17,2,4,128]{3,0,2,1:T(8,128)S(1)}, f32[17,2,4,128]{3,0,2,1:T(8,128)S(1)}, u32[]{:S(2)}, u32[]{:S(2)}) collective-permute-start(f32[17,2,4,128]{3,0,2,1:T(8,128)S(1)} %get-tuple-element.23), channel_id=1, source_target_pairs={{1,0},{2,1},{3,2},{4,3},{5,4},{6,5},{7,6},{8,7},{9,8},{10,9},{11,1... | collective-permute-start | bytes 208904 | tf_op jit(solution)/shard_map/ppermute | solution.py:272
  8.2 0.3 collective-permute-done.1
  8.5 3.9 %collective-permute-done = f32[17,2,4,128]{3,0,2,1:T(8,128)S(1)} collective-permute-done((f32[17,2,4,128]{3,0,2,1:T(8,128)S(1)}, f32[17,2,4,128]{3,0,2,1:T(8,128)S(1)}, u32[]{:S(2)}, u32[]{:S(2)}) %collective-permute-start) | collective-permute-done | bytes 69664 | tf_op jit(solution)/shard_map/ppermute | solution.py:272
  12.5 1.3 %collective-permute-start.3 = (f32[17,2,4,384]{3,0,2,1:T(8,128)S(1)}, f32[17,2,4,384]{3,0,2,1:T(8,128)S(1)}, u32[]{:S(2)}, u32[]{:S(2)}) collective-permute-start(f32[17,2,4,384]{3,0,2,1:T(8,128)S(1)} %pad_maximum_fusion.2), channel_id=1, source_target_pairs={{256,0},{512,256},{768,512},{257,1},{513,257},{769,513},{258,2},{5... | collective-permute-start | bytes 626696 | tf_op jit(solution)/shard_map/ppermute | solution.py:272
  13.8 4.0 %collective-permute-start.2 = (f32[17,2,4,384]{3,0,2,1:T(8,128)S(1)}, f32[17,2,4,384]{3,0,2,1:T(8,128)S(1)}, u32[]{:S(2)}, u32[]{:S(2)}) collective-permute-start(f32[17,2,4,384]{3,0,2,1:T(8,128)S(1)} %pad_maximum_fusion.2), channel_id=1, source_target_pairs={{0,256},{256,512},{512,768},{1,257},{257,513},{513,769},{2,258},{2... | collective-permute-start | bytes 626696 | tf_op jit(solution)/shard_map/ppermute | solution.py:272
  17.8 2.2 %collective-permute-done.3 = f32[17,2,4,384]{3,0,2,1:T(8,128)S(1)} collective-permute-done((f32[17,2,4,384]{3,0,2,1:T(8,128)S(1)}, f32[17,2,4,384]{3,0,2,1:T(8,128)S(1)}, u32[]{:S(2)}, u32[]{:S(2)}) %collective-permute-start.3) | collective-permute-done | bytes 208928 | tf_op jit(solution)/shard_map/ppermute | solution.py:272
  19.9 1.5 %collective-permute-done.2 = f32[17,2,4,384]{3,0,2,1:T(8,128)S(1)} collective-permute-done((f32[17,2,4,384]{3,0,2,1:T(8,128)S(1)}, f32[17,2,4,384]{3,0,2,1:T(8,128)S(1)}, u32[]{:S(2)}, u32[]{:S(2)}) %collective-permute-start.2) | collective-permute-done | bytes 208928 | tf_op jit(solution)/shard_map/ppermute | solution.py:272
  21.4 0.1 pad_maximum_fusion.1
  21.5 0.1 fusion
  21.5 6.6 %collective-permute-start.4 = (f32[17,6,2,384]{3,0,2,1:T(8,128)S(1)}, f32[17,6,2,384]{3,0,2,1:T(8,128)S(1)}, u32[]{:S(2)}, u32[]{:S(2)}) collective-permute-start(f32[17,6,2,384]{3,0,2,1:T(8,128)S(1)} %get-tuple-element.20), channel_id=1, source_target_pairs={{0,32},{32,64},{64,96},{96,128},{128,160},{160,192},{192,224},{1,3... | collective-permute-start | bytes 940040 | tf_op jit(solution)/shard_map/ppermute | solution.py:272
  28.1 9.8 %collective-permute-start.5 = (f32[17,6,2,384]{3,0,2,1:T(8,128)S(1)}, f32[17,6,2,384]{3,0,2,1:T(8,128)S(1)}, u32[]{:S(2)}, u32[]{:S(2)}) collective-permute-start(f32[17,6,2,384]{3,0,2,1:T(8,128)S(1)} %get-tuple-element.21), channel_id=1, source_target_pairs={{32,0},{64,32},{96,64},{128,96},{160,128},{192,160},{224,192},{33,... | collective-permute-start | bytes 940040 | tf_op jit(solution)/shard_map/ppermute | solution.py:272
  37.9 0.0 collective-permute-done.4
  37.9 1.4 %collective-permute-done.5 = f32[17,6,2,384]{3,0,2,1:T(8,128)S(1)} collective-permute-done((f32[17,6,2,384]{3,0,2,1:T(8,128)S(1)}, f32[17,6,2,384]{3,0,2,1:T(8,128)S(1)}, u32[]{:S(2)}, u32[]{:S(2)}) %collective-permute-start.5) | collective-permute-done | bytes 313376 | tf_op jit(solution)/shard_map/ppermute | solution.py:272
  39.3 0.1 pad_maximum_fusion
  39.5 1.1 slice_bitcast_fusion.v_ref
  40.6 0.1 pad_maximum_fusion.3
  40.6 0.6 copy.14
  41.3 3.5 %moments.1 = (f32[4,6,16,384]{3,2,1,0:T(8,128)}, f32[5,8,384]{2,1,0:T(8,128)}, f32[5,8,384]{2,1,0:T(8,128)}, f32[5,8,384]{2,1,0:T(8,128)}, f32[8,128]{1,0:T(8,128)}) custom-call(f32[6,8,16,384]{3,2,1,0:T(8,128)} %slice_bitcast_fusion.v_ref, f32[48,384]{1,0:T(8,128)} %bitcast.7), custom_call_target="tpu_custom_call" | custom-call | tf_op jit(solution)/shard_map/moments/pallas_call | solution.py:298
  44.8 0.7 broadcast_in_dim.28
  45.5 13.7 %all_to_all.10 = f32[32,8,128]{2,1,0:T(8,128)S(1)} all-to-all(f32[32,8,128]{2,1,0:T(8,128)S(1)} %broadcast_in_dim.28), channel_id=1, replica_groups=mesh['gx'=4,'gy_0'=4,'gy_1'=2,'gz'=32] {'gx','gy_0','gy_1'}, dimensions={0} | all-to-all | bytes 262144 | tf_op jit(solution)/shard_map/all_to_all | solution.py:278
  59.3 57.8 %all_to_all.11 = f32[32,8,128]{2,1,0:T(8,128)S(1)} all-to-all(f32[32,8,128]{2,1,0:T(8,128)S(1)} %broadcast_in_dim.29), channel_id=1, replica_groups=mesh['gx'=4,'gy_0'=4,'gy_1'=2,'gz'=32] {'gz'}, dimensions={0} | all-to-all | bytes 262144 | tf_op jit(solution)/shard_map/all_to_all | solution.py:278
  117.0 0.6 reduce_sum.29.g_ref
  117.7 6.5 %finish.1 = (f32[2,4,16,256]{3,2,1,0:T(8,128)}, f32[2,4,16,256]{3,2,1,0:T(8,128)}) custom-call(f32[8,128]{1,0:T(8,128)} %reduce_sum.29.g_ref, f32[6,8,16,384]{3,2,1,0:T(8,128)} %slice_bitcast_fusion.v_ref, f32[48,384]{1,0:T(8,128)} %bitcast.8, f32[4,6,16,384]{3,2,1,0:T(8,128)} %get-tuple-element.10.q_ref, f32[5,8,384]{2,1,0:T(8,128)} %get-tuple-element.11.above_ref, ...), custom_call_target="tpu_custom_call" | custom-call | tf_op jit(solution)/shard_map/finish/pallas_call | solution.py:316
  124.1 1.6 %copy.9 = f32[16,2,4,256]{3,2,1,0:T(4,128)} copy(f32[16,2,4,256]{3,0,2,1:T(8,128)} %bitcast.10) | data formatting | bytes 262144
  125.8 1.6 %copy.10 = f32[16,2,4,256]{3,2,1,0:T(4,128)} copy(f32[16,2,4,256]{3,0,2,1:T(8,128)} %bitcast.9) | data formatting | bytes 262144
  (7 shorter events, 0.1 us)
Async XLA Ops:
  2.5 6.0 %collective-permute-start.1 = (f32[17,2,4,128]{3,0,2,1:T(8,128)S(1)}, f32[17,2,4,128]{3,0,2,1:T(8,128)S(1)}, u32[]{:S(2)}, u32[]{:S(2)}) collective-permute-start(f32[17,2,4,128]{3,0,2,1:T(8,128)S(1)} %get-tuple-element.22), channel_id=1, source_target_pairs={{0,1},{1,2},{2,3},{3,4},{4,5},{5,6},{6,7},{7,8},{8,9},{9,10},{10,1... | collective-permute-start | bytes 208904 | tf_op jit(solution)/shard_map/ppermute | solution.py:272
  6.9 5.5 %collective-permute-start = (f32[17,2,4,128]{3,0,2,1:T(8,128)S(1)}, f32[17,2,4,128]{3,0,2,1:T(8,128)S(1)}, u32[]{:S(2)}, u32[]{:S(2)}) collective-permute-start(f32[17,2,4,128]{3,0,2,1:T(8,128)S(1)} %get-tuple-element.23), channel_id=1, source_target_pairs={{1,0},{2,1},{3,2},{4,3},{5,4},{6,5},{7,6},{8,7},{9,8},{10,9},{11,1... | collective-permute-start | bytes 208904 | tf_op jit(solution)/shard_map/ppermute | solution.py:272
  12.5 7.5 %collective-permute-start.3 = (f32[17,2,4,384]{3,0,2,1:T(8,128)S(1)}, f32[17,2,4,384]{3,0,2,1:T(8,128)S(1)}, u32[]{:S(2)}, u32[]{:S(2)}) collective-permute-start(f32[17,2,4,384]{3,0,2,1:T(8,128)S(1)} %pad_maximum_fusion.2), channel_id=1, source_target_pairs={{256,0},{512,256},{768,512},{257,1},{513,257},{769,513},{258,2},{5... | collective-permute-start | bytes 626696 | tf_op jit(solution)/shard_map/ppermute | solution.py:272
  13.8 7.6 %collective-permute-start.2 = (f32[17,2,4,384]{3,0,2,1:T(8,128)S(1)}, f32[17,2,4,384]{3,0,2,1:T(8,128)S(1)}, u32[]{:S(2)}, u32[]{:S(2)}) collective-permute-start(f32[17,2,4,384]{3,0,2,1:T(8,128)S(1)} %pad_maximum_fusion.2), channel_id=1, source_target_pairs={{0,256},{256,512},{512,768},{1,257},{257,513},{513,769},{2,258},{2... | collective-permute-start | bytes 626696 | tf_op jit(solution)/shard_map/ppermute | solution.py:272
  21.5 16.4 %collective-permute-start.4 = (f32[17,6,2,384]{3,0,2,1:T(8,128)S(1)}, f32[17,6,2,384]{3,0,2,1:T(8,128)S(1)}, u32[]{:S(2)}, u32[]{:S(2)}) collective-permute-start(f32[17,6,2,384]{3,0,2,1:T(8,128)S(1)} %get-tuple-element.20), channel_id=1, source_target_pairs={{0,32},{32,64},{64,96},{96,128},{128,160},{160,192},{192,224},{1,3... | collective-permute-start | bytes 940040 | tf_op jit(solution)/shard_map/ppermute | solution.py:272
  28.1 11.2 %collective-permute-start.5 = (f32[17,6,2,384]{3,0,2,1:T(8,128)S(1)}, f32[17,6,2,384]{3,0,2,1:T(8,128)S(1)}, u32[]{:S(2)}, u32[]{:S(2)}) collective-permute-start(f32[17,6,2,384]{3,0,2,1:T(8,128)S(1)} %get-tuple-element.21), channel_id=1, source_target_pairs={{32,0},{64,32},{96,64},{128,96},{160,128},{192,160},{224,192},{33,... | collective-permute-start | bytes 940040 | tf_op jit(solution)/shard_map/ppermute | solution.py:272

commit v2 on v1

--- a/solution.py
+++ b/solution.py
@@ -98,16 +98,59 @@
     return slice(tile * LANES, (tile + 1) * LANES)
 
 
-def moments_kernel(v_ref, e_ref, q_ref, above_ref, below_ref, both_ref, g_ref, low_ref, qlow_ref, w_ref):
-    ext_x, ext_y = v_ref.shape[0], v_ref.shape[1]
+def pack_kernel(n_ref, lo_ref, hi_ref, ext_x, ext_y):
+    nodes = ext_x * ext_y
+    for first, out_ref in ((True, lo_ref), (False, hi_ref)):
+        base = 0 if first else n_ref.shape[0] // 2
+        turn = 0 if first else 2
+        lane = lax.broadcasted_iota(jnp.int32, (COLS, LANES), 1)
+        packed = jnp.zeros((COLS, LANES), jnp.float32)
+        for node in range(nodes):
+            value = n_ref[pl.ds(base + node, COLS, stride=nodes), :]
+            shift = (2 * node + turn) % LANES
+            moved = pltpu.roll(value, shift, 1) if shift else value
+            packed = jnp.where(lane // 2 == node, moved, packed)
+        out_ref[:COLS, :] = packed
+        lane = lax.broadcasted_iota(jnp.int32, (ext_y, LANES), 1)
+        packed = jnp.zeros((ext_y, LANES), jnp.float32)
+        for x in range(ext_x):
+            start = base + COLS * nodes + x * ext_y
+            value = n_ref[start : start + ext_y, :]
+            shift = (2 * x + turn) % LANES
+            moved = pltpu.roll(value, shift, 1) if shift else value
+            packed = jnp.where(lane // 2 == x, moved, packed)
+        out_ref[COLS : COLS + ext_y, :] = packed
+
+
+def ends_tile(before, after, index):
+    lane = lax.broadcasted_iota(jnp.int32, before.shape, 1)
+    back, ahead = (-2 * index) % LANES, (LANES - 2 - 2 * index) % LANES
+    follows = pltpu.roll(after, back, 1) if back else after
+    comes = pltpu.roll(before, ahead, 1) if ahead else before
+    return jnp.where(lane < 2, follows, jnp.where(lane >= LANES - 2, comes, 0.0))
+
+
+def moments_kernel(
+    moduli_ref, n_ref, before_ref, after_ref,
+    v_ref, q_ref, above_ref, below_ref, both_ref, g_ref,
+    low_ref, qlow_ref, e_ref,
+):
+    ext_x, ext_y = low_ref.shape[0], low_ref.shape[1]
+    nodes = ext_x * ext_y
+    base = n_ref.shape[0] // 2
+    for x in range(ext_x):
+        start = COLS * nodes + x * ext_y
+        third = ends_tile(before_ref[COLS : COLS + ext_y, :], after_ref[COLS : COLS + ext_y, :], x)
+        tiles = [n_ref[t * base + start : t * base + start + ext_y, :] for t in range(2)] + [third]
+        for t in range(3):
+            modulus = jnp.zeros_like(third)
+            for level in range(moduli_ref.shape[0]):
+                modulus = jnp.where(tiles[t] == level + 1.0, moduli_ref[level], modulus)
+            e_ref[x, :, tile_of(t)] = modulus
     for ex in range(ext_x - 1):
-        for tile in range(3):
-            pass
         flat = []
-        for tile in range(3):
-            ours = e_ref[ex * ext_y : ex * ext_y + ext_y, tile_of(tile)]
-            next_x = e_ref[(ex + 1) * ext_y : (ex + 1) * ext_y + ext_y, tile_of(tile)]
-            both_x = ours + next_x
+        for t in range(3):
+            both_x = e_ref[ex, :, tile_of(t)] + e_ref[ex + 1, :, tile_of(t)]
             flat.append(both_x + pltpu.roll(both_x, ext_y - 1, 0))
         ahead = shifted(flat, 1)
         weights = [(0.125 * UNIT) * (flat[t] + ahead[t]) for t in range(3)]
@@ -116,9 +159,16 @@
             above_ref[ex, :, tile_of(t)] = weights[t]
             below_ref[ex, :, tile_of(t)] = behind[t]
             both_ref[ex, :, tile_of(t)] = weights[t] + behind[t]
+    before, after = before_ref[:COLS, :], after_ref[:COLS, :]
     for x in range(ext_x):
         for y in range(ext_y):
-            low_ref[x, y] = lowered(v_ref[x, y])
+            node = x * ext_y + y
+            tiles = [n_ref[pl.ds(t * base + node, COLS, stride=nodes), :] for t in range(2)]
+            tiles.append(ends_tile(before, after, node))
+            for t in range(3):
+                low_ref[x, y, :, tile_of(t)] = lowered(tiles[t])
+                if 0 < x < ext_x - 1 and 0 < y < ext_y - 1:
+                    v_ref[x - 1, y - 1, :, tile_of(t)] = tiles[t]
 
     def weight(ref):
         return lambda ex, ey, t: ref[ex, ey : ey + 1, tile_of(t)]
@@ -127,7 +177,7 @@
     for x in range(1, ext_x - 1):
         for y in range(1, ext_y - 1):
             image = operator(
-                lambda t: v_ref[x, y, :, tile_of(t)],
+                lambda t: v_ref[x - 1, y - 1, :, tile_of(t)],
                 lambda i, j, t: low_ref[i, j, :, tile_of(t)],
                 *sides,
                 x,
@@ -136,7 +186,7 @@
                 y,
             )
             for t in range(3):
-                inside = e_ref[x * ext_y + y : x * ext_y + y + 1, tile_of(t)] > 0.0
+                inside = e_ref[x, y : y + 1, tile_of(t)] > 0.0
                 value = jnp.where(inside, image[t], 0.0)
                 q_ref[x - 1, y - 1, :, tile_of(t)] = value
                 qlow_ref[x - 1, y - 1, :, tile_of(t)] = lowered(value)
@@ -153,7 +203,7 @@
                 x,
                 y,
             )
-            b = v_ref[x, y, :, : 2 * LANES]
+            b = v_ref[x - 1, y - 1, :, : 2 * LANES]
             q = q_ref[x - 1, y - 1, :, : 2 * LANES]
             w = jnp.concatenate(image[:2], axis=1)
             left = jnp.concatenate([b, q], axis=0)
@@ -161,18 +211,61 @@
             total = total + lax.dot_general(
                 left, right, (((1,), (1,)), ((), ())), precision=HIGH, preferred_element_type=jnp.float32
             )
-    lane = lax.broadcasted_iota(jnp.int32, (8, LANES), 1)
+    g_ref[...] = pack_moments(total)
+
+
+def pack_moments(total):
     first, second = total[:COLS], total[COLS:]
-    crossed = 0.5 * (first + pltpu.roll(second, COLS, 1))
-    lane16 = lax.broadcasted_iota(jnp.int32, (COLS, LANES), 1)
-    low_pair = jnp.where(lane16 < COLS, first, crossed)
-    high_pair = pltpu.roll(second, LANES - COLS, 1)
-    quarters = (low_pair[:8], low_pair[8:], high_pair[:8], high_pair[8:])
-    packed = jnp.where(lane < 2 * COLS, quarters[0], 0.0)
-    for n in range(1, 4):
-        moved = pltpu.roll(quarters[n], 2 * COLS * n, 1)
-        packed = jnp.where((lane >= 2 * COLS * n) & (lane < 2 * COLS * (n + 1)), moved, packed)
-    g_ref[...] = packed
+    row = lax.broadcasted_iota(jnp.int32, (COLS, LANES), 0)
+    lane = lax.broadcasted_iota(jnp.int32, (COLS, LANES), 1)
+    col = lane % COLS
+    upper = jnp.where(lane < COLS, first, second)
+    lower = jnp.where(
+        lane < COLS,
+        0.5 * (pltpu.roll(first, LANES - COLS, 1) + second),
+        pltpu.roll(second, LANES - COLS, 1),
+    )
+    valid = lane < 2 * COLS
+    square = jnp.where(valid, jnp.where(row <= col, upper, lower), 0.0)
+    diagonal = jnp.sum(jnp.where(valid & (row == col), lower, 0.0), axis=0, keepdims=True)
+    out = []
+    for half in range(2):
+        out.append(square[8 * half : 8 * half + 8])
+    spread_rows = jnp.zeros((8, LANES), jnp.float32)
+    sub8 = lax.broadcasted_iota(jnp.int32, (8, LANES), 0)
+    lane8 = lax.broadcasted_iota(jnp.int32, (8, LANES), 1)
+    for quarter in range(4):
+        piece = out[quarter // 2]
+        if quarter % 2:
+            piece = pltpu.roll(piece, 4, 0)
+        if quarter:
+            piece = pltpu.roll(piece, 2 * COLS * quarter, 1)
+        here = (sub8 < 4) & (lane8 // (2 * COLS) == quarter)
+        spread_rows = jnp.where(here, piece, spread_rows)
+    return jnp.where(sub8 == 4, diagonal, spread_rows)
+
+
+def unpack_moments(packed):
+    sub8 = lax.broadcasted_iota(jnp.int32, (8, LANES), 0)
+    halves = []
+    for half in range(2):
+        a, b = 2 * half, 2 * half + 1
+        top = pltpu.roll(packed, LANES - 2 * COLS * a, 1) if a else packed
+        bottom = pltpu.roll(pltpu.roll(packed, LANES - 2 * COLS * b, 1), 4, 0)
+        halves.append(jnp.where(sub8 < 4, top, bottom))
+    square = jnp.concatenate(halves, axis=0)
+    row = lax.broadcasted_iota(jnp.int32, (COLS, COLS), 0)
+    col = lax.broadcasted_iota(jnp.int32, (COLS, COLS), 1)
+    moments = []
+    for pair in range(2):
+        turned = pltpu.roll(square, LANES - COLS, 1) if pair else square
+        mixed = turned[:, :COLS]
+        diagonal = (pltpu.roll(packed, LANES - COLS, 1) if pair else packed)[4:5, :COLS]
+        flipped = mixed.T
+        moments.append(jnp.where(row <= col, mixed, flipped))
+        lower = jnp.where(row == col, diagonal, jnp.where(row > col, mixed, flipped))
+        moments.append(lower)
+    return moments
 
 
 def dot(left, right, dims=((1,), (0,))):
@@ -205,16 +298,9 @@
     return guess + dot(inv, right - dot(matrix, guess))
 
 
-def finish_kernel(g_ref, v_ref, e_ref, q_ref, above_ref, below_ref, both_ref, sol_ref, res_ref, d_ref, dlow_ref):
-    ext_x, ext_y = v_ref.shape[0], v_ref.shape[1]
-    packed = g_ref[...]
-    turned = [packed] + [pltpu.roll(packed, LANES - 2 * COLS * n, 1) for n in range(1, 4)]
-    low_pair = jnp.concatenate(turned[:2], axis=0)
-    high_pair = jnp.concatenate(turned[2:], axis=0)
-    m0 = low_pair[:, :COLS]
-    m1 = pltpu.roll(low_pair, LANES - COLS, 1)[:, :COLS]
-    m2 = high_pair[:, :COLS]
-    m3 = pltpu.roll(high_pair, LANES - COLS, 1)[:, :COLS]
+def finish_kernel(g_ref, v_ref, q_ref, above_ref, below_ref, both_ref, sol_ref, res_ref, d_ref, dlow_ref):
+    own_x, own_y = v_ref.shape[0], v_ref.shape[1]
+    m0, m1, m2, m3 = unpack_moments(g_ref[...])
     first = ((0,), (0,))
     alpha = solve(m1, m0)
     m1a, m2a, m3a = dot(m1, alpha), dot(m2, alpha), dot(m3, alpha)
@@ -227,39 +313,36 @@
     curved = 0.5 * (curved + curved.T)
     gamma = solve(curved, updated)
     both = jnp.concatenate([mix, -alpha], axis=0)
-    for x in range(1, ext_x - 1):
-        for y in range(1, ext_y - 1):
-            block = jnp.concatenate([v_ref[x, y], q_ref[x - 1, y - 1]], axis=0)
+    for x in range(own_x):
+        for y in range(own_y):
+            block = jnp.concatenate([v_ref[x, y], q_ref[x, y]], axis=0)
             value = dot(both, block, first)
-            inside = e_ref[x * ext_y + y : x * ext_y + y + 1, :] > 0.0
-            value = jnp.where(inside, value, 0.0)
-            d_ref[x - 1, y - 1] = value
-            dlow_ref[x - 1, y - 1] = lowered(value)
+            d_ref[x, y] = value
+            dlow_ref[x, y] = lowered(value)
 
     def weight(ref):
         return lambda ex, ey, t: ref[ex, ey : ey + 1, tile_of(t)]
 
     sides = (weight(above_ref), weight(below_ref), weight(both_ref))
-    zero = jnp.zeros((COLS, COLS), jnp.float32)
-    to_sol = jnp.concatenate([alpha, gamma, zero], axis=0)
+    to_sol = jnp.concatenate([alpha, gamma], axis=0)
     to_res = jnp.concatenate([-alpha, -gamma], axis=0)
-    for x in range(2, ext_x - 2):
-        for y in range(2, ext_y - 2):
+    for x in range(1, own_x - 1):
+        for y in range(1, own_y - 1):
             image = operator(
-                lambda t: d_ref[x - 1, y - 1, :, tile_of(t)],
+                lambda t: d_ref[x, y, :, tile_of(t)],
                 lambda i, j, t: dlow_ref[i, j, :, tile_of(t)],
                 *sides,
-                x - 1,
-                y - 1,
                 x,
                 y,
+                x + 1,
+                y + 1,
             )
             b = v_ref[x, y, :, : 2 * LANES]
-            q = q_ref[x - 1, y - 1, :, : 2 * LANES]
-            d = d_ref[x - 1, y - 1, :, : 2 * LANES]
+            q = q_ref[x, y, :, : 2 * LANES]
+            d = d_ref[x, y, :, : 2 * LANES]
             i2 = jnp.concatenate(image[:2], axis=1)
-            sol_ref[x - 2, y - 2] = dot(to_sol[: 2 * COLS], jnp.concatenate([b, d], axis=0), first)
-            res_ref[x - 2, y - 2] = b + dot(to_res, jnp.concatenate([q, i2], axis=0), first)
+            sol_ref[:, x - 1, y - 1, :] = dot(to_sol, jnp.concatenate([b, d], axis=0), first)
+            res_ref[:, x - 1, y - 1, :] = b + dot(to_res, jnp.concatenate([q, i2], axis=0), first)
 
 
 def ring(axis, step):
@@ -272,54 +355,59 @@
     return lax.ppermute(to_next, axis, ring(axis, 1)), lax.ppermute(to_last, axis, ring(axis, -1))
 
 
-def spread(value, axes):
+def spread(value, axes, groups=None):
     count = lax.axis_size(axes)
     copies = jnp.broadcast_to(value[None], (count, *value.shape))
-    return jnp.sum(lax.all_to_all(copies, axes, 0, 0), axis=0)
+    return jnp.sum(lax.all_to_all(copies, axes, 0, 0, axis_index_groups=groups), axis=0)
+
+
+def near(value):
+    return pltpu.with_memory_space_constraint(value, pltpu.VMEM)
 
 
 def on_device(loads, moduli, material):
-    levels = jnp.arange(moduli.shape[0], dtype=jnp.int32)
-    modulus = jnp.sum(jnp.where(material[..., None] == levels, moduli, 0.0), axis=-1)
-    own = jnp.concatenate([loads, modulus[None]], axis=0)
-    before, after = both_ways("gz", own[..., LANES:], own[..., :LANES])
-    lane = lax.broadcasted_iota(jnp.int32, before.shape, 3)
-    own = jnp.concatenate([own, jnp.where(lane < LANES // 2, after, before)], axis=3)
+    f32 = jnp.float32
+    own = jnp.concatenate([loads, (material[None] + 1).astype(f32)], axis=0)
+    own = jnp.stack([own[..., :LANES], own[..., LANES:]])
     before, after = both_ways("gx", own, own)
-    own = jnp.concatenate([before, own, after], axis=1)
-    before, after = both_ways(GY, own[:, :, 2:], own[:, :, :2])
     own = jnp.concatenate([before, own, after], axis=2)
-    ext_x, ext_y = own.shape[1], own.shape[2]
-    block = jnp.transpose(own[:COLS], (1, 2, 0, 3))
-    modulus = own[COLS].reshape(ext_x * ext_y, 3 * LANES)
-    f32 = jnp.float32
+    before, after = both_ways(GY, own[:, :, :, 2:], own[:, :, :, :2])
+    own = jnp.concatenate([before, own, after], axis=3)
+    ext_x, ext_y = own.shape[2:4]
+    natural = near(own.reshape(2 * (COLS + 1) * ext_x * ext_y, LANES))
+    ends = pltpu.VMEM((COLS + 8, LANES), f32)
+    first, last = pl.pallas_call(
+        functools.partial(pack_kernel, ext_x=ext_x, ext_y=ext_y), out_shape=(ends, ends), name="pack"
+    )(natural)
+    before, after = both_ways("gz", last, first)
     wide = 3 * LANES
-    weights = jax.ShapeDtypeStruct((ext_x - 1, ext_y, wide), f32)
-    image, above, below, both, moments = pl.pallas_call(
+    weights = pltpu.VMEM((ext_x - 1, ext_y, wide), f32)
+    field = pltpu.VMEM((ext_x - 2, ext_y - 2, COLS, wide), f32)
+    in_vmem = pl.BlockSpec(memory_space=pltpu.VMEM)
+    block, image, above, below, both, moments = pl.pallas_call(
         moments_kernel,
-        out_shape=(
-            jax.ShapeDtypeStruct((ext_x - 2, ext_y - 2, COLS, wide), f32),
-            weights,
-            weights,
-            weights,
-            jax.ShapeDtypeStruct((8, LANES), f32),
-        ),
+        out_shape=(field, field, weights, weights, weights, pltpu.VMEM((8, LANES), f32)),
+        in_specs=[pl.BlockSpec(memory_space=pltpu.SMEM), in_vmem, in_vmem, in_vmem],
         scratch_shapes=[
             pltpu.VMEM((ext_x, ext_y, COLS, wide), f32),
             pltpu.VMEM((ext_x - 2, ext_y - 2, COLS, wide), f32),
-            pltpu.VMEM((8, 128), f32),
+            pltpu.VMEM((ext_x, ext_y, wide), f32),
         ],
         name="moments",
-    )(block, modulus)
-    moments = spread(spread(moments, PLANE), "gz")
-    out = jax.ShapeDtypeStruct((ext_x - 4, ext_y - 4, COLS, 2 * LANES), f32)
-    solution, residual = pl.pallas_call(
+    )(moduli, natural, near(before), near(after))
+    rows = 5
+    count = lax.axis_size("gz")
+    middle = [[(i + count // 2) % count for i in range(count)]]
+    moments = spread(moments[:rows].reshape(rows, 1, LANES), PLANE)
+    moments = spread(moments, "gz", middle).reshape(rows, LANES)
+    moments = jnp.concatenate([moments, jnp.zeros((8 - rows, LANES), f32)], axis=0)
+    out = jax.ShapeDtypeStruct(loads.shape, f32)
+    return pl.pallas_call(
         finish_kernel,
         out_shape=(out, out),
-        scratch_shapes=[pltpu.VMEM((ext_x - 2, ext_y - 2, COLS, wide), f32)] * 2,
+        scratch_shapes=[pltpu.VMEM(field.shape, f32)] * 2,
         name="finish",
-    )(moments, block, modulus, image, above, below, both)
-    return jnp.transpose(solution, (2, 0, 1, 3)), jnp.transpose(residual, (2, 0, 1, 3))
+    )(near(moments), near(block), near(image), near(above), near(below), near(both))
 
 
 def solution(mesh):

time: 128 us -> 96.3 us (0.75)
  blocking collectives: 71.5 us -> 52.2 us
  local copies, waits for them, and re-layouts: 6.84 us -> 0.27 us
  waiting for transfers between devices: 9.25 us -> 6.19 us
  Pallas kernels: 9.99 us -> 8.01 us
    all_to_all x2, blocking collectives: 71.5 us -> 52.2 us  [spread(): lax.all_to_all(copies, axes, 0, 0, axis_index_groups=groups)]
    unnamed x4 -> x0, local copies, waits for them, and re-layouts: 4.88 us -> none
    ppermute x3, starting transfers between devices: 14.9 us -> 11 us  [both_ways(): lax.ppermute(to_next, axis, ring(axis, 1))]
    ppermute x3, starting transfers between devices: 12.4 us -> 15.4 us  [both_ways(): lax.ppermute(to_last, axis, ring(axis, -1))]
    ppermute x3, waiting for transfers between devices: 7.47 us -> 4.68 us  [both_ways(): lax.ppermute(to_last, axis, ring(axis, -1))]
    pallas_call x1, Pallas kernels: 6.47 us -> 5.06 us  [on_device(): pl.pallas_call(finish_kernel, out_shape=(out, out), scratch_shapes=[pltpu...]
    reduce_sum x3 -> x2, other arithmetic: 1.47 us -> 0.13 us  [spread(): jnp.sum(lax.all_to_all(copies, axes, 0, 0, axis_index_groups=groups), axi...]
    pallas_call x1 -> x2, Pallas kernels: 3.52 us -> 2.96 us  [the longest x1 2.65 us: on_device(): pl.pallas_call(moments_kernel, out_shape=(field, field, weights, weights,...]
  transfers between devices with their start and end apart: 6 -> 6, of which waited for: 5 -> 4; matrix products, arithmetic and copies ran while one was open for 0% -> 0% of each run, Pallas kernels for 0% -> 0%
where the time goes in v2:
time: 96.3 us; the launch traced here: 95.9 us
  blocking collectives  52.2 us (54%)
  starting transfers between devices  26.3 us (27%)
  Pallas kernels  8.01 us (8%)
  waiting for transfers between devices  6.19 us (6%)
  other arithmetic  2.17 us (2%)
    all_to_all x2, blocking collectives, spread(): lax.all_to_all(copies, axes, 0, 0, axis_index_groups=groups)  52.2 us
    ppermute x3, starting transfers between devices, both_ways(): lax.ppermute(to_last, axis, ring(axis, -1))  15.4 us
    ppermute x3, starting transfers between devices, both_ways(): lax.ppermute(to_next, axis, ring(axis, 1))  11 us
    pallas_call x1, Pallas kernels, on_device(): pl.pallas_call(finish_kernel, out_shape=(out, out), scratch_shapes=[pltpu...  5.06 us
    ppermute x3, waiting for transfers between devices, both_ways(): lax.ppermute(to_last, axis, ring(axis, -1))  4.68 us
    pallas_call x1, Pallas kernels, on_device(): pl.pallas_call(moments_kernel, out_shape=(field, field, weights, weights,...  2.65 us
  transfers between devices with their start and end apart: 6, of which 4 were waited for; matrix products, arithmetic and copies ran while one was open for 0% of the time, Pallas kernels for 0%

profile of v2, /device:TPU:1, one launch (start us, length us, event | category | flops | bytes accessed | tf_op | source)
XLA Modules:
  0.0 95.9 jit_solution(5059556948717657024)
XLA Ops:
  0.6 0.7 convert_bitcast_fusion
  1.3 0.9 fusion.1
  2.3 1.3 %collective-permute-start.1 = (f32[2,17,2,4,128]{4,3,2,1,0:T(4,128)S(1)}, f32[2,17,2,4,128]{4,3,2,1,0:T(4,128)S(1)}, u32[]{:S(2)}, u32[]{:S(2)}) collective-permute-start(f32[2,17,2,4,128]{4,3,2,1,0:T(4,128)S(1)} %pad_maximum_fusion.2), channel_id=1, source_target_pairs={{256,0},{512,256},{768,512},{257,1},{513,257},{769,513},{258,2},{5... | collective-permute-start | bytes 417800 | tf_op jit(solution)/shard_map/ppermute | solution.py:355
  3.6 4.7 %collective-permute-start = (f32[2,17,2,4,128]{4,3,2,1,0:T(4,128)S(1)}, f32[2,17,2,4,128]{4,3,2,1,0:T(4,128)S(1)}, u32[]{:S(2)}, u32[]{:S(2)}) collective-permute-start(f32[2,17,2,4,128]{4,3,2,1,0:T(4,128)S(1)} %pad_maximum_fusion.2), channel_id=1, source_target_pairs={{0,256},{256,512},{512,768},{1,257},{257,513},{513,769},{2,258},{2... | collective-permute-start | bytes 417800 | tf_op jit(solution)/shard_map/ppermute | solution.py:355
  8.2 0.5 collective-permute-done.1
  8.7 1.5 %collective-permute-done = f32[2,17,2,4,128]{4,3,2,1,0:T(4,128)S(1)} collective-permute-done((f32[2,17,2,4,128]{4,3,2,1,0:T(4,128)S(1)}, f32[2,17,2,4,128]{4,3,2,1,0:T(4,128)S(1)}, u32[]{:S(2)}, u32[]{:S(2)}) %collective-permute-start) | collective-permute-done | bytes 139296 | tf_op jit(solution)/shard_map/ppermute | solution.py:355
  10.2 0.1 pad_maximum_fusion.1
  10.4 0.2 fusion.3
  10.5 5.0 %collective-permute-start.2 = (f32[2,17,6,2,128]{4,3,2,1,0:T(2,128)S(1)}, f32[2,17,6,2,128]{4,3,2,1,0:T(2,128)S(1)}, u32[]{:S(2)}, u32[]{:S(2)}) collective-permute-start(f32[2,17,6,2,128]{4,3,2,1,0:T(2,128)S(1)} %get-tuple-element.18), channel_id=1, source_target_pairs={{0,32},{32,64},{64,96},{96,128},{128,160},{160,192},{192,224},{1,3... | collective-permute-start | bytes 626696 | tf_op jit(solution)/shard_map/ppermute | solution.py:355
  15.6 12.8 %collective-permute-start.3 = (f32[2,17,6,2,128]{4,3,2,1,0:T(2,128)S(1)}, f32[2,17,6,2,128]{4,3,2,1,0:T(2,128)S(1)}, u32[]{:S(2)}, u32[]{:S(2)}) collective-permute-start(f32[2,17,6,2,128]{4,3,2,1,0:T(2,128)S(1)} %get-tuple-element.19), channel_id=1, source_target_pairs={{32,0},{64,32},{96,64},{128,96},{160,128},{192,160},{224,192},{33,... | collective-permute-start | bytes 626696 | tf_op jit(solution)/shard_map/ppermute | solution.py:355
  28.3 0.0 collective-permute-done.2
  28.4 1.1 %collective-permute-done.3 = f32[2,17,6,2,128]{4,3,2,1,0:T(2,128)S(1)} collective-permute-done((f32[2,17,6,2,128]{4,3,2,1,0:T(2,128)S(1)}, f32[2,17,6,2,128]{4,3,2,1,0:T(2,128)S(1)}, u32[]{:S(2)}, u32[]{:S(2)}) %collective-permute-start.3) | collective-permute-done | bytes 208928 | tf_op jit(solution)/shard_map/ppermute | solution.py:355
  29.4 0.3 pad_maximum_fusion
  29.7 0.3 pack.1
  30.0 1.3 %collective-permute-start.4 = (f32[24,128]{1,0:T(8,128)S(1)}, f32[24,128]{1,0:T(8,128)S(1)}, u32[]{:S(2)}, u32[]{:S(2)}) collective-permute-start(f32[24,128]{1,0:T(8,128)S(1)} %get-tuple-element.10), channel_id=1, source_target_pairs={{0,1},{1,2},{2,3},{3,4},{4,5},{5,6},{6,7},{7,8},{8,9},{9,10},{10,1... | collective-permute-start | bytes 36872 | tf_op jit(solution)/shard_map/ppermute | solution.py:355
  31.3 1.3 %collective-permute-start.5 = (f32[24,128]{1,0:T(8,128)S(1)}, f32[24,128]{1,0:T(8,128)S(1)}, u32[]{:S(2)}, u32[]{:S(2)}) collective-permute-start(f32[24,128]{1,0:T(8,128)S(1)} %get-tuple-element.11), channel_id=1, source_target_pairs={{1,0},{2,1},{3,2},{4,3},{5,4},{6,5},{7,6},{8,7},{9,8},{10,9},{11,1... | collective-permute-start | bytes 36872 | tf_op jit(solution)/shard_map/ppermute | solution.py:355
  32.6 0.0 collective-permute-done.4.before_ref
  32.6 3.1 %collective-permute-done.5.after_ref = f32[24,128]{1,0:T(8,128)S(1)} collective-permute-done((f32[24,128]{1,0:T(8,128)S(1)}, f32[24,128]{1,0:T(8,128)S(1)}, u32[]{:S(2)}, u32[]{:S(2)}) %collective-permute-start.5) | collective-permute-done | bytes 12320 | tf_op jit(solution)/shard_map/ppermute | solution.py:355
  35.7 2.7 %moments.1 = (f32[4,6,16,384]{3,2,1,0:T(8,128)S(1)}, f32[4,6,16,384]{3,2,1,0:T(8,128)S(1)}, f32[5,8,384]{2,1,0:T(8,128)S(1)}, f32[5,8,384]{2,1,0:T(8,128)S(1)}, ...) custom-call(f32[8]{0:T(128)} %moduli_ref.1, f32[1632,128]{1,0:T(8,128)S(1)} %bitcast.9, ...), custom_call_target="tpu_custom_call" | custom-call | tf_op jit(solution)/shard_map/moments/pallas_call | solution.py:387
  38.4 0.1 broadcast_in_dim.4
  38.4 12.6 %all_to_all.10 = f32[32,5,1,128]{3,2,1,0:T(1,128)S(1)} all-to-all(f32[32,5,1,128]{3,2,1,0:T(1,128)S(1)} %broadcast_in_dim.4), channel_id=1, replica_groups=mesh['gx'=4,'gy_0'=4,'gy_1'=2,'gz'=32] {'gx','gy_0','gy_1'}, dimensions={0} | all-to-all | bytes 163840 | tf_op jit(solution)/shard_map/all_to_all | solution.py:361
  51.1 0.1 reduce_sum.18
  51.2 39.6 %all_to_all.11 = f32[32,5,1,128]{3,2,1,0:T(1,128)S(1)} all-to-all(f32[32,5,1,128]{3,2,1,0:T(1,128)S(1)} %broadcast_in_dim.5), channel_id=1, replica_groups={{16,17,18,19,20,21,22,23,24,25,26,27,28,29,30,31,0,1,2,3,4,5,6,7,8,9,10..., dimensions={0} | all-to-all | bytes 163840 | tf_op jit(solution)/shard_map/all_to_all | solution.py:361
  90.7 0.1 reduce_sum.19
  90.8 5.1 %finish.1 = (f32[16,2,4,256]{3,2,1,0:T(4,128)}, f32[16,2,4,256]{3,2,1,0:T(4,128)}) custom-call(f32[8,128]{1,0:T(8,128)S(1)} %concatenate.15.g_ref, f32[4,6,16,384]{3,2,1,0:T(8,128)S(1)} %get-tuple-element.13.v_ref, f32[4,6,16,384]{3,2,1,0:T(8,128)S(1)} %get-tuple-element.14.q_ref, f32[5,8,384]{2,1,0:T(8,128)S(1)} %get-tuple-element.15.above_ref, ...), custom_call_target="tpu_custom_call" | custom-call | tf_op jit(solution)/shard_map/finish/pallas_call | solution.py:405
  (3 shorter events, 0.1 us)
Async XLA Ops:
  2.3 6.5 %collective-permute-start.1 = (f32[2,17,2,4,128]{4,3,2,1,0:T(4,128)S(1)}, f32[2,17,2,4,128]{4,3,2,1,0:T(4,128)S(1)}, u32[]{:S(2)}, u32[]{:S(2)}) collective-permute-start(f32[2,17,2,4,128]{4,3,2,1,0:T(4,128)S(1)} %pad_maximum_fusion.2), channel_id=1, source_target_pairs={{256,0},{512,256},{768,512},{257,1},{513,257},{769,513},{258,2},{5... | collective-permute-start | bytes 417800 | tf_op jit(solution)/shard_map/ppermute | solution.py:355
  3.6 6.7 %collective-permute-start = (f32[2,17,2,4,128]{4,3,2,1,0:T(4,128)S(1)}, f32[2,17,2,4,128]{4,3,2,1,0:T(4,128)S(1)}, u32[]{:S(2)}, u32[]{:S(2)}) collective-permute-start(f32[2,17,2,4,128]{4,3,2,1,0:T(4,128)S(1)} %pad_maximum_fusion.2), channel_id=1, source_target_pairs={{0,256},{256,512},{512,768},{1,257},{257,513},{513,769},{2,258},{2... | collective-permute-start | bytes 417800 | tf_op jit(solution)/shard_map/ppermute | solution.py:355
  10.5 17.8 %collective-permute-start.2 = (f32[2,17,6,2,128]{4,3,2,1,0:T(2,128)S(1)}, f32[2,17,6,2,128]{4,3,2,1,0:T(2,128)S(1)}, u32[]{:S(2)}, u32[]{:S(2)}) collective-permute-start(f32[2,17,6,2,128]{4,3,2,1,0:T(2,128)S(1)} %get-tuple-element.18), channel_id=1, source_target_pairs={{0,32},{32,64},{64,96},{96,128},{128,160},{160,192},{192,224},{1,3... | collective-permute-start | bytes 626696 | tf_op jit(solution)/shard_map/ppermute | solution.py:355
  15.6 13.8 %collective-permute-start.3 = (f32[2,17,6,2,128]{4,3,2,1,0:T(2,128)S(1)}, f32[2,17,6,2,128]{4,3,2,1,0:T(2,128)S(1)}, u32[]{:S(2)}, u32[]{:S(2)}) collective-permute-start(f32[2,17,6,2,128]{4,3,2,1,0:T(2,128)S(1)} %get-tuple-element.19), channel_id=1, source_target_pairs={{32,0},{64,32},{96,64},{128,96},{160,128},{192,160},{224,192},{33,... | collective-permute-start | bytes 626696 | tf_op jit(solution)/shard_map/ppermute | solution.py:355
  30.0 2.6 %collective-permute-start.4 = (f32[24,128]{1,0:T(8,128)S(1)}, f32[24,128]{1,0:T(8,128)S(1)}, u32[]{:S(2)}, u32[]{:S(2)}) collective-permute-start(f32[24,128]{1,0:T(8,128)S(1)} %get-tuple-element.10), channel_id=1, source_target_pairs={{0,1},{1,2},{2,3},{3,4},{4,5},{5,6},{6,7},{7,8},{8,9},{9,10},{10,1... | collective-permute-start | bytes 36872 | tf_op jit(solution)/shard_map/ppermute | solution.py:355
  31.3 4.4 %collective-permute-start.5 = (f32[24,128]{1,0:T(8,128)S(1)}, f32[24,128]{1,0:T(8,128)S(1)}, u32[]{:S(2)}, u32[]{:S(2)}) collective-permute-start(f32[24,128]{1,0:T(8,128)S(1)} %get-tuple-element.11), channel_id=1, source_target_pairs={{1,0},{2,1},{3,2},{4,3},{5,4},{6,5},{7,6},{8,7},{9,8},{10,9},{11,1... | collective-permute-start | bytes 36872 | tf_op jit(solution)/shard_map/ppermute | solution.py:355

commit v3 on v2

--- a/solution.py
+++ b/solution.py
@@ -292,26 +292,17 @@
     return out[:, :size]
 
 
-def solve(matrix, right):
-    inv = inverse(matrix)
-    guess = dot(inv, right)
-    return guess + dot(inv, right - dot(matrix, guess))
-
-
 def finish_kernel(g_ref, v_ref, q_ref, above_ref, below_ref, both_ref, sol_ref, res_ref, d_ref, dlow_ref):
     own_x, own_y = v_ref.shape[0], v_ref.shape[1]
     m0, m1, m2, m3 = unpack_moments(g_ref[...])
     first = ((0,), (0,))
-    alpha = solve(m1, m0)
-    m1a, m2a, m3a = dot(m1, alpha), dot(m2, alpha), dot(m3, alpha)
-    updated = m0 - m1a - dot(alpha, m1, first) + dot(alpha, m2a, first)
-    beta = solve(m0, updated)
-    row = lax.broadcasted_iota(jnp.int32, (COLS, COLS), 0)
-    col = lax.broadcasted_iota(jnp.int32, (COLS, COLS), 1)
-    mix = beta + jnp.where(row == col, 1.0, 0.0)
-    curved = dot(mix, dot(m1, mix) - m2a, first) + dot(alpha, m3a - dot(m2, mix), first)
-    curved = 0.5 * (curved + curved.T)
-    gamma = solve(curved, updated)
+    inv = inverse(m1)
+    alpha = dot(inv, m0)
+    m2a = dot(m2, alpha)
+    mix = dot(inv, m2a)
+    updated = dot(alpha, m2a, first) - m0
+    curved = dot(alpha, dot(m3, alpha), first) - dot(m2a, mix, first)
+    gamma = dot(inverse(0.5 * (curved + curved.T)), updated)
     both = jnp.concatenate([mix, -alpha], axis=0)
     for x in range(own_x):
         for y in range(own_y):
@@ -345,14 +336,16 @@
             res_ref[:, x - 1, y - 1, :] = b + dot(to_res, jnp.concatenate([q, i2], axis=0), first)
 
 
-def ring(axis, step):
+def both_ways(axis, to_next, to_last, around=False):
     count = lax.axis_size(axis)
-    ends = range(count - 1)
-    return [(i, i + 1) for i in ends] if step > 0 else [(i + 1, i) for i in ends]
-
-
-def both_ways(axis, to_next, to_last):
-    return lax.ppermute(to_next, axis, ring(axis, 1)), lax.ppermute(to_last, axis, ring(axis, -1))
+    steps = range(count) if around else range(count - 1)
+    before = lax.ppermute(to_next, axis, [(i, (i + 1) % count) for i in steps])
+    after = lax.ppermute(to_last, axis, [((i + 1) % count, i) for i in steps])
+    if around:
+        place = lax.axis_index(axis)
+        before = jnp.where(place > 0, before, 0.0)
+        after = jnp.where(place < count - 1, after, 0.0)
+    return before, after
 
 
 def spread(value, axes, groups=None):
@@ -371,7 +364,7 @@
     own = jnp.stack([own[..., :LANES], own[..., LANES:]])
     before, after = both_ways("gx", own, own)
     own = jnp.concatenate([before, own, after], axis=2)
-    before, after = both_ways(GY, own[:, :, :, 2:], own[:, :, :, :2])
+    before, after = both_ways(GY, own[:, :, :, 2:], own[:, :, :, :2], around=True)
     own = jnp.concatenate([before, own, after], axis=3)
     ext_x, ext_y = own.shape[2:4]
     natural = near(own.reshape(2 * (COLS + 1) * ext_x * ext_y, LANES))
@@ -397,9 +390,9 @@
     )(moduli, natural, near(before), near(after))
     rows = 5
     count = lax.axis_size("gz")
-    middle = [[(i + count // 2) % count for i in range(count)]]
-    moments = spread(moments[:rows].reshape(rows, 1, LANES), PLANE)
-    moments = spread(moments, "gz", middle).reshape(rows, LANES)
+    middle = [[(i + 5 * count // 8) % count for i in range(count)]]
+    moments = spread(moments[:rows].reshape(rows, 1, LANES), "gz", middle)
+    moments = spread(moments, PLANE).reshape(rows, LANES)
     moments = jnp.concatenate([moments, jnp.zeros((8 - rows, LANES), f32)], axis=0)
     out = jax.ShapeDtypeStruct(loads.shape, f32)
     return pl.pallas_call(

time: 96.3 us -> 94 us (0.976)
  starting transfers between devices: 26.3 us -> 23.2 us
  blocking collectives: 52.2 us -> 54.2 us
  Pallas kernels: 8.01 us -> 6.77 us
    ppermute x6, starting transfers between devices: 26.3 us -> 23.2 us  [the longest x3 14.1 us: both_ways(): after = lax.ppermute(to_last, axis, [((i + 1) % count, i) for i in steps])]
    all_to_all x2, blocking collectives: 52.2 us -> 54.2 us  [spread(): lax.all_to_all(copies, axes, 0, 0, axis_index_groups=groups)]
    pallas_call x1, Pallas kernels: 5.06 us -> 3.82 us  [on_device(): pl.pallas_call(finish_kernel, out_shape=(out, out), scratch_shapes=[pltpu...]
  transfers between devices with their start and end apart: 6 -> 6, of which waited for: 4 -> 5; matrix products, arithmetic and copies ran while one was open for 0% -> 0% of each run, Pallas kernels for 0% -> 0%
where the time goes in v3:
time: 94 us; the launch traced here: 93.6 us
  blocking collectives  54.2 us (58%)
  starting transfers between devices  23.2 us (25%)
  Pallas kernels  6.77 us (7%)
  waiting for transfers between devices  6.11 us (6%)
  other arithmetic  2.37 us (3%)
    all_to_all x2, blocking collectives, spread(): lax.all_to_all(copies, axes, 0, 0, axis_index_groups=groups)  54.2 us
    ppermute x3, starting transfers between devices, both_ways(): after = lax.ppermute(to_last, axis, [((i + 1) % count, i) for i in steps])  14.1 us
    ppermute x3, starting transfers between devices, both_ways(): before = lax.ppermute(to_next, axis, [(i, (i + 1) % count) for i in steps])  9.07 us
    pallas_call x1, Pallas kernels, on_device(): pl.pallas_call(finish_kernel, out_shape=(out, out), scratch_shapes=[pltpu...  3.82 us
    ppermute x3, waiting for transfers between devices, both_ways(): after = lax.ppermute(to_last, axis, [((i + 1) % count, i) for i in steps])  3.69 us
    pallas_call x1, Pallas kernels, on_device(): pl.pallas_call(moments_kernel, out_shape=(field, field, weights, weights,...  2.65 us
    ppermute x3, waiting for transfers between devices, both_ways(): before = lax.ppermute(to_next, axis, [(i, (i + 1) % count) for i in steps])  2.42 us
  transfers between devices with their start and end apart: 6, of which 5 were waited for; matrix products, arithmetic and copies ran while one was open for 0% of the time, Pallas kernels for 0%

profile of v3, /device:TPU:1, one launch (start us, length us, event | category | flops | bytes accessed | tf_op | source)
XLA Modules:
  0.0 93.6 jit_solution(9286581786720732096)
XLA Ops:
  0.6 0.7 convert_bitcast_fusion
  1.3 0.9 fusion.1
  2.3 1.3 %collective-permute-start.1 = (f32[2,17,2,4,128]{4,3,2,1,0:T(4,128)S(1)}, f32[2,17,2,4,128]{4,3,2,1,0:T(4,128)S(1)}, u32[]{:S(2)}, u32[]{:S(2)}) collective-permute-start(f32[2,17,2,4,128]{4,3,2,1,0:T(4,128)S(1)} %pad_maximum_fusion.2), channel_id=1, source_target_pairs={{256,0},{512,256},{768,512},{257,1},{513,257},{769,513},{258,2},{5... | collective-permute-start | bytes 417800 | tf_op jit(solution)/shard_map/ppermute | solution.py:343
  3.6 4.7 %collective-permute-start = (f32[2,17,2,4,128]{4,3,2,1,0:T(4,128)S(1)}, f32[2,17,2,4,128]{4,3,2,1,0:T(4,128)S(1)}, u32[]{:S(2)}, u32[]{:S(2)}) collective-permute-start(f32[2,17,2,4,128]{4,3,2,1,0:T(4,128)S(1)} %pad_maximum_fusion.2), channel_id=1, source_target_pairs={{0,256},{256,512},{512,768},{1,257},{257,513},{513,769},{2,258},{2... | collective-permute-start | bytes 417800 | tf_op jit(solution)/shard_map/ppermute | solution.py:342
  8.2 0.5 collective-permute-done.1
  8.7 1.5 %collective-permute-done = f32[2,17,2,4,128]{4,3,2,1,0:T(4,128)S(1)} collective-permute-done((f32[2,17,2,4,128]{4,3,2,1,0:T(4,128)S(1)}, f32[2,17,2,4,128]{4,3,2,1,0:T(4,128)S(1)}, u32[]{:S(2)}, u32[]{:S(2)}) %collective-permute-start) | collective-permute-done | bytes 139296 | tf_op jit(solution)/shard_map/ppermute | solution.py:342
  10.2 0.1 pad_maximum_fusion.1
  10.4 0.2 fusion.3
  10.5 3.1 %collective-permute-start.2 = (f32[2,17,6,2,128]{4,3,2,1,0:T(2,128)S(1)}, f32[2,17,6,2,128]{4,3,2,1,0:T(2,128)S(1)}, u32[]{:S(2)}, u32[]{:S(2)}) collective-permute-start(f32[2,17,6,2,128]{4,3,2,1,0:T(2,128)S(1)} %get-tuple-element.18), channel_id=1, source_target_pairs={{0,32},{32,64},{64,96},{96,128},{128,160},{160,192},{192,224},{224... | collective-permute-start | bytes 626696 | tf_op jit(solution)/shard_map/ppermute | solution.py:342
  13.7 11.5 %collective-permute-start.3 = (f32[2,17,6,2,128]{4,3,2,1,0:T(2,128)S(1)}, f32[2,17,6,2,128]{4,3,2,1,0:T(2,128)S(1)}, u32[]{:S(2)}, u32[]{:S(2)}) collective-permute-start(f32[2,17,6,2,128]{4,3,2,1,0:T(2,128)S(1)} %get-tuple-element.19), channel_id=1, source_target_pairs={{32,0},{64,32},{96,64},{128,96},{160,128},{192,160},{224,192},{0,2... | collective-permute-start | bytes 626696 | tf_op jit(solution)/shard_map/ppermute | solution.py:343
  25.2 0.9 collective-permute-done.2
  26.1 0.1 broadcast_select_fusion.1
  26.2 0.1 collective-permute-done.3
  26.2 0.1 broadcast_select_fusion
  26.3 0.3 pad_maximum_fusion
  26.6 0.3 pack.1
  26.9 1.3 %collective-permute-start.4 = (f32[24,128]{1,0:T(8,128)S(1)}, f32[24,128]{1,0:T(8,128)S(1)}, u32[]{:S(2)}, u32[]{:S(2)}) collective-permute-start(f32[24,128]{1,0:T(8,128)S(1)} %get-tuple-element.10), channel_id=1, source_target_pairs={{0,1},{1,2},{2,3},{3,4},{4,5},{5,6},{6,7},{7,8},{8,9},{9,10},{10,1... | collective-permute-start | bytes 36872 | tf_op jit(solution)/shard_map/ppermute | solution.py:342
  28.2 1.3 %collective-permute-start.5 = (f32[24,128]{1,0:T(8,128)S(1)}, f32[24,128]{1,0:T(8,128)S(1)}, u32[]{:S(2)}, u32[]{:S(2)}) collective-permute-start(f32[24,128]{1,0:T(8,128)S(1)} %get-tuple-element.11), channel_id=1, source_target_pairs={{1,0},{2,1},{3,2},{4,3},{5,4},{6,5},{7,6},{8,7},{9,8},{10,9},{11,1... | collective-permute-start | bytes 36872 | tf_op jit(solution)/shard_map/ppermute | solution.py:343
  29.5 0.0 collective-permute-done.4.before_ref
  29.5 3.1 %collective-permute-done.5.after_ref = f32[24,128]{1,0:T(8,128)S(1)} collective-permute-done((f32[24,128]{1,0:T(8,128)S(1)}, f32[24,128]{1,0:T(8,128)S(1)}, u32[]{:S(2)}, u32[]{:S(2)}) %collective-permute-start.5) | collective-permute-done | bytes 12320 | tf_op jit(solution)/shard_map/ppermute | solution.py:343
  32.7 2.7 %moments.1 = (f32[4,6,16,384]{3,2,1,0:T(8,128)S(1)}, f32[4,6,16,384]{3,2,1,0:T(8,128)S(1)}, f32[5,8,384]{2,1,0:T(8,128)S(1)}, f32[5,8,384]{2,1,0:T(8,128)S(1)}, ...) custom-call(f32[8]{0:T(128)} %moduli_ref.1, f32[1632,128]{1,0:T(8,128)S(1)} %bitcast.9, ...), custom_call_target="tpu_custom_call" | custom-call | tf_op jit(solution)/shard_map/moments/pallas_call | solution.py:380
  35.3 0.1 broadcast_in_dim.10
  35.4 36.7 %all_to_all.10 = f32[32,5,1,128]{3,2,1,0:T(1,128)S(1)} all-to-all(f32[32,5,1,128]{3,2,1,0:T(1,128)S(1)} %broadcast_in_dim.10), channel_id=1, replica_groups={{20,21,22,23,24,25,26,27,28,29,30,31,0,1,2,3,4,5,6,7,8,9,10,11,12,13,14..., dimensions={0} | all-to-all | bytes 163840 | tf_op jit(solution)/shard_map/all_to_all | solution.py:354
  72.1 0.1 reduce_sum.18
  72.3 17.5 %all_to_all.11 = f32[32,5,1,128]{3,2,1,0:T(1,128)S(1)} all-to-all(f32[32,5,1,128]{3,2,1,0:T(1,128)S(1)} %broadcast_in_dim.20), channel_id=1, replica_groups=mesh['gx'=4,'gy_0'=4,'gy_1'=2,'gz'=32] {'gx','gy_0','gy_1'}, dimensions={0} | all-to-all | bytes 163840 | tf_op jit(solution)/shard_map/all_to_all | solution.py:354
  89.7 0.1 reduce_sum.19
  89.8 3.8 %finish.1 = (f32[16,2,4,256]{3,2,1,0:T(4,128)}, f32[16,2,4,256]{3,2,1,0:T(4,128)}) custom-call(f32[8,128]{1,0:T(8,128)S(1)} %concatenate.15.g_ref, f32[4,6,16,384]{3,2,1,0:T(8,128)S(1)} %get-tuple-element.13.v_ref, f32[4,6,16,384]{3,2,1,0:T(8,128)S(1)} %get-tuple-element.14.q_ref, f32[5,8,384]{2,1,0:T(8,128)S(1)} %get-tuple-element.15.above_ref, ...), custom_call_target="tpu_custom_call" | custom-call | tf_op jit(solution)/shard_map/finish/pallas_call | solution.py:398
  (3 shorter events, 0.1 us)
Async XLA Ops:
  2.3 6.5 %collective-permute-start.1 = (f32[2,17,2,4,128]{4,3,2,1,0:T(4,128)S(1)}, f32[2,17,2,4,128]{4,3,2,1,0:T(4,128)S(1)}, u32[]{:S(2)}, u32[]{:S(2)}) collective-permute-start(f32[2,17,2,4,128]{4,3,2,1,0:T(4,128)S(1)} %pad_maximum_fusion.2), channel_id=1, source_target_pairs={{256,0},{512,256},{768,512},{257,1},{513,257},{769,513},{258,2},{5... | collective-permute-start | bytes 417800 | tf_op jit(solution)/shard_map/ppermute | solution.py:343
  3.6 6.7 %collective-permute-start = (f32[2,17,2,4,128]{4,3,2,1,0:T(4,128)S(1)}, f32[2,17,2,4,128]{4,3,2,1,0:T(4,128)S(1)}, u32[]{:S(2)}, u32[]{:S(2)}) collective-permute-start(f32[2,17,2,4,128]{4,3,2,1,0:T(4,128)S(1)} %pad_maximum_fusion.2), channel_id=1, source_target_pairs={{0,256},{256,512},{512,768},{1,257},{257,513},{513,769},{2,258},{2... | collective-permute-start | bytes 417800 | tf_op jit(solution)/shard_map/ppermute | solution.py:342
  10.5 15.6 %collective-permute-start.2 = (f32[2,17,6,2,128]{4,3,2,1,0:T(2,128)S(1)}, f32[2,17,6,2,128]{4,3,2,1,0:T(2,128)S(1)}, u32[]{:S(2)}, u32[]{:S(2)}) collective-permute-start(f32[2,17,6,2,128]{4,3,2,1,0:T(2,128)S(1)} %get-tuple-element.18), channel_id=1, source_target_pairs={{0,32},{32,64},{64,96},{96,128},{128,160},{160,192},{192,224},{224... | collective-permute-start | bytes 626696 | tf_op jit(solution)/shard_map/ppermute | solution.py:342
  13.7 12.6 %collective-permute-start.3 = (f32[2,17,6,2,128]{4,3,2,1,0:T(2,128)S(1)}, f32[2,17,6,2,128]{4,3,2,1,0:T(2,128)S(1)}, u32[]{:S(2)}, u32[]{:S(2)}) collective-permute-start(f32[2,17,6,2,128]{4,3,2,1,0:T(2,128)S(1)} %get-tuple-element.19), channel_id=1, source_target_pairs={{32,0},{64,32},{96,64},{128,96},{160,128},{192,160},{224,192},{0,2... | collective-permute-start | bytes 626696 | tf_op jit(solution)/shard_map/ppermute | solution.py:343
  26.9 2.6 %collective-permute-start.4 = (f32[24,128]{1,0:T(8,128)S(1)}, f32[24,128]{1,0:T(8,128)S(1)}, u32[]{:S(2)}, u32[]{:S(2)}) collective-permute-start(f32[24,128]{1,0:T(8,128)S(1)} %get-tuple-element.10), channel_id=1, source_target_pairs={{0,1},{1,2},{2,3},{3,4},{4,5},{5,6},{6,7},{7,8},{8,9},{9,10},{10,1... | collective-permute-start | bytes 36872 | tf_op jit(solution)/shard_map/ppermute | solution.py:342
  28.2 4.4 %collective-permute-start.5 = (f32[24,128]{1,0:T(8,128)S(1)}, f32[24,128]{1,0:T(8,128)S(1)}, u32[]{:S(2)}, u32[]{:S(2)}) collective-permute-start(f32[24,128]{1,0:T(8,128)S(1)} %get-tuple-element.11), channel_id=1, source_target_pairs={{1,0},{2,1},{3,2},{4,3},{5,4},{6,5},{7,6},{8,7},{9,8},{10,9},{11,1... | collective-permute-start | bytes 36872 | tf_op jit(solution)/shard_map/ppermute | solution.py:343

commit v4 on v3

v4 whole, which is shorter than its diff:
```python
import functools

import jax
import jax.numpy as jnp
import numpy as np
from jax import lax
from jax.experimental import pallas as pl
from jax.experimental.pallas import tpu as pltpu
from jax.sharding import Mesh
from jax.sharding import PartitionSpec as P

PLANE = ("gx", "gy_0", "gy_1")
GY = ("gy_0", "gy_1")
SIGMA = 0.25
COLS = 16
LANES = 128
EDGE = LANES // 4
HIGH = lax.Precision.HIGHEST


def stiffness_table():
    line_mass = np.array([[1.0 / 3.0, 1.0 / 6.0], [1.0 / 6.0, 1.0 / 3.0]])
    line_stiff = np.array([[1.0, -1.0], [-1.0, 1.0]])
    table = np.zeros((8, 8))
    for target in range(8):
        for source in range(8):
            target_bits = [target >> 2 & 1, target >> 1 & 1, target & 1]
            source_bits = [source >> 2 & 1, source >> 1 & 1, source & 1]
            total = 0.0
            for stiff_dim in range(3):
                factor = 1.0
                for other in range(3):
                    if other == stiff_dim:
                        factor = factor * line_stiff[target_bits[other], source_bits[other]]
                    else:
                        factor = factor * line_mass[target_bits[other], source_bits[other]]
                total = total + factor
            table[target, source] = total
    return table


def kernel_scale():
    table = np.asarray(jnp.asarray(stiffness_table(), jnp.bfloat16).astype(jnp.float32))
    unit = -float(table[0, 7])
    for target in range(8):
        for source in range(8):
            bits = bin(target ^ source).count("1")
            want = (4.0, 0.0, -1.0, -1.0)[bits] * unit
            assert abs(float(table[target, source]) - want) < 1e-12
    return unit


UNIT = kernel_scale()


def lowered(value):
    return value.astype(jnp.bfloat16).astype(jnp.float32)


def tile_of(tile):
    return slice(tile * LANES, (tile + 1) * LANES)


def lanes_of(value):
    return lax.broadcasted_iota(jnp.int32, value.shape, 1)


def turn(value, amount):
    amount %= LANES
    return pltpu.roll(value, amount, 1) if amount else value


def shifted(tiles, step, beyond=None):
    count = len(tiles)
    turned = [turn(t, -step) for t in tiles]
    past = turn(beyond, -step) if beyond is not None else turned[0 if step > 0 else -1]
    lane = lanes_of(tiles[0])
    if step > 0:
        return [jnp.where(lane < LANES - 1, turned[i], turned[i + 1] if i + 1 < count else past) for i in range(count)]
    return [jnp.where(lane > 0, turned[i], turned[i - 1] if i else past) for i in range(count)]


def terms(low, sides, tile, x, y, wx, wy):
    above, below, both = sides
    around = {(i, j): low(x + i, y + j, tile) for i in (-1, 0, 1) for j in (-1, 0, 1)}
    centre = 4.0 * around[0, 0]
    total = None
    for i in (-1, 1):
        for j in (-1, 1):
            ex, ey = wx + (i - 1) // 2, wy + (j - 1) // 2
            others = around[i, 0] + around[0, j] + around[i, j]
            new = (
                both(ex, ey, tile) * (centre - around[i, j]),
                below(ex, ey, tile) * others,
                above(ex, ey, tile) * others,
            )
            total = new if total is None else tuple(a + b for a, b in zip(total, new))
    return total


def operator(field, low, sides, count, x, y, wx, wy):
    plane, down, up = zip(*[terms(low, sides, t, x, y, wx, wy) for t in range(count)])
    from_above, from_below = shifted(down, 1), shifted(up, -1)
    return [SIGMA * field(t) + (plane[t] - from_above[t] - from_below[t]) for t in range(count)]


def split_terms(value, count):
    parts = []
    for n in range(count):
        part = value.astype(jnp.bfloat16)
        parts.append(part)
        if n + 1 < count:
            value = value - part.astype(jnp.float32)
    return jnp.concatenate(parts, axis=0)


def rows_of(refs, flags_ref, tile, x, y, first, count):
    before_ref, mid_ref, after_ref, ext_x = refs
    if y < 2:
        ref, wide, at, flag = before_ref, 2, y, 0
    elif y < 6:
        ref, wide, at, flag = mid_ref, 4, y - 2, None
    else:
        ref, wide, at, flag = after_ref, 2, y - 6, 1
    stride = ext_x * wide
    start = tile * (ref.shape[0] // 2) + first * stride + x * wide + at
    value = ref[pl.ds(start, count, stride=stride), :] if count > 1 else ref[start : start + 1, :]
    if flag is not None:
        value = jnp.where(flags_ref[flag : flag + 1, :] > 0.0, value, 0.0)
    return value


def front_kernel(moduli_ref, loads_ref, material_ref, own_ref, levels_ref):
    for t in range(2):
        own_ref[t, :COLS] = loads_ref[:, :, :, tile_of(t)]
        own_ref[t, COLS] = (material_ref[:, :, tile_of(t)] + 1).astype(jnp.float32)
    for level in range(moduli_ref.shape[0]):
        levels_ref[level : level + 1, :] = jnp.full((1, LANES), moduli_ref[level], jnp.float32)


def pack_kernel(flags_ref, before_ref, mid_ref, after_ref, lo_ref, hi_ref, ext_x, ext_y):
    refs = (before_ref, mid_ref, after_ref, ext_x)
    for tile, out_ref in ((0, lo_ref), (1, hi_ref)):
        offset = 2 * tile
        lane = lax.broadcasted_iota(jnp.int32, (COLS, LANES), 1)
        packed = jnp.zeros((COLS, LANES), jnp.float32)
        ids = [jnp.zeros((1, LANES), jnp.float32)] * ext_y
        for x in range(ext_x):
            for y in range(ext_y):
                node = x * ext_y + y
                value = rows_of(refs, flags_ref, tile, x, y, 0, COLS)
                packed = jnp.where(lane // 2 == node, turn(value, 2 * node + offset), packed)
                value = rows_of(refs, flags_ref, tile, x, y, COLS, 1)
                ids[y] = jnp.where(lane[:1] // 2 == x, turn(value, 2 * x + offset), ids[y])
        out_ref[:COLS, :] = packed
        for y in range(ext_y):
            out_ref[COLS + y : COLS + y + 1, :] = ids[y]


def modulus_of(levels_ref, ids):
    modulus = jnp.zeros_like(ids)
    for level in range(levels_ref.shape[0]):
        modulus = jnp.where(ids == level + 1.0, levels_ref[level : level + 1, :], modulus)
    return modulus


def element_weights(e_ref, above_ref, below_ref, both_ref, count):
    ext_x, ext_y = e_ref.shape[:2]
    for ex in range(ext_x - 1):
        flat = []
        for t in range(count):
            both_x = e_ref[ex, :, tile_of(t)] + e_ref[ex + 1, :, tile_of(t)]
            flat.append(both_x + pltpu.roll(both_x, ext_y - 1, 0))
        ahead = shifted(flat, 1)
        weights = [(0.125 * UNIT) * (flat[t] + ahead[t]) for t in range(count)]
        behind = shifted(weights, -1)
        for t in range(count):
            above_ref[ex, :, tile_of(t)] = weights[t]
            below_ref[ex, :, tile_of(t)] = behind[t]
            both_ref[ex, :, tile_of(t)] = weights[t] + behind[t]


def sides_of(*refs):
    return tuple(lambda ex, ey, t, ref=ref: ref[ex, ey : ey + 1, tile_of(t)] for ref in refs)


def first_image(v_ref, low_ref, e_ref, sides, q_ref, qlow_ref, count):
    ext_x, ext_y = low_ref.shape[0], low_ref.shape[1]
    for x in range(1, ext_x - 1):
        for y in range(1, ext_y - 1):
            image = operator(
                lambda t: v_ref[x - 1, y - 1, :, tile_of(t)],
                lambda i, j, t: low_ref[i, j, :, tile_of(t)],
                sides, count, x, y, x, y,
            )
            for t in range(count):
                value = jnp.where(e_ref[x, y : y + 1, tile_of(t)] > 0.0, image[t], 0.0)
                q_ref[x - 1, y - 1, :, tile_of(t)] = value
                qlow_ref[x - 1, y - 1, :, tile_of(t)] = lowered(value)


def gram_terms(v_ref, q_ref, qlow_ref, sides, count, keep, left_ref, right_ref):
    own_x, own_y = v_ref.shape[0], v_ref.shape[1]
    node = 0
    for x in range(1, own_x - 1):
        for y in range(1, own_y - 1):
            image = operator(
                lambda t: q_ref[x, y, :, tile_of(t)],
                lambda i, j, t: qlow_ref[i, j, :, tile_of(t)],
                sides, count, x, y, x + 1, y + 1,
            )
            for t in range(count):
                b, q = v_ref[x, y, :, tile_of(t)], q_ref[x, y, :, tile_of(t)]
                at = tile_of(node * count + t)
                left = jnp.concatenate([b, q], axis=0)
                left = jnp.where(keep(lanes_of(left), t), left, 0.0)
                left_ref[:, at] = split_terms(left, 3)
                right = jnp.concatenate([b, q, image[t], jnp.zeros_like(b)], axis=0)
                right_ref[:, at] = split_terms(right, 3)
            node += 1
    product = lax.dot_general(
        left_ref[...], right_ref[...], (((1,), (1,)), ((), ())), preferred_element_type=jnp.float32
    )
    half = LANES // 2
    third = jnp.concatenate([product[:, LANES:], jnp.zeros((6 * COLS, half), jnp.float32)], axis=1)
    folded = product[:, :LANES] + turn(product[:, :LANES], half) + third
    return sum(folded[2 * COLS * n : 2 * COLS * (n + 1)] for n in range(3))


def main_kernel(
    levels_ref, flags_ref, before_ref, mid_ref, after_ref,
    v_ref, q_ref, above_ref, below_ref, both_ref, total_ref, ve_ref, ie_ref,
    low_ref, qlow_ref, e_ref, left_ref, right_ref,
):
    ext_x, ext_y = low_ref.shape[0], low_ref.shape[1]
    refs = (before_ref, mid_ref, after_ref, ext_x)
    for x in range(ext_x):
        for y in range(ext_y):
            tiles = [rows_of(refs, flags_ref, t, x, y, COLS, 1) for t in range(2)]
            lane = lanes_of(tiles[0])
            edge = jnp.where(lane < EDGE, tiles[0], jnp.where(lane < 2 * EDGE, turn(tiles[1], 2 * EDGE), 0.0))
            ie_ref[x, y : y + 1, :] = edge
            for t in range(2):
                e_ref[x, y : y + 1, tile_of(t)] = tiles[t]
        for t in range(2):
            e_ref[x, :, tile_of(t)] = modulus_of(levels_ref, e_ref[x, :, tile_of(t)])
    element_weights(e_ref, above_ref, below_ref, both_ref, 2)
    for x in range(ext_x):
        for y in range(ext_y):
            tiles = [rows_of(refs, flags_ref, t, x, y, 0, COLS) for t in range(2)]
            lane = lanes_of(tiles[0])
            edge = jnp.where(lane < EDGE, tiles[0], jnp.where(lane < 2 * EDGE, turn(tiles[1], 2 * EDGE), 0.0))
            ve_ref[x, y] = edge
            for t in range(2):
                low_ref[x, y, :, tile_of(t)] = lowered(tiles[t])
                if 0 < x < ext_x - 1 and 0 < y < ext_y - 1:
                    v_ref[x - 1, y - 1, :, tile_of(t)] = tiles[t]
    sides = sides_of(above_ref, below_ref, both_ref)
    first_image(v_ref, low_ref, e_ref, sides, q_ref, qlow_ref, 2)
    total_ref[...] = gram_terms(
        v_ref, q_ref, qlow_ref, sides, 2,
        lambda lane, t: lane >= 2 if t == 0 else lane < LANES - 2,
        left_ref, right_ref,
    )


def edge_kernel(
    levels_ref, total_ref, ve_ref, ie_ref, before_ref, after_ref,
    v_ref, q_ref, above_ref, below_ref, both_ref, g_ref,
    low_ref, qlow_ref, e_ref, left_ref, right_ref,
):
    ext_x, ext_y = low_ref.shape[0], low_ref.shape[1]

    def with_ends(own, before, after, index):
        lane = lanes_of(own)
        follows, comes = turn(after, LANES // 2 - 2 * index), turn(before, LANES - 2 - 2 * index)
        value = jnp.where(lane >= LANES - 2, comes, own)
        return jnp.where((lane >= LANES // 2) & (lane < LANES // 2 + 2), follows, value)

    for x in range(ext_x):
        ids = with_ends(ie_ref[x], before_ref[COLS : COLS + ext_y, :], after_ref[COLS : COLS + ext_y, :], x)
        e_ref[x] = modulus_of(levels_ref, ids)
    element_weights(e_ref, above_ref, below_ref, both_ref, 1)
    before, after = before_ref[:COLS, :], after_ref[:COLS, :]
    for x in range(ext_x):
        for y in range(ext_y):
            value = with_ends(ve_ref[x, y], before, after, x * ext_y + y)
            low_ref[x, y] = lowered(value)
            if 0 < x < ext_x - 1 and 0 < y < ext_y - 1:
                v_ref[x - 1, y - 1] = value
    sides = sides_of(above_ref, below_ref, both_ref)
    first_image(v_ref, low_ref, e_ref, sides, q_ref, qlow_ref, 1)
    total = gram_terms(
        v_ref, q_ref, qlow_ref, sides, 1,
        lambda lane, t: (lane < 2) | ((lane >= 2 * EDGE - 2) & (lane < 2 * EDGE)),
        left_ref, right_ref,
    )
    g_ref[...] = pack_moments(total_ref[...] + total)


def pack_moments(total):
    first, second = total[:COLS], total[COLS:]
    row = lax.broadcasted_iota(jnp.int32, (COLS, LANES), 0)
    lane = lax.broadcasted_iota(jnp.int32, (COLS, LANES), 1)
    col = lane % COLS
    upper = jnp.where(lane < COLS, first, second)
    lower = jnp.where(
        lane < COLS,
        0.5 * (pltpu.roll(first, LANES - COLS, 1) + second),
        pltpu.roll(second, LANES - COLS, 1),
    )
    valid = lane < 2 * COLS
    square = jnp.where(valid, jnp.where(row <= col, upper, lower), 0.0)
    diagonal = jnp.sum(jnp.where(valid & (row == col), lower, 0.0), axis=0, keepdims=True)
    out = []
    for half in range(2):
        out.append(square[8 * half : 8 * half + 8])
    spread_rows = jnp.zeros((8, LANES), jnp.float32)
    sub8 = lax.broadcasted_iota(jnp.int32, (8, LANES), 0)
    lane8 = lax.broadcasted_iota(jnp.int32, (8, LANES), 1)
    for quarter in range(4):
        piece = out[quarter // 2]
        if quarter % 2:
            piece = pltpu.roll(piece, 4, 0)
        if quarter:
            piece = pltpu.roll(piece, 2 * COLS * quarter, 1)
        here = (sub8 < 4) & (lane8 // (2 * COLS) == quarter)
        spread_rows = jnp.where(here, piece, spread_rows)
    return jnp.where(sub8 == 4, diagonal, spread_rows)


def unpack_moments(packed):
    sub8 = lax.broadcasted_iota(jnp.int32, (8, LANES), 0)
    halves = []
    for half in range(2):
        a, b = 2 * half, 2 * half + 1
        top = pltpu.roll(packed, LANES - 2 * COLS * a, 1) if a else packed
        bottom = pltpu.roll(pltpu.roll(packed, LANES - 2 * COLS * b, 1), 4, 0)
        halves.append(jnp.where(sub8 < 4, top, bottom))
    square = jnp.concatenate(halves, axis=0)
    row = lax.broadcasted_iota(jnp.int32, (COLS, COLS), 0)
    col = lax.broadcasted_iota(jnp.int32, (COLS, COLS), 1)
    moments = []
    for pair in range(2):
        turned = pltpu.roll(square, LANES - COLS, 1) if pair else square
        mixed = turned[:, :COLS]
        diagonal = (pltpu.roll(packed, LANES - COLS, 1) if pair else packed)[4:5, :COLS]
        flipped = mixed.T
        moments.append(jnp.where(row <= col, mixed, flipped))
        lower = jnp.where(row == col, diagonal, jnp.where(row > col, mixed, flipped))
        moments.append(lower)
    return moments


def dot(left, right, dims=((1,), (0,))):
    return lax.dot_general(left, right, (dims, ((), ())), precision=HIGH, preferred_element_type=jnp.float32)


def sweeps(matrix):
    size = COLS
    sub = lax.broadcasted_iota(jnp.int32, (size, LANES), 0)
    rows = [jnp.broadcast_to(matrix[:, i : i + 1], (size, LANES)) for i in range(size)]
    for k in range(size):
        scale = 1.0 / rows[k][k : k + 1, :]
        pivot_row = rows[k] * scale
        for i in range(size):
            if i != k:
                factor = rows[i][k : k + 1, :]
                moved = rows[i] - factor * pivot_row
                rows[i] = jnp.where(sub == k, factor * scale, moved)
        rows[k] = jnp.where(sub == k, -scale, pivot_row)
        yield None
    lane = lax.broadcasted_iota(jnp.int32, (size, LANES), 1)
    out = jnp.zeros((size, LANES), jnp.float32)
    for i in range(size):
        out = jnp.where(lane == i, -rows[i], out)
    yield out[:, :size]


def mixer(coeffs, count):
    flipped = split_terms(coeffs.T, count)
    return jnp.concatenate([flipped] * count, axis=1)


def mixed(left, block, count):
    out = jnp.dot(left, split_terms(block, count), preferred_element_type=jnp.float32)
    size = out.shape[0] // count
    return sum(out[size * n : size * (n + 1)] for n in range(count))


def finish_kernel(
    g_ref, v_ref, q_ref, above_ref, below_ref, both_ref,
    ve_ref, qe_ref, abovee_ref, belowe_ref, bothe_ref,
    sol_ref, res_ref, d_ref, dlow_ref, w0_ref, w1_ref, w2_ref,
):
    own_x, own_y = v_ref.shape[0], v_ref.shape[1]
    m0, m1, m2, m3 = unpack_moments(g_ref[...])
    first = ((0,), (0,))
    *_, inv = sweeps(m1)
    alpha = dot(inv, m0)
    m2a = dot(m2, alpha)
    mix = dot(inv, m2a)
    left = mixer(jnp.concatenate([mix, -alpha], axis=0), 3)
    updated = dot(alpha, m2a, first) - m0
    curved = dot(alpha, dot(m3, alpha), first) - dot(m2a, mix, first)
    steps = sweeps(0.5 * (curved + curved.T))
    inv = None
    for x in range(own_x):
        for y in range(own_y):
            q0, q1, qe = q_ref[x, y, :, :LANES], q_ref[x, y, :, LANES:], qe_ref[x, y]
            lane = lanes_of(qe)
            q0 = jnp.where(lane == 0, qe, q0)
            q1 = jnp.where(lane == LANES - 1, turn(qe, LANES // 2), q1)
            block = jnp.concatenate(
                [
                    jnp.concatenate([v_ref[x, y], ve_ref[x, y]], axis=1),
                    jnp.concatenate([q0, q1, qe], axis=1),
                ],
                axis=0,
            )
            value = mixed(left, block, 3)
            d_ref[x, y] = value
            dlow_ref[x, y] = lowered(value)
            if inv is None:
                inv = next(steps)
    gamma = dot(inv, updated)
    edge, main = (abovee_ref, belowe_ref, bothe_ref), (above_ref, below_ref, both_ref)
    whole = (w0_ref, w1_ref, w2_ref)
    for end_ref, main_ref, whole_ref in zip(edge, main, whole):
        for ex in range(1, own_x):
            end = end_ref[ex]
            lane = lanes_of(end)
            whole_ref[ex, :, :LANES] = jnp.where(lane == 0, end, main_ref[ex, :, :LANES])
            end = turn(end, LANES // 2)
            whole_ref[ex, :, LANES:] = jnp.where(lane == LANES - 1, end, main_ref[ex, :, LANES:])
    main, edge = sides_of(*whole), sides_of(*edge)
    zero = jnp.zeros((COLS, COLS), jnp.float32)
    last = mixer(
        jnp.concatenate(
            [
                jnp.concatenate([alpha, gamma, zero, zero], axis=0),
                jnp.concatenate([zero, zero, -alpha, -gamma], axis=0),
            ],
            axis=1,
        ),
        2,
    )
    for x in range(1, own_x - 1):
        for y in range(1, own_y - 1):
            low = lambda i, j, t: dlow_ref[i, j, :, tile_of(t)]
            at = (x, y, x + 1, y + 1)
            plane, down, up = zip(*[terms(low, main, t, *at) for t in range(2)])
            ends = terms(lambda i, j, t: dlow_ref[i, j, :, tile_of(2)], edge, 0, *at)
            from_above = shifted(down, 1, turn(ends[1], LANES // 2))
            from_below = shifted(up, -1, ends[2])
            image = [
                SIGMA * d_ref[x, y, :, tile_of(t)] + (plane[t] - from_above[t] - from_below[t])
                for t in range(2)
            ]
            q0, q1, qe = q_ref[x, y, :, :LANES], q_ref[x, y, :, LANES:], qe_ref[x, y]
            lane = lanes_of(qe)
            q0 = jnp.where(lane == 0, qe, q0)
            q1 = jnp.where(lane == LANES - 1, turn(qe, LANES // 2), q1)
            b = v_ref[x, y]
            block = jnp.concatenate(
                [
                    b,
                    d_ref[x, y, :, : 2 * LANES],
                    jnp.concatenate([q0, q1], axis=1),
                    jnp.concatenate(image, axis=1),
                ],
                axis=0,
            )
            out = mixed(last, block, 2)
            sol_ref[:, x - 1, y - 1, :] = out[:COLS]
            res_ref[:, x - 1, y - 1, :] = b + out[COLS:]


def both_ways(axis, to_next, to_last, around=False):
    count = lax.axis_size(axis)
    steps = range(count) if around else range(count - 1)
    before = lax.ppermute(to_next, axis, [(i, (i + 1) % count) for i in steps])
    after = lax.ppermute(to_last, axis, [((i + 1) % count, i) for i in steps])
    return before, after


def spread(value, axes, groups=None):
    count = lax.axis_size(axes)
    copies = jnp.broadcast_to(value[None], (count, *value.shape))
    return jnp.sum(lax.all_to_all(copies, axes, 0, 0, axis_index_groups=groups), axis=0)


def near(value):
    return pltpu.with_memory_space_constraint(value, pltpu.VMEM)


def on_device(loads, moduli, material):
    f32, bf16, wide = jnp.float32, jnp.bfloat16, 2 * LANES
    own_x, own_y = material.shape[:2]
    ext_x, ext_y = own_x + 4, own_y + 4
    own, levels = pl.pallas_call(
        front_kernel,
        out_shape=(
            pltpu.VMEM((2, COLS + 1, own_x, own_y, LANES), f32),
            pltpu.VMEM((moduli.shape[0], LANES), f32),
        ),
        in_specs=[
            pl.BlockSpec(memory_space=pltpu.SMEM),
            pl.BlockSpec(memory_space=pltpu.VMEM),
            pl.BlockSpec(memory_space=pltpu.VMEM),
        ],
        name="front",
    )(moduli, loads, material)
    place = lax.axis_index(GY)
    row = lax.broadcasted_iota(jnp.int32, (8, LANES), 0)
    flags = jnp.where(row == 0, place > 0, place < lax.axis_size(GY) - 1).astype(f32)
    before, after = both_ways("gx", own, own)
    mid = jnp.concatenate([before, own, after], axis=2)
    before, after = both_ways(GY, mid[:, :, :, 2:], mid[:, :, :, :2], around=True)
    flat = [near(part.reshape(-1, LANES)) for part in (before, mid, after)]
    ends = pltpu.VMEM((COLS + 8, LANES), f32)
    first, last = pl.pallas_call(
        functools.partial(pack_kernel, ext_x=ext_x, ext_y=ext_y), out_shape=(ends, ends), name="pack"
    )(near(flags), *flat)
    before, after = both_ways("gz", last, first)
    nodes = own_x * own_y

    def weights(size):
        return (pltpu.VMEM((ext_x - 1, ext_y, size), f32),) * 3

    def fields(size):
        return (pltpu.VMEM((ext_x - 2, ext_y - 2, COLS, size), f32),) * 2

    def scratch(size):
        return [
            pltpu.VMEM((ext_x, ext_y, COLS, size), f32),
            pltpu.VMEM((ext_x - 2, ext_y - 2, COLS, size), f32),
            pltpu.VMEM((ext_x, ext_y, size), f32),
            pltpu.VMEM((6 * COLS, nodes * size), bf16),
            pltpu.VMEM((12 * COLS, nodes * size), bf16),
        ]

    *main, total, edge, ids = pl.pallas_call(
        main_kernel,
        out_shape=(
            *fields(wide),
            *weights(wide),
            pltpu.VMEM((2 * COLS, LANES), f32),
            pltpu.VMEM((ext_x, ext_y, COLS, LANES), f32),
            pltpu.VMEM((ext_x, ext_y, LANES), f32),
        ),
        scratch_shapes=scratch(wide),
        name="main",
    )(near(levels), near(flags), *flat)
    *edges, moments = pl.pallas_call(
        edge_kernel,
        out_shape=(*fields(LANES), *weights(LANES), pltpu.VMEM((8, LANES), f32)),
        scratch_shapes=scratch(LANES),
        name="edge",
    )(*[near(value) for value in (levels, total, edge, ids, before, after)])
    rows = 5
    count = lax.axis_size("gz")
    middle = [[(i + 5 * count // 8) % count for i in range(count)]]
    moments = spread(moments[:rows].reshape(rows, 1, LANES), "gz", middle)
    moments = spread(moments, PLANE).reshape(rows, LANES)
    moments = jnp.concatenate([moments, jnp.zeros((8 - rows, LANES), f32)], axis=0)
    out = jax.ShapeDtypeStruct(loads.shape, f32)
    return pl.pallas_call(
        finish_kernel,
        out_shape=(out, out),
        scratch_shapes=[pltpu.VMEM((ext_x - 2, ext_y - 2, COLS, 3 * LANES), f32)] * 2
        + [pltpu.VMEM((ext_x - 1, ext_y, wide), f32)] * 3,
        name="finish",
    )(*[near(value) for value in (moments, *main, *edges)])


def solution(mesh):
    wide, long = mesh.shape["gy"] // 2, mesh.shape["gz"]
    split = Mesh(mesh.devices.reshape(mesh.shape["gx"], wide, 2, long), ("gx", "gy_0", "gy_1", "gz"))
    spec = P(None, "gx", GY, "gz")
    return jax.shard_map(
        on_device,
        mesh=split,
        in_specs=(spec, P(), P("gx", GY, "gz")),
        out_specs=(spec, spec),
        check_vma=False,
    )
```

time: 94 us -> 89.6 us (0.953)
  starting transfers between devices: 23.2 us -> 20.4 us
  waiting for transfers between devices: 6.11 us -> 8.74 us
  blocking collectives: 54.2 us -> 51.6 us
  other arithmetic: 2.37 us -> 0.14 us
    ppermute x3, starting transfers between devices: 9.07 us -> 5.32 us  [both_ways(): before = lax.ppermute(to_next, axis, [(i, (i + 1) % count) for i in steps])]
    ppermute x3, waiting for transfers between devices: 3.69 us -> 6.37 us  [both_ways(): after = lax.ppermute(to_last, axis, [((i + 1) % count, i) for i in steps])]
    all_to_all x2, blocking collectives: 54.2 us -> 51.6 us  [spread(): lax.all_to_all(copies, axes, 0, 0, axis_index_groups=groups)]
    ppermute x3, starting transfers between devices: 14.1 us -> 15.1 us  [both_ways(): after = lax.ppermute(to_last, axis, [((i + 1) % count, i) for i in steps])]
    pallas_call x1 -> x3, Pallas kernels: 2.65 us -> 3.65 us  [the longest x1 1.59 us: on_device(): pl.pallas_call(main_kernel, out_shape=(*fields(wide), *weights(wide), plt...]
    another operation x2 -> x0, other arithmetic: 0.95 us -> none  [on_device(): own = jnp.stack([own[..., :LANES], own[..., LANES:]])]
  transfers between devices with their start and end apart: 6 -> 6, of which waited for: 5 -> 5; matrix products, arithmetic and copies ran while one was open for 0% -> 0% of each run, Pallas kernels for 0% -> 2%
where the time goes in v4:
time: 89.6 us; the launch traced here: 89.3 us
  blocking collectives  51.6 us (58%)
  starting transfers between devices  20.4 us (23%)
  waiting for transfers between devices  8.74 us (10%)
  Pallas kernels  7.21 us (8%)
    all_to_all x2, blocking collectives, spread(): lax.all_to_all(copies, axes, 0, 0, axis_index_groups=groups)  51.6 us
    ppermute x3, starting transfers between devices, both_ways(): after = lax.ppermute(to_last, axis, [((i + 1) % count, i) for i in steps])  15.1 us
    ppermute x3, waiting for transfers between devices, both_ways(): after = lax.ppermute(to_last, axis, [((i + 1) % count, i) for i in steps])  6.37 us
    ppermute x3, starting transfers between devices, both_ways(): before = lax.ppermute(to_next, axis, [(i, (i + 1) % count) for i in steps])  5.32 us
    pallas_call x1, Pallas kernels, on_device(): pl.pallas_call(finish_kernel, out_shape=(out, out), scratch_shapes=[pltpu...  3.2 us
    ppermute x3, waiting for transfers between devices, both_ways(): before = lax.ppermute(to_next, axis, [(i, (i + 1) % count) for i in steps])  2.36 us
  transfers between devices with their start and end apart: 6, of which 5 were waited for; matrix products, arithmetic and copies ran while one was open for 0% of the time, Pallas kernels for 2%

profile of v4, /device:TPU:1, one launch (start us, length us, event | category | flops | bytes accessed | tf_op | source)
XLA Modules:
  0.0 89.3 jit_solution(6074568565561600455)
XLA Ops:
  0.6 0.9 %front.1 = (f32[2,17,2,4,128]{4,3,2,1,0:T(4,128)S(1)}, f32[8,128]{1,0:T(8,128)S(1)}) custom-call(f32[8]{0:T(128)} %moduli_ref.1, f32[16,2,4,256]{3,2,1,0:T(4,128)} %loads_ref.1, s32[2,4,256]{2,1,0:T(4,128)} %material_ref.1), custom_call_target="tpu_custom_call" | custom-call | tf_op jit(solution)/shard_map/front/pallas_call | solution.py:501
  1.6 4.0 %collective-permute-start = (f32[2,17,2,4,128]{4,3,2,1,0:T(4,128)S(1)}, f32[2,17,2,4,128]{4,3,2,1,0:T(4,128)S(1)}, u32[]{:S(2)}, u32[]{:S(2)}) collective-permute-start(f32[2,17,2,4,128]{4,3,2,1,0:T(4,128)S(1)} %get-tuple-element.21), channel_id=1, source_target_pairs={{0,256},{256,512},{512,768},{1,257},{257,513},{513,769},{2,258},{2... | collective-permute-start | bytes 417800 | tf_op jit(solution)/shard_map/ppermute | solution.py:482
  5.6 1.3 %collective-permute-start.1 = (f32[2,17,2,4,128]{4,3,2,1,0:T(4,128)S(1)}, f32[2,17,2,4,128]{4,3,2,1,0:T(4,128)S(1)}, u32[]{:S(2)}, u32[]{:S(2)}) collective-permute-start(f32[2,17,2,4,128]{4,3,2,1,0:T(4,128)S(1)} %get-tuple-element.21), channel_id=1, source_target_pairs={{256,0},{512,256},{768,512},{257,1},{513,257},{769,513},{258,2},{5... | collective-permute-start | bytes 417800 | tf_op jit(solution)/shard_map/ppermute | solution.py:483
  6.9 0.7 collective-permute-done
  7.7 3.8 %collective-permute-done.1 = f32[2,17,2,4,128]{4,3,2,1,0:T(4,128)S(1)} collective-permute-done((f32[2,17,2,4,128]{4,3,2,1,0:T(4,128)S(1)}, f32[2,17,2,4,128]{4,3,2,1,0:T(4,128)S(1)}, u32[]{:S(2)}, u32[]{:S(2)}) %collective-permute-start.1) | collective-permute-done | bytes 139296 | tf_op jit(solution)/shard_map/ppermute | solution.py:483
  11.4 0.2 fusion
  11.6 12.5 %collective-permute-start.3 = (f32[2,17,6,2,128]{4,3,2,1,0:T(2,128)S(1)}, f32[2,17,6,2,128]{4,3,2,1,0:T(2,128)S(1)}, u32[]{:S(2)}, u32[]{:S(2)}) collective-permute-start(f32[2,17,6,2,128]{4,3,2,1,0:T(2,128)S(1)} %get-tuple-element.38), channel_id=1, source_target_pairs={{32,0},{64,32},{96,64},{128,96},{160,128},{192,160},{224,192},{0,2... | collective-permute-start | bytes 626696 | tf_op jit(solution)/shard_map/ppermute | solution.py:483
  24.2 0.0 collective-permute-start.2
  24.2 1.1 %collective-permute-done.3 = f32[2,17,6,2,128]{4,3,2,1,0:T(2,128)S(1)} collective-permute-done((f32[2,17,6,2,128]{4,3,2,1,0:T(2,128)S(1)}, f32[2,17,6,2,128]{4,3,2,1,0:T(2,128)S(1)}, u32[]{:S(2)}, u32[]{:S(2)}) %collective-permute-start.3) | collective-permute-done | bytes 208928 | tf_op jit(solution)/shard_map/ppermute | solution.py:483
  25.2 1.7 %collective-permute-done.2 = f32[2,17,6,2,128]{4,3,2,1,0:T(2,128)S(1)} collective-permute-done((f32[2,17,6,2,128]{4,3,2,1,0:T(2,128)S(1)}, f32[2,17,6,2,128]{4,3,2,1,0:T(2,128)S(1)}, u32[]{:S(2)}, u32[]{:S(2)}) %collective-permute-start.2) | collective-permute-done | bytes 208928 | tf_op jit(solution)/shard_map/ppermute | solution.py:482
  26.9 0.1 iota.7.flags_ref
  27.0 0.4 pack.1
  27.4 1.3 %collective-permute-start.4 = (f32[24,128]{1,0:T(8,128)S(1)}, f32[24,128]{1,0:T(8,128)S(1)}, u32[]{:S(2)}, u32[]{:S(2)}) collective-permute-start(f32[24,128]{1,0:T(8,128)S(1)} %get-tuple-element.25), channel_id=1, source_target_pairs={{0,1},{1,2},{2,3},{3,4},{4,5},{5,6},{6,7},{7,8},{8,9},{9,10},{10,1... | collective-permute-start | bytes 36872 | tf_op jit(solution)/shard_map/ppermute | solution.py:482
  28.6 1.3 %collective-permute-start.5 = (f32[24,128]{1,0:T(8,128)S(1)}, f32[24,128]{1,0:T(8,128)S(1)}, u32[]{:S(2)}, u32[]{:S(2)}) collective-permute-start(f32[24,128]{1,0:T(8,128)S(1)} %get-tuple-element.26), channel_id=1, source_target_pairs={{1,0},{2,1},{3,2},{4,3},{5,4},{6,5},{7,6},{8,7},{9,8},{10,9},{11,1... | collective-permute-start | bytes 36872 | tf_op jit(solution)/shard_map/ppermute | solution.py:483
  29.9 1.6 %main.1 = (f32[4,6,16,256]{3,2,1,0:T(8,128)S(1)}, f32[4,6,16,256]{3,2,1,0:T(8,128)S(1)}, f32[5,8,256]{2,1,0:T(8,128)S(1)}, f32[5,8,256]{2,1,0:T(8,128)S(1)}, f32...) custom-call(f32[8,128]{1,0:T(8,128)S(1)} %get-tuple-element.20.levels_r, ...), custom_call_target="tpu_custom_call" | custom-call | tf_op jit(solution)/shard_map/main/pallas_call | solution.py:543
  31.5 0.0 collective-permute-done.4.before_ref
  31.6 1.5 %collective-permute-done.5.after_ref = f32[24,128]{1,0:T(8,128)S(1)} collective-permute-done((f32[24,128]{1,0:T(8,128)S(1)}, f32[24,128]{1,0:T(8,128)S(1)}, u32[]{:S(2)}, u32[]{:S(2)}) %collective-permute-start.5) | collective-permute-done | bytes 12320 | tf_op jit(solution)/shard_map/ppermute | solution.py:483
  33.1 1.1 %edge.1 = (f32[4,6,16,128]{3,2,1,0:T(8,128)S(1)}, f32[4,6,16,128]{3,2,1,0:T(8,128)S(1)}, f32[5,8,128]{2,1,0:T(8,128)S(1)}, f32[5,8,128]{2,1,0:T(8,128)S(1)}, f32...) custom-call(f32[8,128]{1,0:T(8,128)S(1)} %get-tuple-element.20.levels_ref, f32[32,128]{1,0:T(8,128)S(1)} %get-tuple-element.22.total_ref, ...), custom_call_target="tpu_custom_call" | custom-call | tf_op jit(solution)/shard_map/edge/pallas_call | solution.py:555
  34.2 0.1 broadcast_in_dim.22
  34.3 34.1 %all_to_all.10 = f32[32,5,1,128]{3,2,1,0:T(1,128)S(1)} all-to-all(f32[32,5,1,128]{3,2,1,0:T(1,128)S(1)} %broadcast_in_dim.22), channel_id=1, replica_groups={{20,21,22,23,24,25,26,27,28,29,30,31,0,1,2,3,4,5,6,7,8,9,10,11,12,13,14..., dimensions={0} | all-to-all | bytes 163840 | tf_op jit(solution)/shard_map/all_to_all | solution.py:490
  68.3 0.1 reduce_sum.18
  68.4 17.6 %all_to_all.11 = f32[32,5,1,128]{3,2,1,0:T(1,128)S(1)} all-to-all(f32[32,5,1,128]{3,2,1,0:T(1,128)S(1)} %broadcast_in_dim.23), channel_id=1, replica_groups=mesh['gx'=4,'gy_0'=4,'gy_1'=2,'gz'=32] {'gx','gy_0','gy_1'}, dimensions={0} | all-to-all | bytes 163840 | tf_op jit(solution)/shard_map/all_to_all | solution.py:490
  86.0 0.1 reduce_sum.19
  86.1 3.2 %finish.1 = (f32[16,2,4,256]{3,2,1,0:T(4,128)}, f32[16,2,4,256]{3,2,1,0:T(4,128)}) custom-call(f32[8,128]{1,0:T(8,128)S(1)} %concatenate.7.g_ref, f32[4,6,16,256]{3,2,1,0:T(8,128)S(1)} %get-tuple-element.28.v_ref, f32[4,6,16,256]{3,2,1,0:T(8,128)S(1)} %get-tuple-element.29.q_ref, f32[5,8,256]{2,1,0:T(8,128)S(1)} %get-tuple-element.30.above_ref, ...), custom_call_target="tpu_custom_call" | custom-call | tf_op jit(solution)/shard_map/finish/pallas_call | solution.py:568
  (6 shorter events, 0.1 us)
Async XLA Ops:
  1.6 6.0 %collective-permute-start = (f32[2,17,2,4,128]{4,3,2,1,0:T(4,128)S(1)}, f32[2,17,2,4,128]{4,3,2,1,0:T(4,128)S(1)}, u32[]{:S(2)}, u32[]{:S(2)}) collective-permute-start(f32[2,17,2,4,128]{4,3,2,1,0:T(4,128)S(1)} %get-tuple-element.21), channel_id=1, source_target_pairs={{0,256},{256,512},{512,768},{1,257},{257,513},{513,769},{2,258},{2... | collective-permute-start | bytes 417800 | tf_op jit(solution)/shard_map/ppermute | solution.py:482
  5.6 5.8 %collective-permute-start.1 = (f32[2,17,2,4,128]{4,3,2,1,0:T(4,128)S(1)}, f32[2,17,2,4,128]{4,3,2,1,0:T(4,128)S(1)}, u32[]{:S(2)}, u32[]{:S(2)}) collective-permute-start(f32[2,17,2,4,128]{4,3,2,1,0:T(4,128)S(1)} %get-tuple-element.21), channel_id=1, source_target_pairs={{256,0},{512,256},{768,512},{257,1},{513,257},{769,513},{258,2},{5... | collective-permute-start | bytes 417800 | tf_op jit(solution)/shard_map/ppermute | solution.py:483
  11.6 13.6 %collective-permute-start.3 = (f32[2,17,6,2,128]{4,3,2,1,0:T(2,128)S(1)}, f32[2,17,6,2,128]{4,3,2,1,0:T(2,128)S(1)}, u32[]{:S(2)}, u32[]{:S(2)}) collective-permute-start(f32[2,17,6,2,128]{4,3,2,1,0:T(2,128)S(1)} %get-tuple-element.38), channel_id=1, source_target_pairs={{32,0},{64,32},{96,64},{128,96},{160,128},{192,160},{224,192},{0,2... | collective-permute-start | bytes 626696 | tf_op jit(solution)/shard_map/ppermute | solution.py:483
  24.2 2.7 %collective-permute-start.2 = (f32[2,17,6,2,128]{4,3,2,1,0:T(2,128)S(1)}, f32[2,17,6,2,128]{4,3,2,1,0:T(2,128)S(1)}, u32[]{:S(2)}, u32[]{:S(2)}) collective-permute-start(f32[2,17,6,2,128]{4,3,2,1,0:T(2,128)S(1)} %get-tuple-element.39), channel_id=1, source_target_pairs={{0,32},{32,64},{64,96},{96,128},{128,160},{160,192},{192,224},{224... | collective-permute-start | bytes 626696 | tf_op jit(solution)/shard_map/ppermute | solution.py:482
  27.4 4.2 %collective-permute-start.4 = (f32[24,128]{1,0:T(8,128)S(1)}, f32[24,128]{1,0:T(8,128)S(1)}, u32[]{:S(2)}, u32[]{:S(2)}) collective-permute-start(f32[24,128]{1,0:T(8,128)S(1)} %get-tuple-element.25), channel_id=1, source_target_pairs={{0,1},{1,2},{2,3},{3,4},{4,5},{5,6},{6,7},{7,8},{8,9},{9,10},{10,1... | collective-permute-start | bytes 36872 | tf_op jit(solution)/shard_map/ppermute | solution.py:482
  28.6 4.4 %collective-permute-start.5 = (f32[24,128]{1,0:T(8,128)S(1)}, f32[24,128]{1,0:T(8,128)S(1)}, u32[]{:S(2)}, u32[]{:S(2)}) collective-permute-start(f32[24,128]{1,0:T(8,128)S(1)} %get-tuple-element.26), channel_id=1, source_target_pairs={{1,0},{2,1},{3,2},{4,3},{5,4},{6,5},{7,6},{8,7},{9,8},{10,9},{11,1... | collective-permute-start | bytes 36872 | tf_op jit(solution)/shard_map/ppermute | solution.py:483

commit v5 on v4

--- a/solution.py
+++ b/solution.py
@@ -484,10 +484,11 @@
     return before, after
 
 
-def spread(value, axes, groups=None):
+def spread(value, axes, root):
     count = lax.axis_size(axes)
     copies = jnp.broadcast_to(value[None], (count, *value.shape))
-    return jnp.sum(lax.all_to_all(copies, axes, 0, 0, axis_index_groups=groups), axis=0)
+    group = [(root + i) % count for i in range(count)]
+    return jnp.sum(lax.all_to_all(copies, axes, 0, 0, axis_index_groups=[group]), axis=0)
 
 
 def near(value):
@@ -559,10 +560,10 @@
         name="edge",
     )(*[near(value) for value in (levels, total, edge, ids, before, after)])
     rows = 5
-    count = lax.axis_size("gz")
-    middle = [[(i + 5 * count // 8) % count for i in range(count)]]
-    moments = spread(moments[:rows].reshape(rows, 1, LANES), "gz", middle)
-    moments = spread(moments, PLANE).reshape(rows, LANES)
+    length, chips = lax.axis_size("gz"), lax.axis_size("gy_0")
+    moments = spread(moments[:rows].reshape(rows, 1, LANES), "gz", 9 * length // 16)
+    middle = (lax.axis_size("gx") // 2 * chips + chips // 2) * 2 + 1
+    moments = spread(moments, PLANE, middle).reshape(rows, LANES)
     moments = jnp.concatenate([moments, jnp.zeros((8 - rows, LANES), f32)], axis=0)
     out = jax.ShapeDtypeStruct(loads.shape, f32)
     return pl.pallas_call(

time: 89.6 us -> 85.1 us (0.950)
  blocking collectives: 51.6 us -> 47.1 us
    all_to_all x2, blocking collectives: 51.6 us -> 47.1 us  [spread(): lax.all_to_all(copies, axes, 0, 0, axis_index_groups=[group])]
where the time goes in v5:
time: 85.1 us; the launch traced here: 84.8 us
  blocking collectives  47.1 us (55%)
  starting transfers between devices  20.4 us (24%)
  waiting for transfers between devices  8.74 us (10%)
  Pallas kernels  7.21 us (8%)
    all_to_all x2, blocking collectives, spread(): lax.all_to_all(copies, axes, 0, 0, axis_index_groups=[group])  47.1 us
    ppermute x3, starting transfers between devices, both_ways(): after = lax.ppermute(to_last, axis, [((i + 1) % count, i) for i in steps])  15.1 us
    ppermute x3, waiting for transfers between devices, both_ways(): after = lax.ppermute(to_last, axis, [((i + 1) % count, i) for i in steps])  6.37 us
    ppermute x3, starting transfers between devices, both_ways(): before = lax.ppermute(to_next, axis, [(i, (i + 1) % count) for i in steps])  5.32 us
    pallas_call x1, Pallas kernels, on_device(): pl.pallas_call(finish_kernel, out_shape=(out, out), scratch_shapes=[pltpu...  3.2 us
    ppermute x3, waiting for transfers between devices, both_ways(): before = lax.ppermute(to_next, axis, [(i, (i + 1) % count) for i in steps])  2.36 us
  transfers between devices with their start and end apart: 6, of which 5 were waited for; matrix products, arithmetic and copies ran while one was open for 0% of the time, Pallas kernels for 2%

profile of v5, /device:TPU:1, one launch (start us, length us, event | category | flops | bytes accessed | tf_op | source)
XLA Modules:
  0.0 84.8 jit_solution(17610658160203302698)
XLA Ops:
  0.6 0.9 %front.1 = (f32[2,17,2,4,128]{4,3,2,1,0:T(4,128)S(1)}, f32[8,128]{1,0:T(8,128)S(1)}) custom-call(f32[8]{0:T(128)} %moduli_ref.1, f32[16,2,4,256]{3,2,1,0:T(4,128)} %loads_ref.1, s32[2,4,256]{2,1,0:T(4,128)} %material_ref.1), custom_call_target="tpu_custom_call" | custom-call | tf_op jit(solution)/shard_map/front/pallas_call | solution.py:502
  1.6 4.0 %collective-permute-start = (f32[2,17,2,4,128]{4,3,2,1,0:T(4,128)S(1)}, f32[2,17,2,4,128]{4,3,2,1,0:T(4,128)S(1)}, u32[]{:S(2)}, u32[]{:S(2)}) collective-permute-start(f32[2,17,2,4,128]{4,3,2,1,0:T(4,128)S(1)} %get-tuple-element.21), channel_id=1, source_target_pairs={{0,256},{256,512},{512,768},{1,257},{257,513},{513,769},{2,258},{2... | collective-permute-start | bytes 417800 | tf_op jit(solution)/shard_map/ppermute | solution.py:482
  5.6 1.3 %collective-permute-start.1 = (f32[2,17,2,4,128]{4,3,2,1,0:T(4,128)S(1)}, f32[2,17,2,4,128]{4,3,2,1,0:T(4,128)S(1)}, u32[]{:S(2)}, u32[]{:S(2)}) collective-permute-start(f32[2,17,2,4,128]{4,3,2,1,0:T(4,128)S(1)} %get-tuple-element.21), channel_id=1, source_target_pairs={{256,0},{512,256},{768,512},{257,1},{513,257},{769,513},{258,2},{5... | collective-permute-start | bytes 417800 | tf_op jit(solution)/shard_map/ppermute | solution.py:483
  6.9 0.7 collective-permute-done
  7.7 3.8 %collective-permute-done.1 = f32[2,17,2,4,128]{4,3,2,1,0:T(4,128)S(1)} collective-permute-done((f32[2,17,2,4,128]{4,3,2,1,0:T(4,128)S(1)}, f32[2,17,2,4,128]{4,3,2,1,0:T(4,128)S(1)}, u32[]{:S(2)}, u32[]{:S(2)}) %collective-permute-start.1) | collective-permute-done | bytes 139296 | tf_op jit(solution)/shard_map/ppermute | solution.py:483
  11.4 0.2 fusion
  11.6 12.5 %collective-permute-start.3 = (f32[2,17,6,2,128]{4,3,2,1,0:T(2,128)S(1)}, f32[2,17,6,2,128]{4,3,2,1,0:T(2,128)S(1)}, u32[]{:S(2)}, u32[]{:S(2)}) collective-permute-start(f32[2,17,6,2,128]{4,3,2,1,0:T(2,128)S(1)} %get-tuple-element.38), channel_id=1, source_target_pairs={{32,0},{64,32},{96,64},{128,96},{160,128},{192,160},{224,192},{0,2... | collective-permute-start | bytes 626696 | tf_op jit(solution)/shard_map/ppermute | solution.py:483
  24.2 0.0 collective-permute-start.2
  24.2 1.1 %collective-permute-done.3 = f32[2,17,6,2,128]{4,3,2,1,0:T(2,128)S(1)} collective-permute-done((f32[2,17,6,2,128]{4,3,2,1,0:T(2,128)S(1)}, f32[2,17,6,2,128]{4,3,2,1,0:T(2,128)S(1)}, u32[]{:S(2)}, u32[]{:S(2)}) %collective-permute-start.3) | collective-permute-done | bytes 208928 | tf_op jit(solution)/shard_map/ppermute | solution.py:483
  25.2 1.7 %collective-permute-done.2 = f32[2,17,6,2,128]{4,3,2,1,0:T(2,128)S(1)} collective-permute-done((f32[2,17,6,2,128]{4,3,2,1,0:T(2,128)S(1)}, f32[2,17,6,2,128]{4,3,2,1,0:T(2,128)S(1)}, u32[]{:S(2)}, u32[]{:S(2)}) %collective-permute-start.2) | collective-permute-done | bytes 208928 | tf_op jit(solution)/shard_map/ppermute | solution.py:482
  26.9 0.1 iota.7.flags_ref
  27.0 0.4 pack.1
  27.4 1.3 %collective-permute-start.4 = (f32[24,128]{1,0:T(8,128)S(1)}, f32[24,128]{1,0:T(8,128)S(1)}, u32[]{:S(2)}, u32[]{:S(2)}) collective-permute-start(f32[24,128]{1,0:T(8,128)S(1)} %get-tuple-element.25), channel_id=1, source_target_pairs={{0,1},{1,2},{2,3},{3,4},{4,5},{5,6},{6,7},{7,8},{8,9},{9,10},{10,1... | collective-permute-start | bytes 36872 | tf_op jit(solution)/shard_map/ppermute | solution.py:482
  28.6 1.3 %collective-permute-start.5 = (f32[24,128]{1,0:T(8,128)S(1)}, f32[24,128]{1,0:T(8,128)S(1)}, u32[]{:S(2)}, u32[]{:S(2)}) collective-permute-start(f32[24,128]{1,0:T(8,128)S(1)} %get-tuple-element.26), channel_id=1, source_target_pairs={{1,0},{2,1},{3,2},{4,3},{5,4},{6,5},{7,6},{8,7},{9,8},{10,9},{11,1... | collective-permute-start | bytes 36872 | tf_op jit(solution)/shard_map/ppermute | solution.py:483
  29.9 1.6 %main.1 = (f32[4,6,16,256]{3,2,1,0:T(8,128)S(1)}, f32[4,6,16,256]{3,2,1,0:T(8,128)S(1)}, f32[5,8,256]{2,1,0:T(8,128)S(1)}, f32[5,8,256]{2,1,0:T(8,128)S(1)}, f32...) custom-call(f32[8,128]{1,0:T(8,128)S(1)} %get-tuple-element.20.levels_r, ...), custom_call_target="tpu_custom_call" | custom-call | tf_op jit(solution)/shard_map/main/pallas_call | solution.py:544
  31.5 0.0 collective-permute-done.4.before_ref
  31.6 1.5 %collective-permute-done.5.after_ref = f32[24,128]{1,0:T(8,128)S(1)} collective-permute-done((f32[24,128]{1,0:T(8,128)S(1)}, f32[24,128]{1,0:T(8,128)S(1)}, u32[]{:S(2)}, u32[]{:S(2)}) %collective-permute-start.5) | collective-permute-done | bytes 12320 | tf_op jit(solution)/shard_map/ppermute | solution.py:483
  33.1 1.1 %edge.1 = (f32[4,6,16,128]{3,2,1,0:T(8,128)S(1)}, f32[4,6,16,128]{3,2,1,0:T(8,128)S(1)}, f32[5,8,128]{2,1,0:T(8,128)S(1)}, f32[5,8,128]{2,1,0:T(8,128)S(1)}, f32...) custom-call(f32[8,128]{1,0:T(8,128)S(1)} %get-tuple-element.20.levels_ref, f32[32,128]{1,0:T(8,128)S(1)} %get-tuple-element.22.total_ref, ...), custom_call_target="tpu_custom_call" | custom-call | tf_op jit(solution)/shard_map/edge/pallas_call | solution.py:556
  34.2 0.1 broadcast_in_dim.22
  34.3 33.0 %all_to_all.10 = f32[32,5,1,128]{3,2,1,0:T(1,128)S(1)} all-to-all(f32[32,5,1,128]{3,2,1,0:T(1,128)S(1)} %broadcast_in_dim.22), channel_id=1, replica_groups={{18,19,20,21,22,23,24,25,26,27,28,29,30,31,0,1,2,3,4,5,6,7,8,9,10,11,12..., dimensions={0} | all-to-all | bytes 163840 | tf_op jit(solution)/shard_map/all_to_all | solution.py:491
  67.3 0.1 reduce_sum.18
  67.4 14.1 %all_to_all.11 = f32[32,5,1,128]{3,2,1,0:T(1,128)S(1)} all-to-all(f32[32,5,1,128]{3,2,1,0:T(1,128)S(1)} %broadcast_in_dim.23), channel_id=1, replica_groups={{672,704,736,768,800,832,864,896,928,960,992,0,32,64,96,128,160,192,224..., dimensions={0} | all-to-all | bytes 163840 | tf_op jit(solution)/shard_map/all_to_all | solution.py:491
  81.5 0.1 reduce_sum.19
  81.6 3.2 %finish.1 = (f32[16,2,4,256]{3,2,1,0:T(4,128)}, f32[16,2,4,256]{3,2,1,0:T(4,128)}) custom-call(f32[8,128]{1,0:T(8,128)S(1)} %concatenate.7.g_ref, f32[4,6,16,256]{3,2,1,0:T(8,128)S(1)} %get-tuple-element.28.v_ref, f32[4,6,16,256]{3,2,1,0:T(8,128)S(1)} %get-tuple-element.29.q_ref, f32[5,8,256]{2,1,0:T(8,128)S(1)} %get-tuple-element.30.above_ref, ...), custom_call_target="tpu_custom_call" | custom-call | tf_op jit(solution)/shard_map/finish/pallas_call | solution.py:569
  (6 shorter events, 0.1 us)
Async XLA Ops:
  1.6 6.0 %collective-permute-start = (f32[2,17,2,4,128]{4,3,2,1,0:T(4,128)S(1)}, f32[2,17,2,4,128]{4,3,2,1,0:T(4,128)S(1)}, u32[]{:S(2)}, u32[]{:S(2)}) collective-permute-start(f32[2,17,2,4,128]{4,3,2,1,0:T(4,128)S(1)} %get-tuple-element.21), channel_id=1, source_target_pairs={{0,256},{256,512},{512,768},{1,257},{257,513},{513,769},{2,258},{2... | collective-permute-start | bytes 417800 | tf_op jit(solution)/shard_map/ppermute | solution.py:482
  5.6 5.8 %collective-permute-start.1 = (f32[2,17,2,4,128]{4,3,2,1,0:T(4,128)S(1)}, f32[2,17,2,4,128]{4,3,2,1,0:T(4,128)S(1)}, u32[]{:S(2)}, u32[]{:S(2)}) collective-permute-start(f32[2,17,2,4,128]{4,3,2,1,0:T(4,128)S(1)} %get-tuple-element.21), channel_id=1, source_target_pairs={{256,0},{512,256},{768,512},{257,1},{513,257},{769,513},{258,2},{5... | collective-permute-start | bytes 417800 | tf_op jit(solution)/shard_map/ppermute | solution.py:483
  11.6 13.6 %collective-permute-start.3 = (f32[2,17,6,2,128]{4,3,2,1,0:T(2,128)S(1)}, f32[2,17,6,2,128]{4,3,2,1,0:T(2,128)S(1)}, u32[]{:S(2)}, u32[]{:S(2)}) collective-permute-start(f32[2,17,6,2,128]{4,3,2,1,0:T(2,128)S(1)} %get-tuple-element.38), channel_id=1, source_target_pairs={{32,0},{64,32},{96,64},{128,96},{160,128},{192,160},{224,192},{0,2... | collective-permute-start | bytes 626696 | tf_op jit(solution)/shard_map/ppermute | solution.py:483
  24.2 2.7 %collective-permute-start.2 = (f32[2,17,6,2,128]{4,3,2,1,0:T(2,128)S(1)}, f32[2,17,6,2,128]{4,3,2,1,0:T(2,128)S(1)}, u32[]{:S(2)}, u32[]{:S(2)}) collective-permute-start(f32[2,17,6,2,128]{4,3,2,1,0:T(2,128)S(1)} %get-tuple-element.39), channel_id=1, source_target_pairs={{0,32},{32,64},{64,96},{96,128},{128,160},{160,192},{192,224},{224... | collective-permute-start | bytes 626696 | tf_op jit(solution)/shard_map/ppermute | solution.py:482
  27.4 4.2 %collective-permute-start.4 = (f32[24,128]{1,0:T(8,128)S(1)}, f32[24,128]{1,0:T(8,128)S(1)}, u32[]{:S(2)}, u32[]{:S(2)}) collective-permute-start(f32[24,128]{1,0:T(8,128)S(1)} %get-tuple-element.25), channel_id=1, source_target_pairs={{0,1},{1,2},{2,3},{3,4},{4,5},{5,6},{6,7},{7,8},{8,9},{9,10},{10,1... | collective-permute-start | bytes 36872 | tf_op jit(solution)/shard_map/ppermute | solution.py:482
  28.6 4.4 %collective-permute-start.5 = (f32[24,128]{1,0:T(8,128)S(1)}, f32[24,128]{1,0:T(8,128)S(1)}, u32[]{:S(2)}, u32[]{:S(2)}) collective-permute-start(f32[24,128]{1,0:T(8,128)S(1)} %get-tuple-element.26), channel_id=1, source_target_pairs={{1,0},{2,1},{3,2},{4,3},{5,4},{6,5},{7,6},{8,7},{9,8},{10,9},{11,1... | collective-permute-start | bytes 36872 | tf_op jit(solution)/shard_map/ppermute | solution.py:483

commit v6 on v5

--- a/solution.py
+++ b/solution.py
@@ -83,19 +83,20 @@
 def terms(low, sides, tile, x, y, wx, wy):
     above, below, both = sides
     around = {(i, j): low(x + i, y + j, tile) for i in (-1, 0, 1) for j in (-1, 0, 1)}
-    centre = 4.0 * around[0, 0]
     total = None
     for i in (-1, 1):
         for j in (-1, 1):
             ex, ey = wx + (i - 1) // 2, wy + (j - 1) // 2
             others = around[i, 0] + around[0, j] + around[i, j]
             new = (
-                both(ex, ey, tile) * (centre - around[i, j]),
+                both(ex, ey, tile) * around[i, j],
                 below(ex, ey, tile) * others,
                 above(ex, ey, tile) * others,
             )
             total = new if total is None else tuple(a + b for a, b in zip(total, new))
-    return total
+    rim = [both(wx + i, wy + j, tile) for i in (-1, 0) for j in (-1, 0)]
+    centre = (4.0 * ((rim[0] + rim[1]) + (rim[2] + rim[3]))) * around[0, 0]
+    return centre - total[0], total[1], total[2]
 
 
 def operator(field, low, sides, count, x, y, wx, wy):
@@ -194,14 +195,15 @@
                 sides, count, x, y, x, y,
             )
             for t in range(count):
-                value = jnp.where(e_ref[x, y : y + 1, tile_of(t)] > 0.0, image[t], 0.0)
+                value = image[t]
+                if count == 1 or x in (1, ext_x - 2) or y in (1, ext_y - 2):
+                    value = jnp.where(e_ref[x, y : y + 1, tile_of(t)] > 0.0, value, 0.0)
                 q_ref[x - 1, y - 1, :, tile_of(t)] = value
                 qlow_ref[x - 1, y - 1, :, tile_of(t)] = lowered(value)
 
 
-def gram_terms(v_ref, q_ref, qlow_ref, sides, count, keep, left_ref, right_ref):
+def own_nodes(v_ref, q_ref, qlow_ref, sides, count):
     own_x, own_y = v_ref.shape[0], v_ref.shape[1]
-    node = 0
     for x in range(1, own_x - 1):
         for y in range(1, own_y - 1):
             image = operator(
@@ -210,21 +212,21 @@
                 sides, count, x, y, x + 1, y + 1,
             )
             for t in range(count):
-                b, q = v_ref[x, y, :, tile_of(t)], q_ref[x, y, :, tile_of(t)]
-                at = tile_of(node * count + t)
-                left = jnp.concatenate([b, q], axis=0)
-                left = jnp.where(keep(lanes_of(left), t), left, 0.0)
-                left_ref[:, at] = split_terms(left, 3)
-                right = jnp.concatenate([b, q, image[t], jnp.zeros_like(b)], axis=0)
-                right_ref[:, at] = split_terms(right, 3)
-            node += 1
-    product = lax.dot_general(
-        left_ref[...], right_ref[...], (((1,), (1,)), ((), ())), preferred_element_type=jnp.float32
-    )
-    half = LANES // 2
-    third = jnp.concatenate([product[:, LANES:], jnp.zeros((6 * COLS, half), jnp.float32)], axis=1)
-    folded = product[:, :LANES] + turn(product[:, :LANES], half) + third
-    return sum(folded[2 * COLS * n : 2 * COLS * (n + 1)] for n in range(3))
+                yield t, v_ref[x, y, :, tile_of(t)], q_ref[x, y, :, tile_of(t)], image[t]
+
+
+def left_terms(right):
+    return jnp.concatenate([right[3 * COLS * n : 3 * COLS * n + 2 * COLS] for n in range(3)], axis=0)
+
+
+def products(left, right):
+    product = lax.dot_general(left, right, (((1,), (1,)), ((), ())), preferred_element_type=jnp.float32)
+    rows = sum(product[2 * COLS * n : 2 * COLS * (n + 1)] for n in range(3))
+    lane = lax.broadcasted_iota(jnp.int32, (2 * COLS, LANES), 1)
+    first = rows[:, :LANES]
+    rest = jnp.concatenate([rows[:, LANES:], jnp.zeros((2 * COLS, 2 * LANES - 9 * COLS), jnp.float32)], axis=1)
+    third = jnp.where(lane < 2 * COLS, turn(first, -6 * COLS), turn(rest, 2 * COLS))
+    return first + turn(first, -3 * COLS) + third
 
 
 def main_kernel(
@@ -257,17 +259,19 @@
                     v_ref[x - 1, y - 1, :, tile_of(t)] = tiles[t]
     sides = sides_of(above_ref, below_ref, both_ref)
     first_image(v_ref, low_ref, e_ref, sides, q_ref, qlow_ref, 2)
-    total_ref[...] = gram_terms(
-        v_ref, q_ref, qlow_ref, sides, 2,
-        lambda lane, t: lane >= 2 if t == 0 else lane < LANES - 2,
-        left_ref, right_ref,
-    )
+    for n, (t, b, q, w) in enumerate(own_nodes(v_ref, q_ref, qlow_ref, sides, 2)):
+        right = split_terms(jnp.concatenate([b, q, w], axis=0), 3)
+        left = left_terms(right)
+        here = lanes_of(left) >= 2 if t == 0 else lanes_of(left) < LANES - 2
+        left_ref[:, tile_of(n)] = jnp.where(here, left, jnp.zeros_like(left))
+        right_ref[:, tile_of(n)] = right
+    total_ref[...] = products(left_ref[...], right_ref[...])
 
 
 def edge_kernel(
     levels_ref, total_ref, ve_ref, ie_ref, before_ref, after_ref,
     v_ref, q_ref, above_ref, below_ref, both_ref, g_ref,
-    low_ref, qlow_ref, e_ref, left_ref, right_ref,
+    low_ref, qlow_ref, e_ref,
 ):
     ext_x, ext_y = low_ref.shape[0], low_ref.shape[1]
 
@@ -290,11 +294,14 @@
                 v_ref[x - 1, y - 1] = value
     sides = sides_of(above_ref, below_ref, both_ref)
     first_image(v_ref, low_ref, e_ref, sides, q_ref, qlow_ref, 1)
-    total = gram_terms(
-        v_ref, q_ref, qlow_ref, sides, 1,
-        lambda lane, t: (lane < 2) | ((lane >= 2 * EDGE - 2) & (lane < 2 * EDGE)),
-        left_ref, right_ref,
-    )
+    right = jnp.zeros((3 * COLS, LANES), jnp.float32)
+    for n, (_, b, q, w) in enumerate(own_nodes(v_ref, q_ref, qlow_ref, sides, 1)):
+        three = jnp.concatenate([b, q, w], axis=0)
+        at = lanes_of(three) - 2 * n
+        here = ((at >= 0) & (at < 2)) | ((at >= 2 * EDGE - 2) & (at < 2 * EDGE))
+        right = jnp.where(here, turn(three, 2 * n), right)
+    right = split_terms(right, 3)
+    total = products(left_terms(right), right)
     g_ref[...] = pack_moments(total_ref[...] + total)
 
 
@@ -356,25 +363,30 @@
     return lax.dot_general(left, right, (dims, ((), ())), precision=HIGH, preferred_element_type=jnp.float32)
 
 
-def sweeps(matrix):
-    size = COLS
-    sub = lax.broadcasted_iota(jnp.int32, (size, LANES), 0)
-    rows = [jnp.broadcast_to(matrix[:, i : i + 1], (size, LANES)) for i in range(size)]
-    for k in range(size):
+def replicated(matrix):
+    return [jnp.broadcast_to(matrix[:, i : i + 1], (COLS, LANES)) for i in range(COLS)]
+
+
+def sweeps(rows):
+    rows = list(rows)
+    sub = lax.broadcasted_iota(jnp.int32, (COLS, LANES), 0)
+    for k in range(COLS):
         scale = 1.0 / rows[k][k : k + 1, :]
         pivot_row = rows[k] * scale
-        for i in range(size):
+        for i in range(COLS):
             if i != k:
                 factor = rows[i][k : k + 1, :]
                 moved = rows[i] - factor * pivot_row
                 rows[i] = jnp.where(sub == k, factor * scale, moved)
         rows[k] = jnp.where(sub == k, -scale, pivot_row)
-        yield None
-    lane = lax.broadcasted_iota(jnp.int32, (size, LANES), 1)
-    out = jnp.zeros((size, LANES), jnp.float32)
-    for i in range(size):
-        out = jnp.where(lane == i, -rows[i], out)
-    yield out[:, :size]
+        yield rows
+
+
+def times(rows, right):
+    parts = [rows[i] * right[i : i + 1, :] for i in range(COLS)]
+    while len(parts) > 1:
+        parts = [a + b for a, b in zip(parts[::2], parts[1::2])]
+    return parts[0]
 
 
 def mixer(coeffs, count):
@@ -396,15 +408,19 @@
     own_x, own_y = v_ref.shape[0], v_ref.shape[1]
     m0, m1, m2, m3 = unpack_moments(g_ref[...])
     first = ((0,), (0,))
-    *_, inv = sweeps(m1)
-    alpha = dot(inv, m0)
-    m2a = dot(m2, alpha)
-    mix = dot(inv, m2a)
-    left = mixer(jnp.concatenate([mix, -alpha], axis=0), 3)
-    updated = dot(alpha, m2a, first) - m0
-    curved = dot(alpha, dot(m3, alpha), first) - dot(m2a, mix, first)
-    steps = sweeps(0.5 * (curved + curved.T))
-    inv = None
+    padding = jnp.zeros((COLS, LANES - COLS), jnp.float32)
+    *_, minus_inv = sweeps(replicated(m1))
+    minus_alpha = times(minus_inv, jnp.concatenate([m0, padding], axis=1))
+    minus_m2a = times(replicated(m2), minus_alpha)
+    mix = times(minus_inv, minus_m2a)[:, :COLS]
+    minus_m3a = times(replicated(m3), minus_alpha)[:, :COLS]
+    minus_alpha, minus_m2a = minus_alpha[:, :COLS], minus_m2a[:, :COLS]
+    alpha = -minus_alpha
+    left = mixer(jnp.concatenate([mix, minus_alpha], axis=0), 3)
+    updated = dot(minus_alpha, minus_m2a, first) - m0
+    curved = dot(minus_alpha, minus_m3a, first) + dot(minus_m2a, mix, first)
+    steps = sweeps(replicated(0.5 * (curved + curved.T)))
+    minus_inv = None
     for x in range(own_x):
         for y in range(own_y):
             q0, q1, qe = q_ref[x, y, :, :LANES], q_ref[x, y, :, LANES:], qe_ref[x, y]
@@ -421,9 +437,8 @@
             value = mixed(left, block, 3)
             d_ref[x, y] = value
             dlow_ref[x, y] = lowered(value)
-            if inv is None:
-                inv = next(steps)
-    gamma = dot(inv, updated)
+            minus_inv = next(steps, minus_inv)
+    gamma = -times(minus_inv, jnp.concatenate([updated, padding], axis=1))[:, :COLS]
     edge, main = (abovee_ref, belowe_ref, bothe_ref), (above_ref, below_ref, both_ref)
     whole = (w0_ref, w1_ref, w2_ref)
     for end_ref, main_ref, whole_ref in zip(edge, main, whole):
@@ -537,8 +552,6 @@
             pltpu.VMEM((ext_x, ext_y, COLS, size), f32),
             pltpu.VMEM((ext_x - 2, ext_y - 2, COLS, size), f32),
             pltpu.VMEM((ext_x, ext_y, size), f32),
-            pltpu.VMEM((6 * COLS, nodes * size), bf16),
-            pltpu.VMEM((12 * COLS, nodes * size), bf16),
         ]
 
     *main, total, edge, ids = pl.pallas_call(
@@ -550,7 +563,8 @@
             pltpu.VMEM((ext_x, ext_y, COLS, LANES), f32),
             pltpu.VMEM((ext_x, ext_y, LANES), f32),
         ),
-        scratch_shapes=scratch(wide),
+        scratch_shapes=scratch(wide)
+        + [pltpu.VMEM((6 * COLS, nodes * wide), bf16), pltpu.VMEM((9 * COLS, nodes * wide), bf16)],
         name="main",
     )(near(levels), near(flags), *flat)
     *edges, moments = pl.pallas_call(
@@ -561,7 +575,7 @@
     )(*[near(value) for value in (levels, total, edge, ids, before, after)])
     rows = 5
     length, chips = lax.axis_size("gz"), lax.axis_size("gy_0")
-    moments = spread(moments[:rows].reshape(rows, 1, LANES), "gz", 9 * length // 16)
+    moments = spread(moments[:rows].reshape(rows, 1, LANES), "gz", 17 * length // 32)
     middle = (lax.axis_size("gx") // 2 * chips + chips // 2) * 2 + 1
     moments = spread(moments, PLANE, middle).reshape(rows, LANES)
     moments = jnp.concatenate([moments, jnp.zeros((8 - rows, LANES), f32)], axis=0)

time: 85.1 us -> 84.2 us (0.989)
  no operation moved by 1% of the time
where the time goes in v6:
time: 84.2 us; the launch traced here: 84 us
  blocking collectives  46.8 us (56%)
  starting transfers between devices  20.4 us (24%)
  waiting for transfers between devices  8.82 us (10%)
  Pallas kernels  6.62 us (8%)
    all_to_all x2, blocking collectives, spread(): lax.all_to_all(copies, axes, 0, 0, axis_index_groups=[group])  46.8 us
    ppermute x3, starting transfers between devices, both_ways(): after = lax.ppermute(to_last, axis, [((i + 1) % count, i) for i in steps])  15.1 us
    ppermute x3, waiting for transfers between devices, both_ways(): after = lax.ppermute(to_last, axis, [((i + 1) % count, i) for i in steps])  6.45 us
    ppermute x3, starting transfers between devices, both_ways(): before = lax.ppermute(to_next, axis, [(i, (i + 1) % count) for i in steps])  5.32 us
    pallas_call x1, Pallas kernels, on_device(): pl.pallas_call(finish_kernel, out_shape=(out, out), scratch_shapes=[pltpu...  2.79 us
    ppermute x3, waiting for transfers between devices, both_ways(): before = lax.ppermute(to_next, axis, [(i, (i + 1) % count) for i in steps])  2.36 us
  transfers between devices with their start and end apart: 6, of which 5 were waited for; matrix products, arithmetic and copies ran while one was open for 0% of the time, Pallas kernels for 2%

profile of v6, /device:TPU:1, one launch (start us, length us, event | category | flops | bytes accessed | tf_op | source)
XLA Modules:
  0.0 84.0 jit_solution(10457910238970023169)
XLA Ops:
  0.6 0.9 %front.1 = (f32[2,17,2,4,128]{4,3,2,1,0:T(4,128)S(1)}, f32[8,128]{1,0:T(8,128)S(1)}) custom-call(f32[8]{0:T(128)} %moduli_ref.1, f32[16,2,4,256]{3,2,1,0:T(4,128)} %loads_ref.1, s32[2,4,256]{2,1,0:T(4,128)} %material_ref.1), custom_call_target="tpu_custom_call" | custom-call | tf_op jit(solution)/shard_map/front/pallas_call | solution.py:517
  1.6 4.0 %collective-permute-start = (f32[2,17,2,4,128]{4,3,2,1,0:T(4,128)S(1)}, f32[2,17,2,4,128]{4,3,2,1,0:T(4,128)S(1)}, u32[]{:S(2)}, u32[]{:S(2)}) collective-permute-start(f32[2,17,2,4,128]{4,3,2,1,0:T(4,128)S(1)} %get-tuple-element.21), channel_id=1, source_target_pairs={{0,256},{256,512},{512,768},{1,257},{257,513},{513,769},{2,258},{2... | collective-permute-start | bytes 417800 | tf_op jit(solution)/shard_map/ppermute | solution.py:497
  5.6 1.3 %collective-permute-start.1 = (f32[2,17,2,4,128]{4,3,2,1,0:T(4,128)S(1)}, f32[2,17,2,4,128]{4,3,2,1,0:T(4,128)S(1)}, u32[]{:S(2)}, u32[]{:S(2)}) collective-permute-start(f32[2,17,2,4,128]{4,3,2,1,0:T(4,128)S(1)} %get-tuple-element.21), channel_id=1, source_target_pairs={{256,0},{512,256},{768,512},{257,1},{513,257},{769,513},{258,2},{5... | collective-permute-start | bytes 417800 | tf_op jit(solution)/shard_map/ppermute | solution.py:498
  6.9 0.7 collective-permute-done
  7.7 3.8 %collective-permute-done.1 = f32[2,17,2,4,128]{4,3,2,1,0:T(4,128)S(1)} collective-permute-done((f32[2,17,2,4,128]{4,3,2,1,0:T(4,128)S(1)}, f32[2,17,2,4,128]{4,3,2,1,0:T(4,128)S(1)}, u32[]{:S(2)}, u32[]{:S(2)}) %collective-permute-start.1) | collective-permute-done | bytes 139296 | tf_op jit(solution)/shard_map/ppermute | solution.py:498
  11.4 0.2 fusion
  11.6 12.5 %collective-permute-start.3 = (f32[2,17,6,2,128]{4,3,2,1,0:T(2,128)S(1)}, f32[2,17,6,2,128]{4,3,2,1,0:T(2,128)S(1)}, u32[]{:S(2)}, u32[]{:S(2)}) collective-permute-start(f32[2,17,6,2,128]{4,3,2,1,0:T(2,128)S(1)} %get-tuple-element.38), channel_id=1, source_target_pairs={{32,0},{64,32},{96,64},{128,96},{160,128},{192,160},{224,192},{0,2... | collective-permute-start | bytes 626696 | tf_op jit(solution)/shard_map/ppermute | solution.py:498
  24.2 0.0 collective-permute-start.2
  24.2 1.1 %collective-permute-done.3 = f32[2,17,6,2,128]{4,3,2,1,0:T(2,128)S(1)} collective-permute-done((f32[2,17,6,2,128]{4,3,2,1,0:T(2,128)S(1)}, f32[2,17,6,2,128]{4,3,2,1,0:T(2,128)S(1)}, u32[]{:S(2)}, u32[]{:S(2)}) %collective-permute-start.3) | collective-permute-done | bytes 208928 | tf_op jit(solution)/shard_map/ppermute | solution.py:498
  25.2 1.7 %collective-permute-done.2 = f32[2,17,6,2,128]{4,3,2,1,0:T(2,128)S(1)} collective-permute-done((f32[2,17,6,2,128]{4,3,2,1,0:T(2,128)S(1)}, f32[2,17,6,2,128]{4,3,2,1,0:T(2,128)S(1)}, u32[]{:S(2)}, u32[]{:S(2)}) %collective-permute-start.2) | collective-permute-done | bytes 208928 | tf_op jit(solution)/shard_map/ppermute | solution.py:497
  26.9 0.1 iota.7.flags_ref
  27.0 0.4 pack.1
  27.4 1.3 %collective-permute-start.4 = (f32[24,128]{1,0:T(8,128)S(1)}, f32[24,128]{1,0:T(8,128)S(1)}, u32[]{:S(2)}, u32[]{:S(2)}) collective-permute-start(f32[24,128]{1,0:T(8,128)S(1)} %get-tuple-element.25), channel_id=1, source_target_pairs={{0,1},{1,2},{2,3},{3,4},{4,5},{5,6},{6,7},{7,8},{8,9},{9,10},{10,1... | collective-permute-start | bytes 36872 | tf_op jit(solution)/shard_map/ppermute | solution.py:497
  28.6 1.3 %collective-permute-start.5 = (f32[24,128]{1,0:T(8,128)S(1)}, f32[24,128]{1,0:T(8,128)S(1)}, u32[]{:S(2)}, u32[]{:S(2)}) collective-permute-start(f32[24,128]{1,0:T(8,128)S(1)} %get-tuple-element.26), channel_id=1, source_target_pairs={{1,0},{2,1},{3,2},{4,3},{5,4},{6,5},{7,6},{8,7},{9,8},{10,9},{11,1... | collective-permute-start | bytes 36872 | tf_op jit(solution)/shard_map/ppermute | solution.py:498
  29.9 1.5 %main.1 = (f32[4,6,16,256]{3,2,1,0:T(8,128)S(1)}, f32[4,6,16,256]{3,2,1,0:T(8,128)S(1)}, f32[5,8,256]{2,1,0:T(8,128)S(1)}, f32[5,8,256]{2,1,0:T(8,128)S(1)}, f32...) custom-call(f32[8,128]{1,0:T(8,128)S(1)} %get-tuple-element.20.levels_r, ...), custom_call_target="tpu_custom_call" | custom-call | tf_op jit(solution)/shard_map/main/pallas_call | solution.py:557
  31.5 0.0 collective-permute-done.4.before_ref
  31.5 1.6 %collective-permute-done.5.after_ref = f32[24,128]{1,0:T(8,128)S(1)} collective-permute-done((f32[24,128]{1,0:T(8,128)S(1)}, f32[24,128]{1,0:T(8,128)S(1)}, u32[]{:S(2)}, u32[]{:S(2)}) %collective-permute-start.5) | collective-permute-done | bytes 12320 | tf_op jit(solution)/shard_map/ppermute | solution.py:498
  33.1 1.0 %edge.1 = (f32[4,6,16,128]{3,2,1,0:T(8,128)S(1)}, f32[4,6,16,128]{3,2,1,0:T(8,128)S(1)}, f32[5,8,128]{2,1,0:T(8,128)S(1)}, f32[5,8,128]{2,1,0:T(8,128)S(1)}, f32...) custom-call(f32[8,128]{1,0:T(8,128)S(1)} %get-tuple-element.20.levels_ref, f32[32,128]{1,0:T(8,128)S(1)} %get-tuple-element.22.total_ref, ...), custom_call_target="tpu_custom_call" | custom-call | tf_op jit(solution)/shard_map/edge/pallas_call | solution.py:570
  34.1 0.1 broadcast_in_dim.22
  34.2 33.0 %all_to_all.10 = f32[32,5,1,128]{3,2,1,0:T(1,128)S(1)} all-to-all(f32[32,5,1,128]{3,2,1,0:T(1,128)S(1)} %broadcast_in_dim.22), channel_id=1, replica_groups={{17,18,19,20,21,22,23,24,25,26,27,28,29,30,31,0,1,2,3,4,5,6,7,8,9,10,11..., dimensions={0} | all-to-all | bytes 163840 | tf_op jit(solution)/shard_map/all_to_all | solution.py:506
  67.2 0.1 reduce_sum.18
  67.3 13.8 %all_to_all.11 = f32[32,5,1,128]{3,2,1,0:T(1,128)S(1)} all-to-all(f32[32,5,1,128]{3,2,1,0:T(1,128)S(1)} %broadcast_in_dim.23), channel_id=1, replica_groups={{672,704,736,768,800,832,864,896,928,960,992,0,32,64,96,128,160,192,224..., dimensions={0} | all-to-all | bytes 163840 | tf_op jit(solution)/shard_map/all_to_all | solution.py:506
  81.1 0.1 reduce_sum.19
  81.2 2.8 %finish.1 = (f32[16,2,4,256]{3,2,1,0:T(4,128)}, f32[16,2,4,256]{3,2,1,0:T(4,128)}) custom-call(f32[8,128]{1,0:T(8,128)S(1)} %concatenate.7.g_ref, f32[4,6,16,256]{3,2,1,0:T(8,128)S(1)} %get-tuple-element.28.v_ref, f32[4,6,16,256]{3,2,1,0:T(8,128)S(1)} %get-tuple-element.29.q_ref, f32[5,8,256]{2,1,0:T(8,128)S(1)} %get-tuple-element.30.above_ref, ...), custom_call_target="tpu_custom_call" | custom-call | tf_op jit(solution)/shard_map/finish/pallas_call | solution.py:583
  (6 shorter events, 0.1 us)
Async XLA Ops:
  1.6 6.0 %collective-permute-start = (f32[2,17,2,4,128]{4,3,2,1,0:T(4,128)S(1)}, f32[2,17,2,4,128]{4,3,2,1,0:T(4,128)S(1)}, u32[]{:S(2)}, u32[]{:S(2)}) collective-permute-start(f32[2,17,2,4,128]{4,3,2,1,0:T(4,128)S(1)} %get-tuple-element.21), channel_id=1, source_target_pairs={{0,256},{256,512},{512,768},{1,257},{257,513},{513,769},{2,258},{2... | collective-permute-start | bytes 417800 | tf_op jit(solution)/shard_map/ppermute | solution.py:497
  5.6 5.8 %collective-permute-start.1 = (f32[2,17,2,4,128]{4,3,2,1,0:T(4,128)S(1)}, f32[2,17,2,4,128]{4,3,2,1,0:T(4,128)S(1)}, u32[]{:S(2)}, u32[]{:S(2)}) collective-permute-start(f32[2,17,2,4,128]{4,3,2,1,0:T(4,128)S(1)} %get-tuple-element.21), channel_id=1, source_target_pairs={{256,0},{512,256},{768,512},{257,1},{513,257},{769,513},{258,2},{5... | collective-permute-start | bytes 417800 | tf_op jit(solution)/shard_map/ppermute | solution.py:498
  11.6 13.6 %collective-permute-start.3 = (f32[2,17,6,2,128]{4,3,2,1,0:T(2,128)S(1)}, f32[2,17,6,2,128]{4,3,2,1,0:T(2,128)S(1)}, u32[]{:S(2)}, u32[]{:S(2)}) collective-permute-start(f32[2,17,6,2,128]{4,3,2,1,0:T(2,128)S(1)} %get-tuple-element.38), channel_id=1, source_target_pairs={{32,0},{64,32},{96,64},{128,96},{160,128},{192,160},{224,192},{0,2... | collective-permute-start | bytes 626696 | tf_op jit(solution)/shard_map/ppermute | solution.py:498
  24.2 2.7 %collective-permute-start.2 = (f32[2,17,6,2,128]{4,3,2,1,0:T(2,128)S(1)}, f32[2,17,6,2,128]{4,3,2,1,0:T(2,128)S(1)}, u32[]{:S(2)}, u32[]{:S(2)}) collective-permute-start(f32[2,17,6,2,128]{4,3,2,1,0:T(2,128)S(1)} %get-tuple-element.39), channel_id=1, source_target_pairs={{0,32},{32,64},{64,96},{96,128},{128,160},{160,192},{192,224},{224... | collective-permute-start | bytes 626696 | tf_op jit(solution)/shard_map/ppermute | solution.py:497
  27.4 4.1 %collective-permute-start.4 = (f32[24,128]{1,0:T(8,128)S(1)}, f32[24,128]{1,0:T(8,128)S(1)}, u32[]{:S(2)}, u32[]{:S(2)}) collective-permute-start(f32[24,128]{1,0:T(8,128)S(1)} %get-tuple-element.25), channel_id=1, source_target_pairs={{0,1},{1,2},{2,3},{3,4},{4,5},{5,6},{6,7},{7,8},{8,9},{9,10},{10,1... | collective-permute-start | bytes 36872 | tf_op jit(solution)/shard_map/ppermute | solution.py:497
  28.6 4.4 %collective-permute-start.5 = (f32[24,128]{1,0:T(8,128)S(1)}, f32[24,128]{1,0:T(8,128)S(1)}, u32[]{:S(2)}, u32[]{:S(2)}) collective-permute-start(f32[24,128]{1,0:T(8,128)S(1)} %get-tuple-element.26), channel_id=1, source_target_pairs={{1,0},{2,1},{3,2},{4,3},{5,4},{6,5},{7,6},{8,7},{9,8},{10,9},{11,1... | collective-permute-start | bytes 36872 | tf_op jit(solution)/shard_map/ppermute | solution.py:498

commit v7 on v6

--- a/solution.py
+++ b/solution.py
@@ -116,15 +116,19 @@
 
 
 def rows_of(refs, flags_ref, tile, x, y, first, count):
-    before_ref, mid_ref, after_ref, ext_x = refs
-    if y < 2:
-        ref, wide, at, flag = before_ref, 2, y, 0
-    elif y < 6:
-        ref, wide, at, flag = mid_ref, 4, y - 2, None
+    before_x_ref, own_ref, after_x_ref, before_ref, before_last_ref, after_ref, after_last_ref = refs
+    flag = None
+    if 2 <= y < 6:
+        ref, column, wide, tall, at = (before_x_ref, own_ref, after_x_ref)[x // 2], x % 2, 2, 4, y - 2
     else:
-        ref, wide, at, flag = after_ref, 2, y - 6, 1
-    stride = ext_x * wide
-    start = tile * (ref.shape[0] // 2) + first * stride + x * wide + at
+        low = y < 2
+        flag, at, tall = (0, y, 2) if low else (1, y - 6, 2)
+        if x < 4:
+            ref, column, wide = before_ref if low else after_ref, x, 4
+        else:
+            ref, column, wide = before_last_ref if low else after_last_ref, x - 4, 2
+    stride = wide * tall
+    start = tile * (ref.shape[0] // 2) + first * stride + column * tall + at
     value = ref[pl.ds(start, count, stride=stride), :] if count > 1 else ref[start : start + 1, :]
     if flag is not None:
         value = jnp.where(flags_ref[flag : flag + 1, :] > 0.0, value, 0.0)
@@ -139,8 +143,8 @@
         levels_ref[level : level + 1, :] = jnp.full((1, LANES), moduli_ref[level], jnp.float32)
 
 
-def pack_kernel(flags_ref, before_ref, mid_ref, after_ref, lo_ref, hi_ref, ext_x, ext_y):
-    refs = (before_ref, mid_ref, after_ref, ext_x)
+def pack_kernel(flags_ref, *refs, ext_x, ext_y):
+    *refs, lo_ref, hi_ref = refs
     for tile, out_ref in ((0, lo_ref), (1, hi_ref)):
         offset = 2 * tile
         lane = lax.broadcasted_iota(jnp.int32, (COLS, LANES), 1)
@@ -230,12 +234,12 @@
 
 
 def main_kernel(
-    levels_ref, flags_ref, before_ref, mid_ref, after_ref,
+    levels_ref, flags_ref, a_ref, b_ref, c_ref, d_ref, e0_ref, f_ref, g_ref,
     v_ref, q_ref, above_ref, below_ref, both_ref, total_ref, ve_ref, ie_ref,
     low_ref, qlow_ref, e_ref, left_ref, right_ref,
 ):
     ext_x, ext_y = low_ref.shape[0], low_ref.shape[1]
-    refs = (before_ref, mid_ref, after_ref, ext_x)
+    refs = (a_ref, b_ref, c_ref, d_ref, e0_ref, f_ref, g_ref)
     for x in range(ext_x):
         for y in range(ext_y):
             tiles = [rows_of(refs, flags_ref, t, x, y, COLS, 1) for t in range(2)]
@@ -531,9 +535,11 @@
     row = lax.broadcasted_iota(jnp.int32, (8, LANES), 0)
     flags = jnp.where(row == 0, place > 0, place < lax.axis_size(GY) - 1).astype(f32)
     before, after = both_ways("gx", own, own)
-    mid = jnp.concatenate([before, own, after], axis=2)
-    before, after = both_ways(GY, mid[:, :, :, 2:], mid[:, :, :, :2], around=True)
-    flat = [near(part.reshape(-1, LANES)) for part in (before, mid, after)]
+    part = jnp.concatenate([before, own], axis=2)
+    parts = part[:, :, :, 2:], part[:, :, :, :2]
+    sides = both_ways(GY, *parts, around=True)
+    lasts = both_ways(GY, after[:, :, :, 2:], after[:, :, :, :2], around=True)
+    flat = [near(v.reshape(-1, LANES)) for v in (before, own, after, sides[0], lasts[0], sides[1], lasts[1])]
     ends = pltpu.VMEM((COLS + 8, LANES), f32)
     first, last = pl.pallas_call(
         functools.partial(pack_kernel, ext_x=ext_x, ext_y=ext_y), out_shape=(ends, ends), name="pack"
@@ -590,9 +596,10 @@
 
 
 def solution(mesh):
-    wide, long = mesh.shape["gy"] // 2, mesh.shape["gz"]
-    split = Mesh(mesh.devices.reshape(mesh.shape["gx"], wide, 2, long), ("gx", "gy_0", "gy_1", "gz"))
+    chips, long = mesh.shape["gy"] // 2, mesh.shape["gz"]
+    split = Mesh(mesh.devices.reshape(mesh.shape["gx"], chips, 2, long), ("gx", "gy_0", "gy_1", "gz"))
     spec = P(None, "gx", GY, "gz")
+
     return jax.shard_map(
         on_device,
         mesh=split,

time: 84.2 us -> 84 us (level)
  waiting for transfers between devices: 8.82 us -> 3.66 us
  starting transfers between devices: 20.4 us -> 24.1 us
  blocking collectives: 46.8 us -> 48 us
    ppermute x3 -> x4, waiting for transfers between devices: 6.45 us -> 2.5 us  [both_ways(): after = lax.ppermute(to_last, axis, [((i + 1) % count, i) for i in steps])]
    ppermute x3 -> x4, starting transfers between devices: 15.1 us -> 18.8 us  [both_ways(): after = lax.ppermute(to_last, axis, [((i + 1) % count, i) for i in steps])]
    all_to_all x2, blocking collectives: 46.8 us -> 48 us  [spread(): lax.all_to_all(copies, axes, 0, 0, axis_index_groups=[group])]
    ppermute x3 -> x4, waiting for transfers between devices: 2.36 us -> 1.16 us  [both_ways(): before = lax.ppermute(to_next, axis, [(i, (i + 1) % count) for i in steps])]
    ppermute x3 -> x4, starting transfers between devices: 5.32 us -> 5.32 us  [both_ways(): before = lax.ppermute(to_next, axis, [(i, (i + 1) % count) for i in steps])]
  transfers between devices with their start and end apart: 6 -> 8, of which waited for: 5 -> 4; matrix products, arithmetic and copies ran while one was open for 0% -> 0% of each run, Pallas kernels for 2% -> 2%
where the time goes in v7:
time: 84 us; the launch traced here: 83.7 us
  blocking collectives  48 us (57%)
  starting transfers between devices  24.1 us (29%)
  Pallas kernels  6.64 us (8%)
  waiting for transfers between devices  3.66 us (4%)
    all_to_all x2, blocking collectives, spread(): lax.all_to_all(copies, axes, 0, 0, axis_index_groups=[group])  48 us
    ppermute x4, starting transfers between devices, both_ways(): after = lax.ppermute(to_last, axis, [((i + 1) % count, i) for i in steps])  18.8 us
    ppermute x4, starting transfers between devices, both_ways(): before = lax.ppermute(to_next, axis, [(i, (i + 1) % count) for i in steps])  5.32 us
    pallas_call x1, Pallas kernels, on_device(): pl.pallas_call(finish_kernel, out_shape=(out, out), scratch_shapes=[pltpu...  2.79 us
    ppermute x4, waiting for transfers between devices, both_ways(): after = lax.ppermute(to_last, axis, [((i + 1) % count, i) for i in steps])  2.5 us
  transfers between devices with their start and end apart: 8, of which 4 were waited for; matrix products, arithmetic and copies ran while one was open for 0% of the time, Pallas kernels for 2%

profile of v7, /device:TPU:1, one launch (start us, length us, event | category | flops | bytes accessed | tf_op | source)
XLA Modules:
  0.0 83.7 jit_solution(10167532907835989471)
XLA Ops:
  0.6 0.9 %front.1 = (f32[2,17,2,4,128]{4,3,2,1,0:T(4,128)S(1)}, f32[8,128]{1,0:T(8,128)S(1)}) custom-call(f32[8]{0:T(128)} %moduli_ref.1, f32[16,2,4,256]{3,2,1,0:T(4,128)} %loads_ref.1, s32[2,4,256]{2,1,0:T(4,128)} %material_ref.1), custom_call_target="tpu_custom_call" | custom-call | tf_op jit(solution)/shard_map/front/pallas_call | solution.py:521
  1.6 4.0 %collective-permute-start = (f32[2,17,2,4,128]{4,3,2,1,0:T(4,128)S(1)}, f32[2,17,2,4,128]{4,3,2,1,0:T(4,128)S(1)}, u32[]{:S(2)}, u32[]{:S(2)}) collective-permute-start(f32[2,17,2,4,128]{4,3,2,1,0:T(4,128)S(1)} %get-tuple-element.21), channel_id=1, source_target_pairs={{0,256},{256,512},{512,768},{1,257},{257,513},{513,769},{2,258},{2... | collective-permute-start | bytes 417800 | tf_op jit(solution)/shard_map/ppermute | solution.py:501
  5.6 1.3 %collective-permute-start.1 = (f32[2,17,2,4,128]{4,3,2,1,0:T(4,128)S(1)}, f32[2,17,2,4,128]{4,3,2,1,0:T(4,128)S(1)}, u32[]{:S(2)}, u32[]{:S(2)}) collective-permute-start(f32[2,17,2,4,128]{4,3,2,1,0:T(4,128)S(1)} %get-tuple-element.21), channel_id=1, source_target_pairs={{256,0},{512,256},{768,512},{257,1},{513,257},{769,513},{258,2},{5... | collective-permute-start | bytes 417800 | tf_op jit(solution)/shard_map/ppermute | solution.py:502
  6.9 0.7 collective-permute-done
  7.7 0.1 fusion
  7.8 12.0 %collective-permute-start.4 = (f32[2,17,4,2,128]{4,3,2,1,0:T(2,128)S(1)}, f32[2,17,4,2,128]{4,3,2,1,0:T(2,128)S(1)}, u32[]{:S(2)}, u32[]{:S(2)}) collective-permute-start(f32[2,17,4,2,128]{4,3,2,1,0:T(2,128)S(1)} %get-tuple-element.38), channel_id=1, source_target_pairs={{32,0},{64,32},{96,64},{128,96},{160,128},{192,160},{224,192},{0,2... | collective-permute-start | bytes 417800 | tf_op jit(solution)/shard_map/ppermute | solution.py:502
  19.7 0.0 collective-permute-start.2
  19.7 0.0 collective-permute-done.1
  19.8 0.1 fusion.1
  19.8 4.2 %collective-permute-start.5 = (f32[2,17,2,2,128]{4,3,2,1,0:T(2,128)S(1)}, f32[2,17,2,2,128]{4,3,2,1,0:T(2,128)S(1)}, u32[]{:S(2)}, u32[]{:S(2)}) collective-permute-start(f32[2,17,2,2,128]{4,3,2,1,0:T(2,128)S(1)} %get-tuple-element.40), channel_id=1, source_target_pairs={{32,0},{64,32},{96,64},{128,96},{160,128},{192,160},{224,192},{0,2... | collective-permute-start | bytes 208904 | tf_op jit(solution)/shard_map/ppermute | solution.py:502
  24.0 0.0 collective-permute-start.3
  24.0 0.9 %collective-permute-done.5 = f32[2,17,2,2,128]{4,3,2,1,0:T(2,128)S(1)} collective-permute-done((f32[2,17,2,2,128]{4,3,2,1,0:T(2,128)S(1)}, f32[2,17,2,2,128]{4,3,2,1,0:T(2,128)S(1)}, u32[]{:S(2)}, u32[]{:S(2)}) %collective-permute-start.5) | collective-permute-done | bytes 69664 | tf_op jit(solution)/shard_map/ppermute | solution.py:502
  24.9 0.5 collective-permute-done.3
  25.4 0.0 collective-permute-done.4
  25.4 0.0 collective-permute-done.2
  25.4 0.1 iota.7.flags_ref
  25.5 0.4 pack.1
  25.8 1.3 %collective-permute-start.6 = (f32[24,128]{1,0:T(8,128)S(1)}, f32[24,128]{1,0:T(8,128)S(1)}, u32[]{:S(2)}, u32[]{:S(2)}) collective-permute-start(f32[24,128]{1,0:T(8,128)S(1)} %get-tuple-element.25), channel_id=1, source_target_pairs={{0,1},{1,2},{2,3},{3,4},{4,5},{5,6},{6,7},{7,8},{8,9},{9,10},{10,1... | collective-permute-start | bytes 36872 | tf_op jit(solution)/shard_map/ppermute | solution.py:501
  27.1 1.3 %collective-permute-start.7 = (f32[24,128]{1,0:T(8,128)S(1)}, f32[24,128]{1,0:T(8,128)S(1)}, u32[]{:S(2)}, u32[]{:S(2)}) collective-permute-start(f32[24,128]{1,0:T(8,128)S(1)} %get-tuple-element.26), channel_id=1, source_target_pairs={{1,0},{2,1},{3,2},{4,3},{5,4},{6,5},{7,6},{8,7},{9,8},{10,9},{11,1... | collective-permute-start | bytes 36872 | tf_op jit(solution)/shard_map/ppermute | solution.py:502
  28.4 1.5 %main.1 = (f32[4,6,16,256]{3,2,1,0:T(8,128)S(1)}, f32[4,6,16,256]{3,2,1,0:T(8,128)S(1)}, f32[5,8,256]{2,1,0:T(8,128)S(1)}, f32[5,8,256]{2,1,0:T(8,128)S(1)}, f32...) custom-call(f32[8,128]{1,0:T(8,128)S(1)} %get-tuple-element.20.levels_r, ...), custom_call_target="tpu_custom_call" | custom-call | tf_op jit(solution)/shard_map/main/pallas_call | solution.py:563
  30.0 0.0 collective-permute-done.6.before_ref
  30.0 1.6 %collective-permute-done.7.after_ref = f32[24,128]{1,0:T(8,128)S(1)} collective-permute-done((f32[24,128]{1,0:T(8,128)S(1)}, f32[24,128]{1,0:T(8,128)S(1)}, u32[]{:S(2)}, u32[]{:S(2)}) %collective-permute-start.7) | collective-permute-done | bytes 12320 | tf_op jit(solution)/shard_map/ppermute | solution.py:502
  31.6 1.0 %edge.1 = (f32[4,6,16,128]{3,2,1,0:T(8,128)S(1)}, f32[4,6,16,128]{3,2,1,0:T(8,128)S(1)}, f32[5,8,128]{2,1,0:T(8,128)S(1)}, f32[5,8,128]{2,1,0:T(8,128)S(1)}, f32...) custom-call(f32[8,128]{1,0:T(8,128)S(1)} %get-tuple-element.20.levels_ref, f32[32,128]{1,0:T(8,128)S(1)} %get-tuple-element.22.total_ref, ...), custom_call_target="tpu_custom_call" | custom-call | tf_op jit(solution)/shard_map/edge/pallas_call | solution.py:576
  32.6 0.1 broadcast_in_dim.22
  32.7 32.6 %all_to_all.10 = f32[32,5,1,128]{3,2,1,0:T(1,128)S(1)} all-to-all(f32[32,5,1,128]{3,2,1,0:T(1,128)S(1)} %broadcast_in_dim.22), channel_id=1, replica_groups={{17,18,19,20,21,22,23,24,25,26,27,28,29,30,31,0,1,2,3,4,5,6,7,8,9,10,11..., dimensions={0} | all-to-all | bytes 163840 | tf_op jit(solution)/shard_map/all_to_all | solution.py:510
  65.3 0.1 reduce_sum.18
  65.4 15.4 %all_to_all.11 = f32[32,5,1,128]{3,2,1,0:T(1,128)S(1)} all-to-all(f32[32,5,1,128]{3,2,1,0:T(1,128)S(1)} %broadcast_in_dim.23), channel_id=1, replica_groups={{672,704,736,768,800,832,864,896,928,960,992,0,32,64,96,128,160,192,224..., dimensions={0} | all-to-all | bytes 163840 | tf_op jit(solution)/shard_map/all_to_all | solution.py:510
  80.8 0.1 reduce_sum.19
  80.9 2.8 %finish.1 = (f32[16,2,4,256]{3,2,1,0:T(4,128)}, f32[16,2,4,256]{3,2,1,0:T(4,128)}) custom-call(f32[8,128]{1,0:T(8,128)S(1)} %concatenate.7.g_ref, f32[4,6,16,256]{3,2,1,0:T(8,128)S(1)} %get-tuple-element.28.v_ref, f32[4,6,16,256]{3,2,1,0:T(8,128)S(1)} %get-tuple-element.29.q_ref, f32[5,8,256]{2,1,0:T(8,128)S(1)} %get-tuple-element.30.above_ref, ...), custom_call_target="tpu_custom_call" | custom-call | tf_op jit(solution)/shard_map/finish/pallas_call | solution.py:589
  (5 shorter events, 0.1 us)
Async XLA Ops:
  1.6 6.0 %collective-permute-start = (f32[2,17,2,4,128]{4,3,2,1,0:T(4,128)S(1)}, f32[2,17,2,4,128]{4,3,2,1,0:T(4,128)S(1)}, u32[]{:S(2)}, u32[]{:S(2)}) collective-permute-start(f32[2,17,2,4,128]{4,3,2,1,0:T(4,128)S(1)} %get-tuple-element.21), channel_id=1, source_target_pairs={{0,256},{256,512},{512,768},{1,257},{257,513},{513,769},{2,258},{2... | collective-permute-start | bytes 417800 | tf_op jit(solution)/shard_map/ppermute | solution.py:501
  5.6 14.1 %collective-permute-start.1 = (f32[2,17,2,4,128]{4,3,2,1,0:T(4,128)S(1)}, f32[2,17,2,4,128]{4,3,2,1,0:T(4,128)S(1)}, u32[]{:S(2)}, u32[]{:S(2)}) collective-permute-start(f32[2,17,2,4,128]{4,3,2,1,0:T(4,128)S(1)} %get-tuple-element.21), channel_id=1, source_target_pairs={{256,0},{512,256},{768,512},{257,1},{513,257},{769,513},{258,2},{5... | collective-permute-start | bytes 417800 | tf_op jit(solution)/shard_map/ppermute | solution.py:502
  7.8 17.6 %collective-permute-start.4 = (f32[2,17,4,2,128]{4,3,2,1,0:T(2,128)S(1)}, f32[2,17,4,2,128]{4,3,2,1,0:T(2,128)S(1)}, u32[]{:S(2)}, u32[]{:S(2)}) collective-permute-start(f32[2,17,4,2,128]{4,3,2,1,0:T(2,128)S(1)} %get-tuple-element.38), channel_id=1, source_target_pairs={{32,0},{64,32},{96,64},{128,96},{160,128},{192,160},{224,192},{0,2... | collective-permute-start | bytes 417800 | tf_op jit(solution)/shard_map/ppermute | solution.py:502
  19.7 5.7 %collective-permute-start.2 = (f32[2,17,4,2,128]{4,3,2,1,0:T(2,128)S(1)}, f32[2,17,4,2,128]{4,3,2,1,0:T(2,128)S(1)}, u32[]{:S(2)}, u32[]{:S(2)}) collective-permute-start(f32[2,17,4,2,128]{4,3,2,1,0:T(2,128)S(1)} %get-tuple-element.39), channel_id=1, source_target_pairs={{0,32},{32,64},{64,96},{96,128},{128,160},{160,192},{192,224},{224... | collective-permute-start | bytes 417800 | tf_op jit(solution)/shard_map/ppermute | solution.py:501
  19.8 5.1 %collective-permute-start.5 = (f32[2,17,2,2,128]{4,3,2,1,0:T(2,128)S(1)}, f32[2,17,2,2,128]{4,3,2,1,0:T(2,128)S(1)}, u32[]{:S(2)}, u32[]{:S(2)}) collective-permute-start(f32[2,17,2,2,128]{4,3,2,1,0:T(2,128)S(1)} %get-tuple-element.40), channel_id=1, source_target_pairs={{32,0},{64,32},{96,64},{128,96},{160,128},{192,160},{224,192},{0,2... | collective-permute-start | bytes 208904 | tf_op jit(solution)/shard_map/ppermute | solution.py:502
  24.0 1.4 %collective-permute-start.3 = (f32[2,17,2,2,128]{4,3,2,1,0:T(2,128)S(1)}, f32[2,17,2,2,128]{4,3,2,1,0:T(2,128)S(1)}, u32[]{:S(2)}, u32[]{:S(2)}) collective-permute-start(f32[2,17,2,2,128]{4,3,2,1,0:T(2,128)S(1)} %get-tuple-element.41), channel_id=1, source_target_pairs={{0,32},{32,64},{64,96},{96,128},{128,160},{160,192},{192,224},{224... | collective-permute-start | bytes 208904 | tf_op jit(solution)/shard_map/ppermute | solution.py:501
  25.8 4.1 %collective-permute-start.6 = (f32[24,128]{1,0:T(8,128)S(1)}, f32[24,128]{1,0:T(8,128)S(1)}, u32[]{:S(2)}, u32[]{:S(2)}) collective-permute-start(f32[24,128]{1,0:T(8,128)S(1)} %get-tuple-element.25), channel_id=1, source_target_pairs={{0,1},{1,2},{2,3},{3,4},{4,5},{5,6},{6,7},{7,8},{8,9},{9,10},{10,1... | collective-permute-start | bytes 36872 | tf_op jit(solution)/shard_map/ppermute | solution.py:501
  27.1 4.4 %collective-permute-start.7 = (f32[24,128]{1,0:T(8,128)S(1)}, f32[24,128]{1,0:T(8,128)S(1)}, u32[]{:S(2)}, u32[]{:S(2)}) collective-permute-start(f32[24,128]{1,0:T(8,128)S(1)} %get-tuple-element.26), channel_id=1, source_target_pairs={{1,0},{2,1},{3,2},{4,3},{5,4},{6,5},{7,6},{8,7},{9,8},{10,9},{11,1... | collective-permute-start | bytes 36872 | tf_op jit(solution)/shard_map/ppermute | solution.py:502

commit v8 on v7

--- a/solution.py
+++ b/solution.py
@@ -16,6 +16,7 @@
 LANES = 128
 EDGE = LANES // 4
 HIGH = lax.Precision.HIGHEST
+GRANT = pltpu.CompilerParams(vmem_limit_bytes=16 * 2**20)
 
 
 def stiffness_table():
@@ -57,6 +58,10 @@
     return value.astype(jnp.bfloat16).astype(jnp.float32)
 
 
+MIDDLE = (2, 3, 4, 5)
+OUTER = (0, 1, 6, 7)
+
+
 def tile_of(tile):
     return slice(tile * LANES, (tile + 1) * LANES)
 
@@ -143,23 +148,27 @@
         levels_ref[level : level + 1, :] = jnp.full((1, LANES), moduli_ref[level], jnp.float32)
 
 
-def pack_kernel(flags_ref, *refs, ext_x, ext_y):
-    *refs, lo_ref, hi_ref = refs
-    for tile, out_ref in ((0, lo_ref), (1, hi_ref)):
+def pack_rows(starts, out_refs, refs, flags_ref, ext_x, ext_y, ys):
+    for tile, (start_ref, out_ref) in enumerate(zip(starts, out_refs)):
         offset = 2 * tile
         lane = lax.broadcasted_iota(jnp.int32, (COLS, LANES), 1)
-        packed = jnp.zeros((COLS, LANES), jnp.float32)
-        ids = [jnp.zeros((1, LANES), jnp.float32)] * ext_y
-        for x in range(ext_x):
-            for y in range(ext_y):
+        packed = jnp.zeros((COLS, LANES), jnp.float32) if start_ref is None else start_ref[:COLS, :]
+        for y in range(ext_y):
+            row = slice(COLS + y, COLS + y + 1)
+            ids = jnp.zeros((1, LANES), jnp.float32) if start_ref is None else start_ref[row, :]
+            for x in range(ext_x) if y in ys else ():
                 node = x * ext_y + y
                 value = rows_of(refs, flags_ref, tile, x, y, 0, COLS)
                 packed = jnp.where(lane // 2 == node, turn(value, 2 * node + offset), packed)
                 value = rows_of(refs, flags_ref, tile, x, y, COLS, 1)
-                ids[y] = jnp.where(lane[:1] // 2 == x, turn(value, 2 * x + offset), ids[y])
+                ids = jnp.where(lane[:1] // 2 == x, turn(value, 2 * x + offset), ids)
+            out_ref[row, :] = ids
         out_ref[:COLS, :] = packed
-        for y in range(ext_y):
-            out_ref[COLS + y : COLS + y + 1, :] = ids[y]
+
+
+def pack_kernel(flags_ref, a_ref, b_ref, c_ref, d_ref, lo0_ref, hi0_ref, lo_ref, hi_ref, ext_x, ext_y):
+    refs = (None, None, None, a_ref, b_ref, c_ref, d_ref)
+    pack_rows((lo0_ref, hi0_ref), (lo_ref, hi_ref), refs, flags_ref, ext_x, ext_y, OUTER)
 
 
 def modulus_of(levels_ref, ids):
@@ -189,10 +198,10 @@
     return tuple(lambda ex, ey, t, ref=ref: ref[ex, ey : ey + 1, tile_of(t)] for ref in refs)
 
 
-def first_image(v_ref, low_ref, e_ref, sides, q_ref, qlow_ref, count):
+def first_image(v_ref, low_ref, e_ref, sides, q_ref, qlow_ref, count, ys):
     ext_x, ext_y = low_ref.shape[0], low_ref.shape[1]
     for x in range(1, ext_x - 1):
-        for y in range(1, ext_y - 1):
+        for y in ys:
             image = operator(
                 lambda t: v_ref[x - 1, y - 1, :, tile_of(t)],
                 lambda i, j, t: low_ref[i, j, :, tile_of(t)],
@@ -233,36 +242,92 @@
     return first + turn(first, -3 * COLS) + third
 
 
+def edge_of(tiles):
+    lane = lanes_of(tiles[0])
+    return jnp.where(lane < EDGE, tiles[0], jnp.where(lane < 2 * EDGE, turn(tiles[1], 2 * EDGE), 0.0))
+
+
+def middle_kernel(
+    levels_ref, before_ref, own_ref, after_ref,
+    v_ref, low_ref, q_ref, qlow_ref, ve_ref, ie_ref, e_ref, lo_ref, hi_ref,
+    above_ref, below_ref, both_ref,
+):
+    ext_x, ext_y = low_ref.shape[0], e_ref.shape[1]
+    refs = (before_ref, own_ref, after_ref, None, None, None, None)
+    e_ref[...] = jnp.zeros_like(e_ref)
+    ie_ref[...] = jnp.zeros_like(ie_ref)
+    for x in range(ext_x):
+        for y in MIDDLE:
+            tiles = [rows_of(refs, None, t, x, y, COLS, 1) for t in range(2)]
+            ie_ref[x, y - 2 : y - 1, :] = edge_of(tiles)
+            for t in range(2):
+                e_ref[x, y - 2 : y - 1, tile_of(t)] = tiles[t]
+            tiles = [rows_of(refs, None, t, x, y, 0, COLS) for t in range(2)]
+            ve_ref[x, y - 2] = edge_of(tiles)
+            for t in range(2):
+                low_ref[x, y - 2, :, tile_of(t)] = lowered(tiles[t])
+                if 0 < x < ext_x - 1:
+                    v_ref[x - 1, y - 2, :, tile_of(t)] = tiles[t]
+        for t in range(2):
+            e_ref[x, :, tile_of(t)] = modulus_of(levels_ref, e_ref[x, :, tile_of(t)])
+    pack_rows((None, None), (lo_ref, hi_ref), refs, None, ext_x, ext_y, MIDDLE)
+    element_weights(e_ref, above_ref, below_ref, both_ref, 2)
+    sides = sides_of(above_ref, below_ref, both_ref)
+    for x in range(1, ext_x - 1):
+        for y in (1, 2):
+            image = operator(
+                lambda t: v_ref[x - 1, y, :, tile_of(t)],
+                lambda i, j, t: low_ref[i, j, :, tile_of(t)],
+                sides, 2, x, y, x, y,
+            )
+            for t in range(2):
+                value = image[t]
+                if x in (1, ext_x - 2):
+                    value = jnp.where(e_ref[x, y : y + 1, tile_of(t)] > 0.0, value, 0.0)
+                q_ref[x - 1, y - 1, :, tile_of(t)] = value
+                qlow_ref[x - 1, y - 1, :, tile_of(t)] = lowered(value)
+
+
 def main_kernel(
-    levels_ref, flags_ref, a_ref, b_ref, c_ref, d_ref, e0_ref, f_ref, g_ref,
+    levels_ref, flags_ref, a_ref, b_ref, c_ref, d_ref,
+    vm_ref, lowm_ref, qm_ref, qlowm_ref, vem_ref, iem_ref, em_ref,
     v_ref, q_ref, above_ref, below_ref, both_ref, total_ref, ve_ref, ie_ref,
     low_ref, qlow_ref, e_ref, left_ref, right_ref,
 ):
     ext_x, ext_y = low_ref.shape[0], low_ref.shape[1]
-    refs = (a_ref, b_ref, c_ref, d_ref, e0_ref, f_ref, g_ref)
+    refs = (None, None, None, a_ref, b_ref, c_ref, d_ref)
     for x in range(ext_x):
-        for y in range(ext_y):
+        ie_ref[x, 2:6, :] = iem_ref[x, 0:4, :]
+        for y in OUTER:
             tiles = [rows_of(refs, flags_ref, t, x, y, COLS, 1) for t in range(2)]
-            lane = lanes_of(tiles[0])
-            edge = jnp.where(lane < EDGE, tiles[0], jnp.where(lane < 2 * EDGE, turn(tiles[1], 2 * EDGE), 0.0))
-            ie_ref[x, y : y + 1, :] = edge
+            ie_ref[x, y : y + 1, :] = edge_of(tiles)
             for t in range(2):
                 e_ref[x, y : y + 1, tile_of(t)] = tiles[t]
         for t in range(2):
+            e_ref[x, 2:6, tile_of(t)] = jnp.zeros((4, LANES), jnp.float32)
             e_ref[x, :, tile_of(t)] = modulus_of(levels_ref, e_ref[x, :, tile_of(t)])
+            e_ref[x, 2:6, tile_of(t)] = em_ref[x, 0:4, tile_of(t)]
     element_weights(e_ref, above_ref, below_ref, both_ref, 2)
     for x in range(ext_x):
         for y in range(ext_y):
+            inner = 0 < x < ext_x - 1 and 0 < y < ext_y - 1
+            if y in MIDDLE:
+                ve_ref[x, y] = vem_ref[x, y - 2]
+                low_ref[x, y] = lowm_ref[x, y - 2]
+                if inner:
+                    v_ref[x - 1, y - 1] = vm_ref[x - 1, y - 2]
+                if inner and y in (3, 4):
+                    q_ref[x - 1, y - 1] = qm_ref[x - 1, y - 3]
+                    qlow_ref[x - 1, y - 1] = qlowm_ref[x - 1, y - 3]
+                continue
             tiles = [rows_of(refs, flags_ref, t, x, y, 0, COLS) for t in range(2)]
-            lane = lanes_of(tiles[0])
-            edge = jnp.where(lane < EDGE, tiles[0], jnp.where(lane < 2 * EDGE, turn(tiles[1], 2 * EDGE), 0.0))
-            ve_ref[x, y] = edge
+            ve_ref[x, y] = edge_of(tiles)
             for t in range(2):
                 low_ref[x, y, :, tile_of(t)] = lowered(tiles[t])
-                if 0 < x < ext_x - 1 and 0 < y < ext_y - 1:
+                if inner:
                     v_ref[x - 1, y - 1, :, tile_of(t)] = tiles[t]
     sides = sides_of(above_ref, below_ref, both_ref)
-    first_image(v_ref, low_ref, e_ref, sides, q_ref, qlow_ref, 2)
+    first_image(v_ref, low_ref, e_ref, sides, q_ref, qlow_ref, 2, (1, 2, 5, 6))
     for n, (t, b, q, w) in enumerate(own_nodes(v_ref, q_ref, qlow_ref, sides, 2)):
         right = split_terms(jnp.concatenate([b, q, w], axis=0), 3)
         left = left_terms(right)
@@ -297,7 +362,7 @@
             if 0 < x < ext_x - 1 and 0 < y < ext_y - 1:
                 v_ref[x - 1, y - 1] = value
     sides = sides_of(above_ref, below_ref, both_ref)
-    first_image(v_ref, low_ref, e_ref, sides, q_ref, qlow_ref, 1)
+    first_image(v_ref, low_ref, e_ref, sides, q_ref, qlow_ref, 1, range(1, ext_y - 1))
     right = jnp.zeros((3 * COLS, LANES), jnp.float32)
     for n, (_, b, q, w) in enumerate(own_nodes(v_ref, q_ref, qlow_ref, sides, 1)):
         three = jnp.concatenate([b, q, w], axis=0)
@@ -462,7 +527,7 @@
             ],
             axis=1,
         ),
-        2,
+        3,
     )
     for x in range(1, own_x - 1):
         for y in range(1, own_y - 1):
@@ -490,7 +555,7 @@
                 ],
                 axis=0,
             )
-            out = mixed(last, block, 2)
+            out = mixed(last, block, 3)
             sol_ref[:, x - 1, y - 1, :] = out[:COLS]
             res_ref[:, x - 1, y - 1, :] = b + out[COLS:]
 
@@ -539,11 +604,33 @@
     parts = part[:, :, :, 2:], part[:, :, :, :2]
     sides = both_ways(GY, *parts, around=True)
     lasts = both_ways(GY, after[:, :, :, 2:], after[:, :, :, :2], around=True)
-    flat = [near(v.reshape(-1, LANES)) for v in (before, own, after, sides[0], lasts[0], sides[1], lasts[1])]
-    ends = pltpu.VMEM((COLS + 8, LANES), f32)
+    line = [near(v.reshape(-1, LANES)) for v in (before, own, after)]
+    flat = [near(v.reshape(-1, LANES)) for v in (sides[0], lasts[0], sides[1], lasts[1])]
+    levels, flags = near(levels), near(flags)
+    ends = (pltpu.VMEM((COLS + 8, LANES), f32),) * 2
+
+    def block(xs, ys, size):
+        return pltpu.VMEM((xs, ys, COLS, size), f32)
+
+    *mid, lo, hi = pl.pallas_call(
+        middle_kernel,
+        out_shape=(
+            block(ext_x - 2, own_y, wide),
+            block(ext_x, own_y, wide),
+            block(ext_x - 2, own_y - 2, wide),
+            block(ext_x - 2, own_y - 2, wide),
+            block(ext_x, own_y, LANES),
+            pltpu.VMEM((ext_x, ext_y, LANES), f32),
+            pltpu.VMEM((ext_x, ext_y, wide), f32),
+            *ends,
+        ),
+        scratch_shapes=[pltpu.VMEM((ext_x - 1, ext_y, wide), f32)] * 3,
+        compiler_params=GRANT,
+        name="middle",
+    )(levels, *line)
     first, last = pl.pallas_call(
-        functools.partial(pack_kernel, ext_x=ext_x, ext_y=ext_y), out_shape=(ends, ends), name="pack"
-    )(near(flags), *flat)
+        functools.partial(pack_kernel, ext_x=ext_x, ext_y=ext_y), out_shape=ends, compiler_params=GRANT, name="pack"
+    )(flags, *flat, near(lo), near(hi))
     before, after = both_ways("gz", last, first)
     nodes = own_x * own_y
 
@@ -571,12 +658,14 @@
         ),
         scratch_shapes=scratch(wide)
         + [pltpu.VMEM((6 * COLS, nodes * wide), bf16), pltpu.VMEM((9 * COLS, nodes * wide), bf16)],
+        compiler_params=GRANT,
         name="main",
-    )(near(levels), near(flags), *flat)
+    )(levels, flags, *flat, *[near(v) for v in mid])
     *edges, moments = pl.pallas_call(
         edge_kernel,
         out_shape=(*fields(LANES), *weights(LANES), pltpu.VMEM((8, LANES), f32)),
         scratch_shapes=scratch(LANES),
+        compiler_params=GRANT,
         name="edge",
     )(*[near(value) for value in (levels, total, edge, ids, before, after)])
     rows = 5
@@ -591,6 +680,7 @@
         out_shape=(out, out),
         scratch_shapes=[pltpu.VMEM((ext_x - 2, ext_y - 2, COLS, 3 * LANES), f32)] * 2
         + [pltpu.VMEM((ext_x - 1, ext_y, wide), f32)] * 3,
+        compiler_params=GRANT,
         name="finish",
     )(*[near(value) for value in (moments, *main, *edges)])
 

time: 84 us -> 83.8 us (level)
  no operation moved by 1% of the time
where the time goes in v8:
time: 83.8 us; the launch traced here: 83.5 us
  blocking collectives  48 us (57%)
  starting transfers between devices  24.1 us (29%)
  Pallas kernels  6.8 us (8%)
  waiting for transfers between devices  3.37 us (4%)
    all_to_all x2, blocking collectives, spread(): lax.all_to_all(copies, axes, 0, 0, axis_index_groups=[group])  48 us
    ppermute x4, starting transfers between devices, both_ways(): after = lax.ppermute(to_last, axis, [((i + 1) % count, i) for i in steps])  18.8 us
    ppermute x4, starting transfers between devices, both_ways(): before = lax.ppermute(to_next, axis, [(i, (i + 1) % count) for i in steps])  5.32 us
    pallas_call x1, Pallas kernels, on_device(): pl.pallas_call(finish_kernel, out_shape=(out, out), scratch_shapes=[pltpu...  2.82 us
    ppermute x4, waiting for transfers between devices, both_ways(): after = lax.ppermute(to_last, axis, [((i + 1) % count, i) for i in steps])  2.21 us
  transfers between devices with their start and end apart: 8, of which 4 were waited for; matrix products, arithmetic and copies ran while one was open for 0% of the time, Pallas kernels for 2%

profile of v8, /device:TPU:1, one launch (start us, length us, event | category | flops | bytes accessed | tf_op | source)
XLA Modules:
  0.0 83.5 jit_solution(13803452122773387018)
XLA Ops:
  0.6 0.9 %front.1 = (f32[2,17,2,4,128]{4,3,2,1,0:T(4,128)S(1)}, f32[8,128]{1,0:T(8,128)S(1)}) custom-call(f32[8]{0:T(128)} %moduli_ref.1, f32[16,2,4,256]{3,2,1,0:T(4,128)} %loads_ref.1, s32[2,4,256]{2,1,0:T(4,128)} %material_ref.1), custom_call_target="tpu_custom_call" | custom-call | tf_op jit(solution)/shard_map/front/pallas_call | solution.py:586
  1.6 4.0 %collective-permute-start = (f32[2,17,2,4,128]{4,3,2,1,0:T(4,128)S(1)}, f32[2,17,2,4,128]{4,3,2,1,0:T(4,128)S(1)}, u32[]{:S(2)}, u32[]{:S(2)}) collective-permute-start(f32[2,17,2,4,128]{4,3,2,1,0:T(4,128)S(1)} %get-tuple-element.30), channel_id=1, source_target_pairs={{0,256},{256,512},{512,768},{1,257},{257,513},{513,769},{2,258},{2... | collective-permute-start | bytes 417800 | tf_op jit(solution)/shard_map/ppermute | solution.py:566
  5.6 1.3 %collective-permute-start.2 = (f32[2,17,2,4,128]{4,3,2,1,0:T(4,128)S(1)}, f32[2,17,2,4,128]{4,3,2,1,0:T(4,128)S(1)}, u32[]{:S(2)}, u32[]{:S(2)}) collective-permute-start(f32[2,17,2,4,128]{4,3,2,1,0:T(4,128)S(1)} %get-tuple-element.30), channel_id=1, source_target_pairs={{256,0},{512,256},{768,512},{257,1},{513,257},{769,513},{258,2},{5... | collective-permute-start | bytes 417800 | tf_op jit(solution)/shard_map/ppermute | solution.py:567
  6.9 0.7 collective-permute-done
  7.7 0.1 fusion
  7.8 12.0 %collective-permute-start.4 = (f32[2,17,4,2,128]{4,3,2,1,0:T(2,128)S(1)}, f32[2,17,4,2,128]{4,3,2,1,0:T(2,128)S(1)}, u32[]{:S(2)}, u32[]{:S(2)}) collective-permute-start(f32[2,17,4,2,128]{4,3,2,1,0:T(2,128)S(1)} %get-tuple-element.56), channel_id=1, source_target_pairs={{32,0},{64,32},{96,64},{128,96},{160,128},{192,160},{224,192},{0,2... | collective-permute-start | bytes 417800 | tf_op jit(solution)/shard_map/ppermute | solution.py:567
  19.7 0.0 collective-permute-start.1
  19.7 0.0 collective-permute-done.2
  19.8 0.1 fusion.1
  19.8 4.2 %collective-permute-start.5 = (f32[2,17,2,2,128]{4,3,2,1,0:T(2,128)S(1)}, f32[2,17,2,2,128]{4,3,2,1,0:T(2,128)S(1)}, u32[]{:S(2)}, u32[]{:S(2)}) collective-permute-start(f32[2,17,2,2,128]{4,3,2,1,0:T(2,128)S(1)} %get-tuple-element.58), channel_id=1, source_target_pairs={{32,0},{64,32},{96,64},{128,96},{160,128},{192,160},{224,192},{0,2... | collective-permute-start | bytes 208904 | tf_op jit(solution)/shard_map/ppermute | solution.py:567
  24.0 0.0 collective-permute-start.3
  24.0 0.5 middle.1
  24.6 0.4 collective-permute-done.5
  24.9 0.5 collective-permute-done.3
  25.4 0.0 collective-permute-done.4
  25.4 0.0 collective-permute-done.1
  25.4 0.1 iota.7.flags_ref
  25.5 0.2 pack.1
  25.7 1.3 %collective-permute-start.6 = (f32[24,128]{1,0:T(8,128)S(1)}, f32[24,128]{1,0:T(8,128)S(1)}, u32[]{:S(2)}, u32[]{:S(2)}) collective-permute-start(f32[24,128]{1,0:T(8,128)S(1)} %get-tuple-element.43), channel_id=1, source_target_pairs={{0,1},{1,2},{2,3},{3,4},{4,5},{5,6},{6,7},{7,8},{8,9},{9,10},{10,1... | collective-permute-start | bytes 36872 | tf_op jit(solution)/shard_map/ppermute | solution.py:566
  27.0 1.3 %collective-permute-start.7 = (f32[24,128]{1,0:T(8,128)S(1)}, f32[24,128]{1,0:T(8,128)S(1)}, u32[]{:S(2)}, u32[]{:S(2)}) collective-permute-start(f32[24,128]{1,0:T(8,128)S(1)} %get-tuple-element.44), channel_id=1, source_target_pairs={{1,0},{2,1},{3,2},{4,3},{5,4},{6,5},{7,6},{8,7},{9,8},{10,9},{11,1... | collective-permute-start | bytes 36872 | tf_op jit(solution)/shard_map/ppermute | solution.py:567
  28.3 1.3 %main.1 = (f32[4,6,16,256]{3,2,1,0:T(8,128)S(1)}, f32[4,6,16,256]{3,2,1,0:T(8,128)S(1)}, f32[5,8,256]{2,1,0:T(8,128)S(1)}, f32[5,8,256]{2,1,0:T(8,128)S(1)}, f32...) custom-call(f32[8,128]{1,0:T(8,128)S(1)} %get-tuple-element.29.levels_r, ...), custom_call_target="tpu_custom_call" | custom-call | tf_op jit(solution)/shard_map/main/pallas_call | solution.py:650
  29.6 0.0 collective-permute-done.6.before_ref
  29.6 1.9 %collective-permute-done.7.after_ref = f32[24,128]{1,0:T(8,128)S(1)} collective-permute-done((f32[24,128]{1,0:T(8,128)S(1)}, f32[24,128]{1,0:T(8,128)S(1)}, u32[]{:S(2)}, u32[]{:S(2)}) %collective-permute-start.7) | collective-permute-done | bytes 12320 | tf_op jit(solution)/shard_map/ppermute | solution.py:567
  31.4 1.0 %edge.1 = (f32[4,6,16,128]{3,2,1,0:T(8,128)S(1)}, f32[4,6,16,128]{3,2,1,0:T(8,128)S(1)}, f32[5,8,128]{2,1,0:T(8,128)S(1)}, f32[5,8,128]{2,1,0:T(8,128)S(1)}, f32...) custom-call(f32[8,128]{1,0:T(8,128)S(1)} %get-tuple-element.29.levels_ref, f32[32,128]{1,0:T(8,128)S(1)} %get-tuple-element.38.total_ref, ...), custom_call_target="tpu_custom_call" | custom-call | tf_op jit(solution)/shard_map/edge/pallas_call | solution.py:664
  32.4 0.1 broadcast_in_dim.22
  32.5 32.4 %all_to_all.10 = f32[32,5,1,128]{3,2,1,0:T(1,128)S(1)} all-to-all(f32[32,5,1,128]{3,2,1,0:T(1,128)S(1)} %broadcast_in_dim.22), channel_id=1, replica_groups={{17,18,19,20,21,22,23,24,25,26,27,28,29,30,31,0,1,2,3,4,5,6,7,8,9,10,11..., dimensions={0} | all-to-all | bytes 163840 | tf_op jit(solution)/shard_map/all_to_all | solution.py:575
  64.9 0.1 reduce_sum.18
  65.1 15.6 %all_to_all.11 = f32[32,5,1,128]{3,2,1,0:T(1,128)S(1)} all-to-all(f32[32,5,1,128]{3,2,1,0:T(1,128)S(1)} %broadcast_in_dim.23), channel_id=1, replica_groups={{672,704,736,768,800,832,864,896,928,960,992,0,32,64,96,128,160,192,224..., dimensions={0} | all-to-all | bytes 163840 | tf_op jit(solution)/shard_map/all_to_all | solution.py:575
  80.6 0.1 reduce_sum.19
  80.7 2.8 %finish.1 = (f32[16,2,4,256]{3,2,1,0:T(4,128)}, f32[16,2,4,256]{3,2,1,0:T(4,128)}) custom-call(f32[8,128]{1,0:T(8,128)S(1)} %concatenate.7.g_ref, f32[4,6,16,256]{3,2,1,0:T(8,128)S(1)} %get-tuple-element.46.v_ref, f32[4,6,16,256]{3,2,1,0:T(8,128)S(1)} %get-tuple-element.47.q_ref, f32[5,8,256]{2,1,0:T(8,128)S(1)} %get-tuple-element.48.above_ref, ...), custom_call_target="tpu_custom_call" | custom-call | tf_op jit(solution)/shard_map/finish/pallas_call | solution.py:678
  (5 shorter events, 0.1 us)
Async XLA Ops:
  1.6 6.0 %collective-permute-start = (f32[2,17,2,4,128]{4,3,2,1,0:T(4,128)S(1)}, f32[2,17,2,4,128]{4,3,2,1,0:T(4,128)S(1)}, u32[]{:S(2)}, u32[]{:S(2)}) collective-permute-start(f32[2,17,2,4,128]{4,3,2,1,0:T(4,128)S(1)} %get-tuple-element.30), channel_id=1, source_target_pairs={{0,256},{256,512},{512,768},{1,257},{257,513},{513,769},{2,258},{2... | collective-permute-start | bytes 417800 | tf_op jit(solution)/shard_map/ppermute | solution.py:566
  5.6 14.1 %collective-permute-start.2 = (f32[2,17,2,4,128]{4,3,2,1,0:T(4,128)S(1)}, f32[2,17,2,4,128]{4,3,2,1,0:T(4,128)S(1)}, u32[]{:S(2)}, u32[]{:S(2)}) collective-permute-start(f32[2,17,2,4,128]{4,3,2,1,0:T(4,128)S(1)} %get-tuple-element.30), channel_id=1, source_target_pairs={{256,0},{512,256},{768,512},{257,1},{513,257},{769,513},{258,2},{5... | collective-permute-start | bytes 417800 | tf_op jit(solution)/shard_map/ppermute | solution.py:567
  7.8 17.6 %collective-permute-start.4 = (f32[2,17,4,2,128]{4,3,2,1,0:T(2,128)S(1)}, f32[2,17,4,2,128]{4,3,2,1,0:T(2,128)S(1)}, u32[]{:S(2)}, u32[]{:S(2)}) collective-permute-start(f32[2,17,4,2,128]{4,3,2,1,0:T(2,128)S(1)} %get-tuple-element.56), channel_id=1, source_target_pairs={{32,0},{64,32},{96,64},{128,96},{160,128},{192,160},{224,192},{0,2... | collective-permute-start | bytes 417800 | tf_op jit(solution)/shard_map/ppermute | solution.py:567
  19.7 5.7 %collective-permute-start.1 = (f32[2,17,4,2,128]{4,3,2,1,0:T(2,128)S(1)}, f32[2,17,4,2,128]{4,3,2,1,0:T(2,128)S(1)}, u32[]{:S(2)}, u32[]{:S(2)}) collective-permute-start(f32[2,17,4,2,128]{4,3,2,1,0:T(2,128)S(1)} %get-tuple-element.57), channel_id=1, source_target_pairs={{0,32},{32,64},{64,96},{96,128},{128,160},{160,192},{192,224},{224... | collective-permute-start | bytes 417800 | tf_op jit(solution)/shard_map/ppermute | solution.py:566
  19.8 5.1 %collective-permute-start.5 = (f32[2,17,2,2,128]{4,3,2,1,0:T(2,128)S(1)}, f32[2,17,2,2,128]{4,3,2,1,0:T(2,128)S(1)}, u32[]{:S(2)}, u32[]{:S(2)}) collective-permute-start(f32[2,17,2,2,128]{4,3,2,1,0:T(2,128)S(1)} %get-tuple-element.58), channel_id=1, source_target_pairs={{32,0},{64,32},{96,64},{128,96},{160,128},{192,160},{224,192},{0,2... | collective-permute-start | bytes 208904 | tf_op jit(solution)/shard_map/ppermute | solution.py:567
  24.0 1.4 %collective-permute-start.3 = (f32[2,17,2,2,128]{4,3,2,1,0:T(2,128)S(1)}, f32[2,17,2,2,128]{4,3,2,1,0:T(2,128)S(1)}, u32[]{:S(2)}, u32[]{:S(2)}) collective-permute-start(f32[2,17,2,2,128]{4,3,2,1,0:T(2,128)S(1)} %get-tuple-element.59), channel_id=1, source_target_pairs={{0,32},{32,64},{64,96},{96,128},{128,160},{160,192},{192,224},{224... | collective-permute-start | bytes 208904 | tf_op jit(solution)/shard_map/ppermute | solution.py:566
  25.7 3.9 %collective-permute-start.6 = (f32[24,128]{1,0:T(8,128)S(1)}, f32[24,128]{1,0:T(8,128)S(1)}, u32[]{:S(2)}, u32[]{:S(2)}) collective-permute-start(f32[24,128]{1,0:T(8,128)S(1)} %get-tuple-element.43), channel_id=1, source_target_pairs={{0,1},{1,2},{2,3},{3,4},{4,5},{5,6},{6,7},{7,8},{8,9},{9,10},{10,1... | collective-permute-start | bytes 36872 | tf_op jit(solution)/shard_map/ppermute | solution.py:566
  27.0 4.4 %collective-permute-start.7 = (f32[24,128]{1,0:T(8,128)S(1)}, f32[24,128]{1,0:T(8,128)S(1)}, u32[]{:S(2)}, u32[]{:S(2)}) collective-permute-start(f32[24,128]{1,0:T(8,128)S(1)} %get-tuple-element.44), channel_id=1, source_target_pairs={{1,0},{2,1},{3,2},{4,3},{5,4},{6,5},{7,6},{8,7},{9,8},{10,9},{11,1... | collective-permute-start | bytes 36872 | tf_op jit(solution)/shard_map/ppermute | solution.py:567

commit v9 on v8

--- a/solution.py
+++ b/solution.py
@@ -169,6 +169,16 @@
 def pack_kernel(flags_ref, a_ref, b_ref, c_ref, d_ref, lo0_ref, hi0_ref, lo_ref, hi_ref, ext_x, ext_y):
     refs = (None, None, None, a_ref, b_ref, c_ref, d_ref)
     pack_rows((lo0_ref, hi0_ref), (lo_ref, hi_ref), refs, flags_ref, ext_x, ext_y, OUTER)
+
+
+def total_kernel(flags_ref, parts_ref, out_ref, count):
+    rows = parts_ref.shape[0] // count
+    sub = lax.broadcasted_iota(jnp.int32, (8, LANES), 0)
+    out = jnp.zeros((8, LANES), jnp.float32)
+    for row in range(rows):
+        part = jnp.sum(parts_ref[pl.ds(row, count, stride=rows), :], axis=0, keepdims=True)
+        out = jnp.where(sub == row, part, out)
+    out_ref[...] = jnp.where(flags_ref[2:3, :] > 0.0, out, 0.0)
 
 
 def modulus_of(levels_ref, ids):
@@ -575,6 +585,15 @@
     return jnp.sum(lax.all_to_all(copies, axes, 0, 0, axis_index_groups=[group]), axis=0)
 
 
+def line_groups(root):
+    wide_x, wide_y, _, long = (lax.axis_size(axis) for axis in (*PLANE, "gz"))
+    at = np.arange(wide_x * wide_y * 2 * long).reshape(wide_x * wide_y, 2, long)
+    order = [(root + i) % long for i in range(long)]
+    lines = [[int(v) for v in at[place, 1, order]] for place in range(wide_x * wide_y)]
+    others = at[:, 0, :].T.reshape(-1, long)
+    return lines + [[int(v) for v in group] for group in others]
+
+
 def near(value):
     return pltpu.with_memory_space_constraint(value, pltpu.VMEM)
 
@@ -598,7 +617,8 @@
     )(moduli, loads, material)
     place = lax.axis_index(GY)
     row = lax.broadcasted_iota(jnp.int32, (8, LANES), 0)
-    flags = jnp.where(row == 0, place > 0, place < lax.axis_size(GY) - 1).astype(f32)
+    flags = jnp.where(row == 0, place > 0, place < lax.axis_size(GY) - 1)
+    flags = jnp.where(row == 2, lax.axis_index("gy_1") == 1, flags).astype(f32)
     before, after = both_ways("gx", own, own)
     part = jnp.concatenate([before, own], axis=2)
     parts = part[:, :, :, 2:], part[:, :, :, :2]
@@ -670,7 +690,16 @@
     )(*[near(value) for value in (levels, total, edge, ids, before, after)])
     rows = 5
     length, chips = lax.axis_size("gz"), lax.axis_size("gy_0")
-    moments = spread(moments[:rows].reshape(rows, 1, LANES), "gz", 17 * length // 32)
+    moments = jnp.sum(lax.all_gather(moments[:rows], "gy_1"), axis=0).reshape(rows, 1, LANES)
+    copies = jnp.broadcast_to(moments[None], (length, *moments.shape))
+    moments = lax.all_to_all(copies, (*PLANE, "gz"), 0, 0, axis_index_groups=line_groups(18 * length // 32))
+    moments = pl.pallas_call(
+        functools.partial(total_kernel, count=length),
+        out_shape=pltpu.VMEM((8, LANES), f32),
+        compiler_params=GRANT,
+        name="total",
+    )(flags, near(moments.reshape(length * rows, LANES)))
+    moments = moments[:rows].reshape(rows, 1, LANES)
     middle = (lax.axis_size("gx") // 2 * chips + chips // 2) * 2 + 1
     moments = spread(moments, PLANE, middle).reshape(rows, LANES)
     moments = jnp.concatenate([moments, jnp.zeros((8 - rows, LANES), f32)], axis=0)

time: 83.8 us -> 83.9 us (level)
    all_to_all x2 -> x1, blocking collectives: 48 us -> 10.2 us  [spread(): lax.all_to_all(copies, axes, 0, 0, axis_index_groups=[group])]
    all_to_all x0 -> x1, blocking collectives: none -> 31.7 us  [on_device(): lax.all_to_all(copies, (*PLANE, 'gz'), 0, 0, axis_index_groups=line_group...]
    all_gather x0 -> x1, blocking collectives: none -> 6.24 us  [on_device(): lax.all_gather(moments[:rows], 'gy_1')]
where the time goes in v9:
time: 83.9 us; the launch traced here: 83.6 us
  blocking collectives  48.1 us (57%)
  starting transfers between devices  24.1 us (29%)
  Pallas kernels  6.82 us (8%)
  waiting for transfers between devices  3.35 us (4%)
    all_to_all x1, blocking collectives, on_device(): lax.all_to_all(copies, (*PLANE, 'gz'), 0, 0, axis_index_groups=line_group...  31.7 us
    ppermute x4, starting transfers between devices, both_ways(): after = lax.ppermute(to_last, axis, [((i + 1) % count, i) for i in steps])  18.8 us
    all_to_all x1, blocking collectives, spread(): lax.all_to_all(copies, axes, 0, 0, axis_index_groups=[group])  10.2 us
    all_gather x1, blocking collectives, on_device(): lax.all_gather(moments[:rows], 'gy_1')  6.24 us
    ppermute x4, starting transfers between devices, both_ways(): before = lax.ppermute(to_next, axis, [(i, (i + 1) % count) for i in steps])  5.32 us
    pallas_call x1, Pallas kernels, on_device(): pl.pallas_call(finish_kernel, out_shape=(out, out), scratch_shapes=[pltpu...  2.82 us
    ppermute x4, waiting for transfers between devices, both_ways(): after = lax.ppermute(to_last, axis, [((i + 1) % count, i) for i in steps])  2.19 us
  transfers between devices with their start and end apart: 8, of which 4 were waited for; matrix products, arithmetic and copies ran while one was open for 0% of the time, Pallas kernels for 2%

profile of v9, /device:TPU:1, one launch (start us, length us, event | category | flops | bytes accessed | tf_op | source)
XLA Modules:
  0.0 83.6 jit_solution(13152312097050453139)
XLA Ops:
  0.6 0.9 %front.1 = (f32[2,17,2,4,128]{4,3,2,1,0:T(4,128)S(1)}, f32[8,128]{1,0:T(8,128)S(1)}) custom-call(f32[8]{0:T(128)} %moduli_ref.1, f32[16,2,4,256]{3,2,1,0:T(4,128)} %loads_ref.1, s32[2,4,256]{2,1,0:T(4,128)} %material_ref.1), custom_call_target="tpu_custom_call" | custom-call | tf_op jit(solution)/shard_map/front/pallas_call | solution.py:605
  1.6 4.0 %collective-permute-start = (f32[2,17,2,4,128]{4,3,2,1,0:T(4,128)S(1)}, f32[2,17,2,4,128]{4,3,2,1,0:T(4,128)S(1)}, u32[]{:S(2)}, u32[]{:S(2)}) collective-permute-start(f32[2,17,2,4,128]{4,3,2,1,0:T(4,128)S(1)} %get-tuple-element.30), channel_id=1, source_target_pairs={{0,256},{256,512},{512,768},{1,257},{257,513},{513,769},{2,258},{2... | collective-permute-start | bytes 417800 | tf_op jit(solution)/shard_map/ppermute | solution.py:576
  5.6 1.3 %collective-permute-start.2 = (f32[2,17,2,4,128]{4,3,2,1,0:T(4,128)S(1)}, f32[2,17,2,4,128]{4,3,2,1,0:T(4,128)S(1)}, u32[]{:S(2)}, u32[]{:S(2)}) collective-permute-start(f32[2,17,2,4,128]{4,3,2,1,0:T(4,128)S(1)} %get-tuple-element.30), channel_id=1, source_target_pairs={{256,0},{512,256},{768,512},{257,1},{513,257},{769,513},{258,2},{5... | collective-permute-start | bytes 417800 | tf_op jit(solution)/shard_map/ppermute | solution.py:577
  6.9 0.7 collective-permute-done
  7.7 0.1 fusion
  7.8 12.0 %collective-permute-start.4 = (f32[2,17,4,2,128]{4,3,2,1,0:T(2,128)S(1)}, f32[2,17,4,2,128]{4,3,2,1,0:T(2,128)S(1)}, u32[]{:S(2)}, u32[]{:S(2)}) collective-permute-start(f32[2,17,4,2,128]{4,3,2,1,0:T(2,128)S(1)} %get-tuple-element.56), channel_id=1, source_target_pairs={{32,0},{64,32},{96,64},{128,96},{160,128},{192,160},{224,192},{0,2... | collective-permute-start | bytes 417800 | tf_op jit(solution)/shard_map/ppermute | solution.py:577
  19.7 0.0 collective-permute-start.1
  19.7 0.0 collective-permute-done.2
  19.8 0.1 fusion.1
  19.8 4.2 %collective-permute-start.5 = (f32[2,17,2,2,128]{4,3,2,1,0:T(2,128)S(1)}, f32[2,17,2,2,128]{4,3,2,1,0:T(2,128)S(1)}, u32[]{:S(2)}, u32[]{:S(2)}) collective-permute-start(f32[2,17,2,2,128]{4,3,2,1,0:T(2,128)S(1)} %get-tuple-element.58), channel_id=1, source_target_pairs={{32,0},{64,32},{96,64},{128,96},{160,128},{192,160},{224,192},{0,2... | collective-permute-start | bytes 208904 | tf_op jit(solution)/shard_map/ppermute | solution.py:577
  24.0 0.0 collective-permute-start.3
  24.0 0.5 middle.1
  24.6 0.3 collective-permute-done.5
  24.9 0.5 collective-permute-done.3
  25.4 0.0 collective-permute-done.4
  25.4 0.0 collective-permute-done.1
  25.4 0.1 iota.10.flags_ref
  25.5 0.2 pack.1
  25.7 1.3 %collective-permute-start.6 = (f32[24,128]{1,0:T(8,128)S(1)}, f32[24,128]{1,0:T(8,128)S(1)}, u32[]{:S(2)}, u32[]{:S(2)}) collective-permute-start(f32[24,128]{1,0:T(8,128)S(1)} %get-tuple-element.43), channel_id=1, source_target_pairs={{0,1},{1,2},{2,3},{3,4},{4,5},{5,6},{6,7},{7,8},{8,9},{9,10},{10,1... | collective-permute-start | bytes 36872 | tf_op jit(solution)/shard_map/ppermute | solution.py:576
  27.0 1.3 %collective-permute-start.7 = (f32[24,128]{1,0:T(8,128)S(1)}, f32[24,128]{1,0:T(8,128)S(1)}, u32[]{:S(2)}, u32[]{:S(2)}) collective-permute-start(f32[24,128]{1,0:T(8,128)S(1)} %get-tuple-element.44), channel_id=1, source_target_pairs={{1,0},{2,1},{3,2},{4,3},{5,4},{6,5},{7,6},{8,7},{9,8},{10,9},{11,1... | collective-permute-start | bytes 36872 | tf_op jit(solution)/shard_map/ppermute | solution.py:577
  28.3 1.3 %main.1 = (f32[4,6,16,256]{3,2,1,0:T(8,128)S(1)}, f32[4,6,16,256]{3,2,1,0:T(8,128)S(1)}, f32[5,8,256]{2,1,0:T(8,128)S(1)}, f32[5,8,256]{2,1,0:T(8,128)S(1)}, f32...) custom-call(f32[8,128]{1,0:T(8,128)S(1)} %get-tuple-element.29.levels_r, ...), custom_call_target="tpu_custom_call" | custom-call | tf_op jit(solution)/shard_map/main/pallas_call | solution.py:670
  29.6 0.0 collective-permute-done.6.before_ref
  29.6 1.8 %collective-permute-done.7.after_ref = f32[24,128]{1,0:T(8,128)S(1)} collective-permute-done((f32[24,128]{1,0:T(8,128)S(1)}, f32[24,128]{1,0:T(8,128)S(1)}, u32[]{:S(2)}, u32[]{:S(2)}) %collective-permute-start.7) | collective-permute-done | bytes 12320 | tf_op jit(solution)/shard_map/ppermute | solution.py:577
  31.4 1.0 %edge.1 = (f32[4,6,16,128]{3,2,1,0:T(8,128)S(1)}, f32[4,6,16,128]{3,2,1,0:T(8,128)S(1)}, f32[5,8,128]{2,1,0:T(8,128)S(1)}, f32[5,8,128]{2,1,0:T(8,128)S(1)}, f32...) custom-call(f32[8,128]{1,0:T(8,128)S(1)} %get-tuple-element.29.levels_ref, f32[32,128]{1,0:T(8,128)S(1)} %get-tuple-element.38.total_ref, ...), custom_call_target="tpu_custom_call" | custom-call | tf_op jit(solution)/shard_map/edge/pallas_call | solution.py:684
  32.4 6.2 %all-gather.1 = f32[2,5,128]{2,1,0:T(8,128)S(1)} all-gather(f32[1,5,128]{2,1,0:T(8,128)S(1)} %slice_bitcast_fusion), channel_id=2, replica_groups=mesh['gx'=4,'gy_0'=4,'gy_1'=2,'gz'=32] {'gy_1'}, dimensions={0}, use_global_device_ids=true | all-gather | bytes 7680 | tf_op jit(solution)/shard_map/all_gather | solution.py:693
  38.7 31.7 %all_to_all.10 = f32[32,5,1,128]{3,2,1,0:T(1,128)S(1)} all-to-all(f32[32,5,1,128]{3,2,1,0:T(1,128)S(1)} %broadcast_in_dim.26), channel_id=1, replica_groups={{50,51,52,53,54,55,56,57,58,59,60,61,62,63,32,33,34,35,36,37,38,39,40,4..., dimensions={0} | all-to-all | bytes 163840 | tf_op jit(solution)/shard_map/all_to_all | solution.py:695
  70.5 10.2 %all_to_all.11 = f32[32,5,1,128]{3,2,1,0:T(1,128)S(1)} all-to-all(f32[32,5,1,128]{3,2,1,0:T(1,128)S(1)} %broadcast_in_dim.27), channel_id=1, replica_groups={{672,704,736,768,800,832,864,896,928,960,992,0,32,64,96,128,160,192,224..., dimensions={0} | all-to-all | bytes 163840 | tf_op jit(solution)/shard_map/all_to_all | solution.py:585
  80.7 0.1 reduce_sum.19
  80.8 2.8 %finish.1 = (f32[16,2,4,256]{3,2,1,0:T(4,128)}, f32[16,2,4,256]{3,2,1,0:T(4,128)}) custom-call(f32[8,128]{1,0:T(8,128)S(1)} %concatenate.7.g_ref, f32[4,6,16,256]{3,2,1,0:T(8,128)S(1)} %get-tuple-element.46.v_ref, f32[4,6,16,256]{3,2,1,0:T(8,128)S(1)} %get-tuple-element.47.q_ref, f32[5,8,256]{2,1,0:T(8,128)S(1)} %get-tuple-element.48.above_ref, ...), custom_call_target="tpu_custom_call" | custom-call | tf_op jit(solution)/shard_map/finish/pallas_call | solution.py:707
  (9 shorter events, 0.2 us)
Async XLA Ops:
  1.6 6.0 %collective-permute-start = (f32[2,17,2,4,128]{4,3,2,1,0:T(4,128)S(1)}, f32[2,17,2,4,128]{4,3,2,1,0:T(4,128)S(1)}, u32[]{:S(2)}, u32[]{:S(2)}) collective-permute-start(f32[2,17,2,4,128]{4,3,2,1,0:T(4,128)S(1)} %get-tuple-element.30), channel_id=1, source_target_pairs={{0,256},{256,512},{512,768},{1,257},{257,513},{513,769},{2,258},{2... | collective-permute-start | bytes 417800 | tf_op jit(solution)/shard_map/ppermute | solution.py:576
  5.6 14.1 %collective-permute-start.2 = (f32[2,17,2,4,128]{4,3,2,1,0:T(4,128)S(1)}, f32[2,17,2,4,128]{4,3,2,1,0:T(4,128)S(1)}, u32[]{:S(2)}, u32[]{:S(2)}) collective-permute-start(f32[2,17,2,4,128]{4,3,2,1,0:T(4,128)S(1)} %get-tuple-element.30), channel_id=1, source_target_pairs={{256,0},{512,256},{768,512},{257,1},{513,257},{769,513},{258,2},{5... | collective-permute-start | bytes 417800 | tf_op jit(solution)/shard_map/ppermute | solution.py:577
  7.8 17.6 %collective-permute-start.4 = (f32[2,17,4,2,128]{4,3,2,1,0:T(2,128)S(1)}, f32[2,17,4,2,128]{4,3,2,1,0:T(2,128)S(1)}, u32[]{:S(2)}, u32[]{:S(2)}) collective-permute-start(f32[2,17,4,2,128]{4,3,2,1,0:T(2,128)S(1)} %get-tuple-element.56), channel_id=1, source_target_pairs={{32,0},{64,32},{96,64},{128,96},{160,128},{192,160},{224,192},{0,2... | collective-permute-start | bytes 417800 | tf_op jit(solution)/shard_map/ppermute | solution.py:577
  19.7 5.7 %collective-permute-start.1 = (f32[2,17,4,2,128]{4,3,2,1,0:T(2,128)S(1)}, f32[2,17,4,2,128]{4,3,2,1,0:T(2,128)S(1)}, u32[]{:S(2)}, u32[]{:S(2)}) collective-permute-start(f32[2,17,4,2,128]{4,3,2,1,0:T(2,128)S(1)} %get-tuple-element.57), channel_id=1, source_target_pairs={{0,32},{32,64},{64,96},{96,128},{128,160},{160,192},{192,224},{224... | collective-permute-start | bytes 417800 | tf_op jit(solution)/shard_map/ppermute | solution.py:576
  19.8 5.1 %collective-permute-start.5 = (f32[2,17,2,2,128]{4,3,2,1,0:T(2,128)S(1)}, f32[2,17,2,2,128]{4,3,2,1,0:T(2,128)S(1)}, u32[]{:S(2)}, u32[]{:S(2)}) collective-permute-start(f32[2,17,2,2,128]{4,3,2,1,0:T(2,128)S(1)} %get-tuple-element.58), channel_id=1, source_target_pairs={{32,0},{64,32},{96,64},{128,96},{160,128},{192,160},{224,192},{0,2... | collective-permute-start | bytes 208904 | tf_op jit(solution)/shard_map/ppermute | solution.py:577
  24.0 1.4 %collective-permute-start.3 = (f32[2,17,2,2,128]{4,3,2,1,0:T(2,128)S(1)}, f32[2,17,2,2,128]{4,3,2,1,0:T(2,128)S(1)}, u32[]{:S(2)}, u32[]{:S(2)}) collective-permute-start(f32[2,17,2,2,128]{4,3,2,1,0:T(2,128)S(1)} %get-tuple-element.59), channel_id=1, source_target_pairs={{0,32},{32,64},{64,96},{96,128},{128,160},{160,192},{192,224},{224... | collective-permute-start | bytes 208904 | tf_op jit(solution)/shard_map/ppermute | solution.py:576
  25.7 3.9 %collective-permute-start.6 = (f32[24,128]{1,0:T(8,128)S(1)}, f32[24,128]{1,0:T(8,128)S(1)}, u32[]{:S(2)}, u32[]{:S(2)}) collective-permute-start(f32[24,128]{1,0:T(8,128)S(1)} %get-tuple-element.43), channel_id=1, source_target_pairs={{0,1},{1,2},{2,3},{3,4},{4,5},{5,6},{6,7},{7,8},{8,9},{9,10},{10,1... | collective-permute-start | bytes 36872 | tf_op jit(solution)/shard_map/ppermute | solution.py:576
  27.0 4.4 %collective-permute-start.7 = (f32[24,128]{1,0:T(8,128)S(1)}, f32[24,128]{1,0:T(8,128)S(1)}, u32[]{:S(2)}, u32[]{:S(2)}) collective-permute-start(f32[24,128]{1,0:T(8,128)S(1)} %get-tuple-element.44), channel_id=1, source_target_pairs={{1,0},{2,1},{3,2},{4,3},{5,4},{6,5},{7,6},{8,7},{9,8},{10,9},{11,1... | collective-permute-start | bytes 36872 | tf_op jit(solution)/shard_map/ppermute | solution.py:577

commit v10 on v9

--- a/solution.py
+++ b/solution.py
@@ -171,14 +171,21 @@
     pack_rows((lo0_ref, hi0_ref), (lo_ref, hi_ref), refs, flags_ref, ext_x, ext_y, OUTER)
 
 
-def total_kernel(flags_ref, parts_ref, out_ref, count):
+def sums_of(parts_ref, count):
     rows = parts_ref.shape[0] // count
     sub = lax.broadcasted_iota(jnp.int32, (8, LANES), 0)
     out = jnp.zeros((8, LANES), jnp.float32)
     for row in range(rows):
         part = jnp.sum(parts_ref[pl.ds(row, count, stride=rows), :], axis=0, keepdims=True)
         out = jnp.where(sub == row, part, out)
-    out_ref[...] = jnp.where(flags_ref[2:3, :] > 0.0, out, 0.0)
+    return out
+
+
+def total_kernel(flags_ref, parts_ref, out_ref, count, copies):
+    rows = parts_ref.shape[0] // count
+    out = jnp.where(flags_ref[2:3, :] > 0.0, sums_of(parts_ref, count), 0.0)
+    for row in range(rows):
+        out_ref[pl.ds(row, copies, stride=rows), :] = jnp.broadcast_to(out[row : row + 1, :], (copies, LANES))
 
 
 def modulus_of(levels_ref, ids):
@@ -485,7 +492,7 @@
     sol_ref, res_ref, d_ref, dlow_ref, w0_ref, w1_ref, w2_ref,
 ):
     own_x, own_y = v_ref.shape[0], v_ref.shape[1]
-    m0, m1, m2, m3 = unpack_moments(g_ref[...])
+    m0, m1, m2, m3 = unpack_moments(sums_of(g_ref, g_ref.shape[0] // 5))
     first = ((0,), (0,))
     padding = jnp.zeros((COLS, LANES - COLS), jnp.float32)
     *_, minus_inv = sweeps(replicated(m1))
@@ -578,13 +585,6 @@
     return before, after
 
 
-def spread(value, axes, root):
-    count = lax.axis_size(axes)
-    copies = jnp.broadcast_to(value[None], (count, *value.shape))
-    group = [(root + i) % count for i in range(count)]
-    return jnp.sum(lax.all_to_all(copies, axes, 0, 0, axis_index_groups=[group]), axis=0)
-
-
 def line_groups(root):
     wide_x, wide_y, _, long = (lax.axis_size(axis) for axis in (*PLANE, "gz"))
     at = np.arange(wide_x * wide_y * 2 * long).reshape(wide_x * wide_y, 2, long)
@@ -692,17 +692,18 @@
     length, chips = lax.axis_size("gz"), lax.axis_size("gy_0")
     moments = jnp.sum(lax.all_gather(moments[:rows], "gy_1"), axis=0).reshape(rows, 1, LANES)
     copies = jnp.broadcast_to(moments[None], (length, *moments.shape))
-    moments = lax.all_to_all(copies, (*PLANE, "gz"), 0, 0, axis_index_groups=line_groups(18 * length // 32))
-    moments = pl.pallas_call(
-        functools.partial(total_kernel, count=length),
-        out_shape=pltpu.VMEM((8, LANES), f32),
+    moments = lax.all_to_all(copies, (*PLANE, "gz"), 0, 0, axis_index_groups=line_groups(19 * length // 32))
+    places = lax.axis_size(PLANE)
+    copies = pl.pallas_call(
+        functools.partial(total_kernel, count=length, copies=places),
+        out_shape=pltpu.VMEM((places * rows, LANES), f32),
         compiler_params=GRANT,
         name="total",
     )(flags, near(moments.reshape(length * rows, LANES)))
-    moments = moments[:rows].reshape(rows, 1, LANES)
     middle = (lax.axis_size("gx") // 2 * chips + chips // 2) * 2 + 1
-    moments = spread(moments, PLANE, middle).reshape(rows, LANES)
-    moments = jnp.concatenate([moments, jnp.zeros((8 - rows, LANES), f32)], axis=0)
+    group = [(middle + i) % places for i in range(places)]
+    copies = copies.reshape(places, rows, 1, LANES)
+    moments = lax.all_to_all(copies, PLANE, 0, 0, axis_index_groups=[group]).reshape(places * rows, LANES)
     out = jax.ShapeDtypeStruct(loads.shape, f32)
     return pl.pallas_call(
         finish_kernel,

time: 83.9 us -> 83.6 us (level)
  no operation moved by 1% of the time
where the time goes in v10:
time: 83.6 us; the launch traced here: 83.4 us
  blocking collectives  48 us (57%)
  starting transfers between devices  24.1 us (29%)
  Pallas kernels  6.83 us (8%)
  waiting for transfers between devices  3.35 us (4%)
    all_to_all x1, blocking collectives, on_device(): lax.all_to_all(copies, (*PLANE, 'gz'), 0, 0, axis_index_groups=line_group...  31.5 us
    ppermute x4, starting transfers between devices, both_ways(): after = lax.ppermute(to_last, axis, [((i + 1) % count, i) for i in steps])  18.8 us
    all_to_all x1, blocking collectives, on_device(): lax.all_to_all(copies, PLANE, 0, 0, axis_index_groups=[group])  10.2 us
    all_gather x1, blocking collectives, on_device(): lax.all_gather(moments[:rows], 'gy_1')  6.24 us
    ppermute x4, starting transfers between devices, both_ways(): before = lax.ppermute(to_next, axis, [(i, (i + 1) % count) for i in steps])  5.32 us
    pallas_call x1, Pallas kernels, on_device(): pl.pallas_call(finish_kernel, out_shape=(out, out), scratch_shapes=[pltpu...  2.82 us
    ppermute x4, waiting for transfers between devices, both_ways(): after = lax.ppermute(to_last, axis, [((i + 1) % count, i) for i in steps])  2.19 us
  transfers between devices with their start and end apart: 8, of which 4 were waited for; matrix products, arithmetic and copies ran while one was open for 0% of the time, Pallas kernels for 2%

profile of v10, /device:TPU:1, one launch (start us, length us, event | category | flops | bytes accessed | tf_op | source)
XLA Modules:
  0.0 83.4 jit_solution(12482908614639587817)
XLA Ops:
  0.6 0.9 %front.1 = (f32[2,17,2,4,128]{4,3,2,1,0:T(4,128)S(1)}, f32[8,128]{1,0:T(8,128)S(1)}) custom-call(f32[8]{0:T(128)} %moduli_ref.1, f32[16,2,4,256]{3,2,1,0:T(4,128)} %loads_ref.1, s32[2,4,256]{2,1,0:T(4,128)} %material_ref.1), custom_call_target="tpu_custom_call" | custom-call | tf_op jit(solution)/shard_map/front/pallas_call | solution.py:605
  1.6 4.0 %collective-permute-start = (f32[2,17,2,4,128]{4,3,2,1,0:T(4,128)S(1)}, f32[2,17,2,4,128]{4,3,2,1,0:T(4,128)S(1)}, u32[]{:S(2)}, u32[]{:S(2)}) collective-permute-start(f32[2,17,2,4,128]{4,3,2,1,0:T(4,128)S(1)} %get-tuple-element.30), channel_id=1, source_target_pairs={{0,256},{256,512},{512,768},{1,257},{257,513},{513,769},{2,258},{2... | collective-permute-start | bytes 417800 | tf_op jit(solution)/shard_map/ppermute | solution.py:583
  5.6 1.3 %collective-permute-start.2 = (f32[2,17,2,4,128]{4,3,2,1,0:T(4,128)S(1)}, f32[2,17,2,4,128]{4,3,2,1,0:T(4,128)S(1)}, u32[]{:S(2)}, u32[]{:S(2)}) collective-permute-start(f32[2,17,2,4,128]{4,3,2,1,0:T(4,128)S(1)} %get-tuple-element.30), channel_id=1, source_target_pairs={{256,0},{512,256},{768,512},{257,1},{513,257},{769,513},{258,2},{5... | collective-permute-start | bytes 417800 | tf_op jit(solution)/shard_map/ppermute | solution.py:584
  6.9 0.7 collective-permute-done
  7.7 0.1 fusion
  7.8 12.0 %collective-permute-start.4 = (f32[2,17,4,2,128]{4,3,2,1,0:T(2,128)S(1)}, f32[2,17,4,2,128]{4,3,2,1,0:T(2,128)S(1)}, u32[]{:S(2)}, u32[]{:S(2)}) collective-permute-start(f32[2,17,4,2,128]{4,3,2,1,0:T(2,128)S(1)} %get-tuple-element.56), channel_id=1, source_target_pairs={{32,0},{64,32},{96,64},{128,96},{160,128},{192,160},{224,192},{0,2... | collective-permute-start | bytes 417800 | tf_op jit(solution)/shard_map/ppermute | solution.py:584
  19.7 0.0 collective-permute-start.1
  19.7 0.0 collective-permute-done.2
  19.8 0.1 fusion.1
  19.8 4.2 %collective-permute-start.5 = (f32[2,17,2,2,128]{4,3,2,1,0:T(2,128)S(1)}, f32[2,17,2,2,128]{4,3,2,1,0:T(2,128)S(1)}, u32[]{:S(2)}, u32[]{:S(2)}) collective-permute-start(f32[2,17,2,2,128]{4,3,2,1,0:T(2,128)S(1)} %get-tuple-element.58), channel_id=1, source_target_pairs={{32,0},{64,32},{96,64},{128,96},{160,128},{192,160},{224,192},{0,2... | collective-permute-start | bytes 208904 | tf_op jit(solution)/shard_map/ppermute | solution.py:584
  24.0 0.0 collective-permute-start.3
  24.0 0.5 middle.1
  24.6 0.3 collective-permute-done.5
  24.9 0.5 collective-permute-done.3
  25.4 0.0 collective-permute-done.4
  25.4 0.0 collective-permute-done.1
  25.4 0.1 iota.10.flags_ref
  25.5 0.2 pack.1
  25.7 1.3 %collective-permute-start.6 = (f32[24,128]{1,0:T(8,128)S(1)}, f32[24,128]{1,0:T(8,128)S(1)}, u32[]{:S(2)}, u32[]{:S(2)}) collective-permute-start(f32[24,128]{1,0:T(8,128)S(1)} %get-tuple-element.43), channel_id=1, source_target_pairs={{0,1},{1,2},{2,3},{3,4},{4,5},{5,6},{6,7},{7,8},{8,9},{9,10},{10,1... | collective-permute-start | bytes 36872 | tf_op jit(solution)/shard_map/ppermute | solution.py:583
  27.0 1.3 %collective-permute-start.7 = (f32[24,128]{1,0:T(8,128)S(1)}, f32[24,128]{1,0:T(8,128)S(1)}, u32[]{:S(2)}, u32[]{:S(2)}) collective-permute-start(f32[24,128]{1,0:T(8,128)S(1)} %get-tuple-element.44), channel_id=1, source_target_pairs={{1,0},{2,1},{3,2},{4,3},{5,4},{6,5},{7,6},{8,7},{9,8},{10,9},{11,1... | collective-permute-start | bytes 36872 | tf_op jit(solution)/shard_map/ppermute | solution.py:584
  28.3 1.3 %main.1 = (f32[4,6,16,256]{3,2,1,0:T(8,128)S(1)}, f32[4,6,16,256]{3,2,1,0:T(8,128)S(1)}, f32[5,8,256]{2,1,0:T(8,128)S(1)}, f32[5,8,256]{2,1,0:T(8,128)S(1)}, f32...) custom-call(f32[8,128]{1,0:T(8,128)S(1)} %get-tuple-element.29.levels_r, ...), custom_call_target="tpu_custom_call" | custom-call | tf_op jit(solution)/shard_map/main/pallas_call | solution.py:670
  29.6 0.0 collective-permute-done.6.before_ref
  29.6 1.8 %collective-permute-done.7.after_ref = f32[24,128]{1,0:T(8,128)S(1)} collective-permute-done((f32[24,128]{1,0:T(8,128)S(1)}, f32[24,128]{1,0:T(8,128)S(1)}, u32[]{:S(2)}, u32[]{:S(2)}) %collective-permute-start.7) | collective-permute-done | bytes 12320 | tf_op jit(solution)/shard_map/ppermute | solution.py:584
  31.4 1.0 %edge.1 = (f32[4,6,16,128]{3,2,1,0:T(8,128)S(1)}, f32[4,6,16,128]{3,2,1,0:T(8,128)S(1)}, f32[5,8,128]{2,1,0:T(8,128)S(1)}, f32[5,8,128]{2,1,0:T(8,128)S(1)}, f32...) custom-call(f32[8,128]{1,0:T(8,128)S(1)} %get-tuple-element.29.levels_ref, f32[32,128]{1,0:T(8,128)S(1)} %get-tuple-element.38.total_ref, ...), custom_call_target="tpu_custom_call" | custom-call | tf_op jit(solution)/shard_map/edge/pallas_call | solution.py:684
  32.4 6.2 %all-gather.1 = f32[2,5,128]{2,1,0:T(8,128)S(1)} all-gather(f32[1,5,128]{2,1,0:T(8,128)S(1)} %slice_bitcast_fusion), channel_id=2, replica_groups=mesh['gx'=4,'gy_0'=4,'gy_1'=2,'gz'=32] {'gy_1'}, dimensions={0}, use_global_device_ids=true | all-gather | bytes 7680 | tf_op jit(solution)/shard_map/all_gather | solution.py:693
  38.7 31.5 %all_to_all.10 = f32[32,5,1,128]{3,2,1,0:T(1,128)S(1)} all-to-all(f32[32,5,1,128]{3,2,1,0:T(1,128)S(1)} %broadcast_in_dim.20), channel_id=1, replica_groups={{51,52,53,54,55,56,57,58,59,60,61,62,63,32,33,34,35,36,37,38,39,40,41,4..., dimensions={0} | all-to-all | bytes 163840 | tf_op jit(solution)/shard_map/all_to_all | solution.py:695
  70.3 10.2 %all_to_all.11 = f32[32,5,1,128]{3,2,1,0:T(1,128)S(1)} all-to-all(f32[32,5,1,128]{3,2,1,0:T(1,128)S(1)} %bitcast.21), channel_id=1, replica_groups={{672,704,736,768,800,832,864,896,928,960,992,0,32,64,96,128,160,192,224..., dimensions={0} | all-to-all | bytes 163840 | tf_op jit(solution)/shard_map/all_to_all | solution.py:706
  80.5 2.8 %finish.1 = (f32[16,2,4,256]{3,2,1,0:T(4,128)}, f32[16,2,4,256]{3,2,1,0:T(4,128)}) custom-call(f32[160,128]{1,0:T(8,128)S(1)} %bitcast.19, f32[4,6,16,256]{3,2,1,0:T(8,128)S(1)} %get-tuple-element.46.v_ref, f32[4,6,16,256]{3,2,1,0:T(8,128)S(1)} %get-tuple-element.47.q_ref, f32[5,8,256]{2,1,0:T(8,128)S(1)} %get-tuple-element.48.above_ref, ...), custom_call_target="tpu_custom_call" | custom-call | tf_op jit(solution)/shard_map/finish/pallas_call | solution.py:708
  (7 shorter events, 0.1 us)
Async XLA Ops:
  1.6 6.0 %collective-permute-start = (f32[2,17,2,4,128]{4,3,2,1,0:T(4,128)S(1)}, f32[2,17,2,4,128]{4,3,2,1,0:T(4,128)S(1)}, u32[]{:S(2)}, u32[]{:S(2)}) collective-permute-start(f32[2,17,2,4,128]{4,3,2,1,0:T(4,128)S(1)} %get-tuple-element.30), channel_id=1, source_target_pairs={{0,256},{256,512},{512,768},{1,257},{257,513},{513,769},{2,258},{2... | collective-permute-start | bytes 417800 | tf_op jit(solution)/shard_map/ppermute | solution.py:583
  5.6 14.1 %collective-permute-start.2 = (f32[2,17,2,4,128]{4,3,2,1,0:T(4,128)S(1)}, f32[2,17,2,4,128]{4,3,2,1,0:T(4,128)S(1)}, u32[]{:S(2)}, u32[]{:S(2)}) collective-permute-start(f32[2,17,2,4,128]{4,3,2,1,0:T(4,128)S(1)} %get-tuple-element.30), channel_id=1, source_target_pairs={{256,0},{512,256},{768,512},{257,1},{513,257},{769,513},{258,2},{5... | collective-permute-start | bytes 417800 | tf_op jit(solution)/shard_map/ppermute | solution.py:584
  7.8 17.6 %collective-permute-start.4 = (f32[2,17,4,2,128]{4,3,2,1,0:T(2,128)S(1)}, f32[2,17,4,2,128]{4,3,2,1,0:T(2,128)S(1)}, u32[]{:S(2)}, u32[]{:S(2)}) collective-permute-start(f32[2,17,4,2,128]{4,3,2,1,0:T(2,128)S(1)} %get-tuple-element.56), channel_id=1, source_target_pairs={{32,0},{64,32},{96,64},{128,96},{160,128},{192,160},{224,192},{0,2... | collective-permute-start | bytes 417800 | tf_op jit(solution)/shard_map/ppermute | solution.py:584
  19.7 5.7 %collective-permute-start.1 = (f32[2,17,4,2,128]{4,3,2,1,0:T(2,128)S(1)}, f32[2,17,4,2,128]{4,3,2,1,0:T(2,128)S(1)}, u32[]{:S(2)}, u32[]{:S(2)}) collective-permute-start(f32[2,17,4,2,128]{4,3,2,1,0:T(2,128)S(1)} %get-tuple-element.57), channel_id=1, source_target_pairs={{0,32},{32,64},{64,96},{96,128},{128,160},{160,192},{192,224},{224... | collective-permute-start | bytes 417800 | tf_op jit(solution)/shard_map/ppermute | solution.py:583
  19.8 5.1 %collective-permute-start.5 = (f32[2,17,2,2,128]{4,3,2,1,0:T(2,128)S(1)}, f32[2,17,2,2,128]{4,3,2,1,0:T(2,128)S(1)}, u32[]{:S(2)}, u32[]{:S(2)}) collective-permute-start(f32[2,17,2,2,128]{4,3,2,1,0:T(2,128)S(1)} %get-tuple-element.58), channel_id=1, source_target_pairs={{32,0},{64,32},{96,64},{128,96},{160,128},{192,160},{224,192},{0,2... | collective-permute-start | bytes 208904 | tf_op jit(solution)/shard_map/ppermute | solution.py:584
  24.0 1.4 %collective-permute-start.3 = (f32[2,17,2,2,128]{4,3,2,1,0:T(2,128)S(1)}, f32[2,17,2,2,128]{4,3,2,1,0:T(2,128)S(1)}, u32[]{:S(2)}, u32[]{:S(2)}) collective-permute-start(f32[2,17,2,2,128]{4,3,2,1,0:T(2,128)S(1)} %get-tuple-element.59), channel_id=1, source_target_pairs={{0,32},{32,64},{64,96},{96,128},{128,160},{160,192},{192,224},{224... | collective-permute-start | bytes 208904 | tf_op jit(solution)/shard_map/ppermute | solution.py:583
  25.7 3.9 %collective-permute-start.6 = (f32[24,128]{1,0:T(8,128)S(1)}, f32[24,128]{1,0:T(8,128)S(1)}, u32[]{:S(2)}, u32[]{:S(2)}) collective-permute-start(f32[24,128]{1,0:T(8,128)S(1)} %get-tuple-element.43), channel_id=1, source_target_pairs={{0,1},{1,2},{2,3},{3,4},{4,5},{5,6},{6,7},{7,8},{8,9},{9,10},{10,1... | collective-permute-start | bytes 36872 | tf_op jit(solution)/shard_map/ppermute | solution.py:583
  27.0 4.4 %collective-permute-start.7 = (f32[24,128]{1,0:T(8,128)S(1)}, f32[24,128]{1,0:T(8,128)S(1)}, u32[]{:S(2)}, u32[]{:S(2)}) collective-permute-start(f32[24,128]{1,0:T(8,128)S(1)} %get-tuple-element.44), channel_id=1, source_target_pairs={{1,0},{2,1},{3,2},{4,3},{5,4},{6,5},{7,6},{8,7},{9,8},{10,9},{11,1... | collective-permute-start | bytes 36872 | tf_op jit(solution)/shard_map/ppermute | solution.py:584

commit v11 on v10

--- a/solution.py
+++ b/solution.py
@@ -179,6 +179,14 @@
         part = jnp.sum(parts_ref[pl.ds(row, count, stride=rows), :], axis=0, keepdims=True)
         out = jnp.where(sub == row, part, out)
     return out
+
+
+def pair_kernel(both_ref, out_ref, rows):
+    copies = out_ref.shape[0] // rows
+    half = both_ref.shape[0] // 2
+    total = both_ref[:half, :] + both_ref[half:, :]
+    for row in range(rows):
+        out_ref[pl.ds(row, copies, stride=rows), :] = jnp.broadcast_to(total[row : row + 1, :], (copies, LANES))
 
 
 def total_kernel(flags_ref, parts_ref, out_ref, count, copies):
@@ -690,8 +698,13 @@
     )(*[near(value) for value in (levels, total, edge, ids, before, after)])
     rows = 5
     length, chips = lax.axis_size("gz"), lax.axis_size("gy_0")
-    moments = jnp.sum(lax.all_gather(moments[:rows], "gy_1"), axis=0).reshape(rows, 1, LANES)
-    copies = jnp.broadcast_to(moments[None], (length, *moments.shape))
+    both = near(lax.all_gather(moments, "gy_1").reshape(-1, LANES))
+    copies = pl.pallas_call(
+        functools.partial(pair_kernel, rows=rows),
+        out_shape=pltpu.VMEM((length * rows, LANES), f32),
+        compiler_params=GRANT,
+        name="pair",
+    )(both).reshape(length, rows, 1, LANES)
     moments = lax.all_to_all(copies, (*PLANE, "gz"), 0, 0, axis_index_groups=line_groups(19 * length // 32))
     places = lax.axis_size(PLANE)
     copies = pl.pallas_call(

time: 83.6 us -> 83.6 us (level)
  no operation moved by 1% of the time
where the time goes in v11:
time: 83.6 us; the launch traced here: 83.3 us
  blocking collectives  48 us (57%)
  starting transfers between devices  24.1 us (29%)
  Pallas kernels  6.85 us (8%)
  waiting for transfers between devices  3.36 us (4%)
    all_to_all x1, blocking collectives, on_device(): lax.all_to_all(copies, (*PLANE, 'gz'), 0, 0, axis_index_groups=line_group...  31.5 us
    ppermute x4, starting transfers between devices, both_ways(): after = lax.ppermute(to_last, axis, [((i + 1) % count, i) for i in steps])  18.8 us
    all_to_all x1, blocking collectives, on_device(): lax.all_to_all(copies, PLANE, 0, 0, axis_index_groups=[group])  10.2 us
    all_gather x1, blocking collectives, on_device(): both = near(lax.all_gather(moments, 'gy_1').reshape(-1, LANES))  6.25 us
    ppermute x4, starting transfers between devices, both_ways(): before = lax.ppermute(to_next, axis, [(i, (i + 1) % count) for i in steps])  5.32 us
    pallas_call x1, Pallas kernels, on_device(): pl.pallas_call(finish_kernel, out_shape=(out, out), scratch_shapes=[pltpu...  2.84 us
    ppermute x4, waiting for transfers between devices, both_ways(): after = lax.ppermute(to_last, axis, [((i + 1) % count, i) for i in steps])  2.2 us
  transfers between devices with their start and end apart: 8, of which 4 were waited for; matrix products, arithmetic and copies ran while one was open for 0% of the time, Pallas kernels for 2%

profile of v11, /device:TPU:1, one launch (start us, length us, event | category | flops | bytes accessed | tf_op | source)
XLA Modules:
  0.0 83.3 jit_solution(248379491934719004)
XLA Ops:
  0.6 0.9 %front.1 = (f32[2,17,2,4,128]{4,3,2,1,0:T(4,128)S(1)}, f32[8,128]{1,0:T(8,128)S(1)}) custom-call(f32[8]{0:T(128)} %moduli_ref.1, f32[16,2,4,256]{3,2,1,0:T(4,128)} %loads_ref.1, s32[2,4,256]{2,1,0:T(4,128)} %material_ref.1), custom_call_target="tpu_custom_call" | custom-call | tf_op jit(solution)/shard_map/front/pallas_call | solution.py:613
  1.6 4.0 %collective-permute-start = (f32[2,17,2,4,128]{4,3,2,1,0:T(4,128)S(1)}, f32[2,17,2,4,128]{4,3,2,1,0:T(4,128)S(1)}, u32[]{:S(2)}, u32[]{:S(2)}) collective-permute-start(f32[2,17,2,4,128]{4,3,2,1,0:T(4,128)S(1)} %get-tuple-element.30), channel_id=1, source_target_pairs={{0,256},{256,512},{512,768},{1,257},{257,513},{513,769},{2,258},{2... | collective-permute-start | bytes 417800 | tf_op jit(solution)/shard_map/ppermute | solution.py:591
  5.6 1.3 %collective-permute-start.2 = (f32[2,17,2,4,128]{4,3,2,1,0:T(4,128)S(1)}, f32[2,17,2,4,128]{4,3,2,1,0:T(4,128)S(1)}, u32[]{:S(2)}, u32[]{:S(2)}) collective-permute-start(f32[2,17,2,4,128]{4,3,2,1,0:T(4,128)S(1)} %get-tuple-element.30), channel_id=1, source_target_pairs={{256,0},{512,256},{768,512},{257,1},{513,257},{769,513},{258,2},{5... | collective-permute-start | bytes 417800 | tf_op jit(solution)/shard_map/ppermute | solution.py:592
  6.9 0.7 collective-permute-done
  7.7 0.1 fusion
  7.8 12.0 %collective-permute-start.4 = (f32[2,17,4,2,128]{4,3,2,1,0:T(2,128)S(1)}, f32[2,17,4,2,128]{4,3,2,1,0:T(2,128)S(1)}, u32[]{:S(2)}, u32[]{:S(2)}) collective-permute-start(f32[2,17,4,2,128]{4,3,2,1,0:T(2,128)S(1)} %get-tuple-element.56), channel_id=1, source_target_pairs={{32,0},{64,32},{96,64},{128,96},{160,128},{192,160},{224,192},{0,2... | collective-permute-start | bytes 417800 | tf_op jit(solution)/shard_map/ppermute | solution.py:592
  19.7 0.0 collective-permute-start.1
  19.7 0.0 collective-permute-done.2
  19.8 0.1 fusion.1
  19.8 4.2 %collective-permute-start.5 = (f32[2,17,2,2,128]{4,3,2,1,0:T(2,128)S(1)}, f32[2,17,2,2,128]{4,3,2,1,0:T(2,128)S(1)}, u32[]{:S(2)}, u32[]{:S(2)}) collective-permute-start(f32[2,17,2,2,128]{4,3,2,1,0:T(2,128)S(1)} %get-tuple-element.58), channel_id=1, source_target_pairs={{32,0},{64,32},{96,64},{128,96},{160,128},{192,160},{224,192},{0,2... | collective-permute-start | bytes 208904 | tf_op jit(solution)/shard_map/ppermute | solution.py:592
  24.0 0.0 collective-permute-start.3
  24.0 0.5 middle.1
  24.6 0.3 collective-permute-done.5
  24.9 0.5 collective-permute-done.3
  25.4 0.0 collective-permute-done.4
  25.4 0.0 collective-permute-done.1
  25.4 0.1 iota.10.flags_ref
  25.5 0.2 pack.1
  25.7 1.3 %collective-permute-start.6 = (f32[24,128]{1,0:T(8,128)S(1)}, f32[24,128]{1,0:T(8,128)S(1)}, u32[]{:S(2)}, u32[]{:S(2)}) collective-permute-start(f32[24,128]{1,0:T(8,128)S(1)} %get-tuple-element.43), channel_id=1, source_target_pairs={{0,1},{1,2},{2,3},{3,4},{4,5},{5,6},{6,7},{7,8},{8,9},{9,10},{10,1... | collective-permute-start | bytes 36872 | tf_op jit(solution)/shard_map/ppermute | solution.py:591
  27.0 1.3 %collective-permute-start.7 = (f32[24,128]{1,0:T(8,128)S(1)}, f32[24,128]{1,0:T(8,128)S(1)}, u32[]{:S(2)}, u32[]{:S(2)}) collective-permute-start(f32[24,128]{1,0:T(8,128)S(1)} %get-tuple-element.44), channel_id=1, source_target_pairs={{1,0},{2,1},{3,2},{4,3},{5,4},{6,5},{7,6},{8,7},{9,8},{10,9},{11,1... | collective-permute-start | bytes 36872 | tf_op jit(solution)/shard_map/ppermute | solution.py:592
  28.3 1.3 %main.1 = (f32[4,6,16,256]{3,2,1,0:T(8,128)S(1)}, f32[4,6,16,256]{3,2,1,0:T(8,128)S(1)}, f32[5,8,256]{2,1,0:T(8,128)S(1)}, f32[5,8,256]{2,1,0:T(8,128)S(1)}, f32...) custom-call(f32[8,128]{1,0:T(8,128)S(1)} %get-tuple-element.29.levels_r, ...), custom_call_target="tpu_custom_call" | custom-call | tf_op jit(solution)/shard_map/main/pallas_call | solution.py:678
  29.6 0.0 collective-permute-done.6.before_ref
  29.6 1.8 %collective-permute-done.7.after_ref = f32[24,128]{1,0:T(8,128)S(1)} collective-permute-done((f32[24,128]{1,0:T(8,128)S(1)}, f32[24,128]{1,0:T(8,128)S(1)}, u32[]{:S(2)}, u32[]{:S(2)}) %collective-permute-start.7) | collective-permute-done | bytes 12320 | tf_op jit(solution)/shard_map/ppermute | solution.py:592
  31.4 1.0 %edge.1 = (f32[4,6,16,128]{3,2,1,0:T(8,128)S(1)}, f32[4,6,16,128]{3,2,1,0:T(8,128)S(1)}, f32[5,8,128]{2,1,0:T(8,128)S(1)}, f32[5,8,128]{2,1,0:T(8,128)S(1)}, f32...) custom-call(f32[8,128]{1,0:T(8,128)S(1)} %get-tuple-element.29.levels_ref, f32[32,128]{1,0:T(8,128)S(1)} %get-tuple-element.38.total_ref, ...), custom_call_target="tpu_custom_call" | custom-call | tf_op jit(solution)/shard_map/edge/pallas_call | solution.py:692
  32.4 6.2 %all-gather.both_ref = f32[16,128]{1,0:T(8,128)S(1)} all-gather(f32[8,128]{1,0:T(8,128)S(1)} %get-tuple-element.45), channel_id=2, replica_groups=mesh['gx'=4,'gy_0'=4,'gy_1'=2,'gz'=32] {'gy_1'}, dimensions={0}, use_global_device_ids=true | all-gather | bytes 12288 | tf_op jit(solution)/shard_map/all_gather | solution.py:701
  38.7 31.5 %all_to_all.10 = f32[32,5,1,128]{3,2,1,0:T(1,128)S(1)} all-to-all(f32[32,5,1,128]{3,2,1,0:T(1,128)S(1)} %bitcast.21), channel_id=1, replica_groups={{51,52,53,54,55,56,57,58,59,60,61,62,63,32,33,34,35,36,37,38,39,40,41,4..., dimensions={0} | all-to-all | bytes 163840 | tf_op jit(solution)/shard_map/all_to_all | solution.py:708
  70.2 10.2 %all_to_all.11 = f32[32,5,1,128]{3,2,1,0:T(1,128)S(1)} all-to-all(f32[32,5,1,128]{3,2,1,0:T(1,128)S(1)} %bitcast.20), channel_id=1, replica_groups={{672,704,736,768,800,832,864,896,928,960,992,0,32,64,96,128,160,192,224..., dimensions={0} | all-to-all | bytes 163840 | tf_op jit(solution)/shard_map/all_to_all | solution.py:719
  80.5 2.8 %finish.1 = (f32[16,2,4,256]{3,2,1,0:T(4,128)}, f32[16,2,4,256]{3,2,1,0:T(4,128)}) custom-call(f32[160,128]{1,0:T(8,128)S(1)} %bitcast.18, f32[4,6,16,256]{3,2,1,0:T(8,128)S(1)} %get-tuple-element.46.v_ref, f32[4,6,16,256]{3,2,1,0:T(8,128)S(1)} %get-tuple-element.47.q_ref, f32[5,8,256]{2,1,0:T(8,128)S(1)} %get-tuple-element.48.above_ref, ...), custom_call_target="tpu_custom_call" | custom-call | tf_op jit(solution)/shard_map/finish/pallas_call | solution.py:721
  (5 shorter events, 0.1 us)
Async XLA Ops:
  1.6 6.0 %collective-permute-start = (f32[2,17,2,4,128]{4,3,2,1,0:T(4,128)S(1)}, f32[2,17,2,4,128]{4,3,2,1,0:T(4,128)S(1)}, u32[]{:S(2)}, u32[]{:S(2)}) collective-permute-start(f32[2,17,2,4,128]{4,3,2,1,0:T(4,128)S(1)} %get-tuple-element.30), channel_id=1, source_target_pairs={{0,256},{256,512},{512,768},{1,257},{257,513},{513,769},{2,258},{2... | collective-permute-start | bytes 417800 | tf_op jit(solution)/shard_map/ppermute | solution.py:591
  5.6 14.1 %collective-permute-start.2 = (f32[2,17,2,4,128]{4,3,2,1,0:T(4,128)S(1)}, f32[2,17,2,4,128]{4,3,2,1,0:T(4,128)S(1)}, u32[]{:S(2)}, u32[]{:S(2)}) collective-permute-start(f32[2,17,2,4,128]{4,3,2,1,0:T(4,128)S(1)} %get-tuple-element.30), channel_id=1, source_target_pairs={{256,0},{512,256},{768,512},{257,1},{513,257},{769,513},{258,2},{5... | collective-permute-start | bytes 417800 | tf_op jit(solution)/shard_map/ppermute | solution.py:592
  7.8 17.6 %collective-permute-start.4 = (f32[2,17,4,2,128]{4,3,2,1,0:T(2,128)S(1)}, f32[2,17,4,2,128]{4,3,2,1,0:T(2,128)S(1)}, u32[]{:S(2)}, u32[]{:S(2)}) collective-permute-start(f32[2,17,4,2,128]{4,3,2,1,0:T(2,128)S(1)} %get-tuple-element.56), channel_id=1, source_target_pairs={{32,0},{64,32},{96,64},{128,96},{160,128},{192,160},{224,192},{0,2... | collective-permute-start | bytes 417800 | tf_op jit(solution)/shard_map/ppermute | solution.py:592
  19.7 5.7 %collective-permute-start.1 = (f32[2,17,4,2,128]{4,3,2,1,0:T(2,128)S(1)}, f32[2,17,4,2,128]{4,3,2,1,0:T(2,128)S(1)}, u32[]{:S(2)}, u32[]{:S(2)}) collective-permute-start(f32[2,17,4,2,128]{4,3,2,1,0:T(2,128)S(1)} %get-tuple-element.57), channel_id=1, source_target_pairs={{0,32},{32,64},{64,96},{96,128},{128,160},{160,192},{192,224},{224... | collective-permute-start | bytes 417800 | tf_op jit(solution)/shard_map/ppermute | solution.py:591
  19.8 5.1 %collective-permute-start.5 = (f32[2,17,2,2,128]{4,3,2,1,0:T(2,128)S(1)}, f32[2,17,2,2,128]{4,3,2,1,0:T(2,128)S(1)}, u32[]{:S(2)}, u32[]{:S(2)}) collective-permute-start(f32[2,17,2,2,128]{4,3,2,1,0:T(2,128)S(1)} %get-tuple-element.58), channel_id=1, source_target_pairs={{32,0},{64,32},{96,64},{128,96},{160,128},{192,160},{224,192},{0,2... | collective-permute-start | bytes 208904 | tf_op jit(solution)/shard_map/ppermute | solution.py:592
  24.0 1.4 %collective-permute-start.3 = (f32[2,17,2,2,128]{4,3,2,1,0:T(2,128)S(1)}, f32[2,17,2,2,128]{4,3,2,1,0:T(2,128)S(1)}, u32[]{:S(2)}, u32[]{:S(2)}) collective-permute-start(f32[2,17,2,2,128]{4,3,2,1,0:T(2,128)S(1)} %get-tuple-element.59), channel_id=1, source_target_pairs={{0,32},{32,64},{64,96},{96,128},{128,160},{160,192},{192,224},{224... | collective-permute-start | bytes 208904 | tf_op jit(solution)/shard_map/ppermute | solution.py:591
  25.7 3.9 %collective-permute-start.6 = (f32[24,128]{1,0:T(8,128)S(1)}, f32[24,128]{1,0:T(8,128)S(1)}, u32[]{:S(2)}, u32[]{:S(2)}) collective-permute-start(f32[24,128]{1,0:T(8,128)S(1)} %get-tuple-element.43), channel_id=1, source_target_pairs={{0,1},{1,2},{2,3},{3,4},{4,5},{5,6},{6,7},{7,8},{8,9},{9,10},{10,1... | collective-permute-start | bytes 36872 | tf_op jit(solution)/shard_map/ppermute | solution.py:591
  27.0 4.4 %collective-permute-start.7 = (f32[24,128]{1,0:T(8,128)S(1)}, f32[24,128]{1,0:T(8,128)S(1)}, u32[]{:S(2)}, u32[]{:S(2)}) collective-permute-start(f32[24,128]{1,0:T(8,128)S(1)} %get-tuple-element.44), channel_id=1, source_target_pairs={{1,0},{2,1},{3,2},{4,3},{5,4},{6,5},{7,6},{8,7},{9,8},{10,9},{11,1... | collective-permute-start | bytes 36872 | tf_op jit(solution)/shard_map/ppermute | solution.py:592
